TPU v7x, 32 devices: a whole 2x2x4 slice. The times are simulated.
32 devices in a mesh: gx: 8 (over z, x), gy: 4 (over y, core).
Axes of the slice: x: 2, y: 2, z: 4, core: 2. Of those that a mesh axis runs over, the one named last changes fastest.
Arguments:
- velocity: float32 [3, 128, 128, 256], P(None, 'gx', 'gy'), may hold values from -6 to 6
- owner_block: int32 [65536, 1], P(('gx', 'gy')), may hold values from 0 to 31, as said below
- base_x: int32 [65536], P(('gx', 'gy')), may hold values from 0 to 16
- base_y: int32 [65536], P(('gx', 'gy')), may hold values from 0 to 32
- base_z: int32 [65536], P(('gx', 'gy')), may hold values from 0 to 255
- delta_weights: float32 [12, 65536], P(None, ('gx', 'gy')), may hold values from 0.1 to 1
- marker_offset: float32 [3, 65536], P(None, ('gx', 'gy')), may hold values from -4 to 4
- sphere_motion: float32 [6, 64], P(None, ('gx', 'gy')), may hold values from -6 to 6
- contact_sphere: int32 [128], P(('gx', 'gy')), may hold values from 0 to 63, as said below
- contact_partner: int32 [128], P(('gx', 'gy')), may hold values from 0 to 63
Outputs:
- velocity_star: float32 [3, 128, 128, 256], P(None, 'gx', 'gy')
- new_motion: float32 [6, 64], P(None, ('gx', 'gy'))
Inputs may be any that keep to these rules, and one draw needn't show every extreme that they name: `owner_block`: block b stands at gx index b // 4 and gy index b % 4. Each marker's owner block is the block of the device that holds the marker or one of the eight blocks beside it (periodic along gx, none beyond the walls along gy). Among the markers of one device, at most 256 have any one owner block other than that device's own, and in every device exactly 256 have one such block. `contact_sphere`: entry k names one of the 2 spheres k // 4 * 2 and after, those of the device that holds entry k.
All inputs are finite; a program needn't handle non-finite values.
Results may differ from a plain program's by a relative error of at most 0.0003.
Values sent between devices are 32-bit elements; how exact they have to be, the bound alone decides.
A program may use at most 64 MiB of HBM per device.

v0:
```python
import functools

import jax
import jax.numpy as jnp
import numpy as np
from jax import lax
from jax.experimental import pallas as pl
from jax.experimental.pallas import tpu as pltpu
from jax.sharding import PartitionSpec as P

ITERS = 4


DIFFUSION = 1.0
RESPONSE = 0.5
DASHPOT = 0.1
TILE_ROWS = 16
TILE_LANES = 128


def shift(array, axis, step, periodic):
    size = lax.axis_size(axis)
    pairs = [(i, (i + step) % size) for i in range(size) if periodic or 0 <= i + step < size]
    return lax.ppermute(array, axis, pairs)


def with_halo(array, axis, dim, width, periodic):
    length = array.shape[dim]
    last = lax.slice_in_dim(array, length - width, length, axis=dim)
    leading = lax.slice_in_dim(array, 0, width, axis=dim)
    before = shift(last, axis, 1, periodic)
    after = shift(leading, axis, -1, periodic)
    return jnp.concatenate([before, array, after], axis=dim)


def weight_table(start, weights, extent, wrapped):
    positions = jnp.arange(extent, dtype=jnp.int32)[:, None]
    table = jnp.zeros((extent, start.shape[0]), jnp.float32)
    for offset in range(4):
        target_cell = start + offset
        if wrapped:
            target_cell = target_cell % extent
        table = table + weights[offset][None, :] * (positions == target_cell[None, :]).astype(
            jnp.float32
        )
    return table


def tables(start_x, start_y, start_z, weights, span_x, span_y, extent_z):
    return (
        weight_table(start_x, weights[0:4], span_x + 4, False),
        weight_table(start_y, weights[4:8], span_y + 4, False),
        weight_table(start_z, weights[8:12], extent_z, True),
    )


def sample_field(field, table_x, table_y, table_z):
    extent_z = field.shape[3]
    partial_z = jnp.dot(field.reshape(-1, extent_z), table_z, precision=lax.Precision.HIGH)
    partial_z = partial_z.reshape(3, field.shape[1], field.shape[2], -1)
    partial_y = jnp.sum(partial_z * table_y[None, None, :, :], axis=2)
    return jnp.sum(partial_y * table_x[None, :, :], axis=1)


def deposit_field(forces, table_x, table_y, table_z):
    spread_xy = forces[:, None, None, :] * table_x[None, :, None, :] * table_y[None, None, :, :]
    count = forces.shape[1]
    flat = lax.dot_general(
        spread_xy.reshape(-1, count),
        table_z,
        (((1,), (1,)), ((), ())),
        precision=lax.Precision.HIGH,
    )
    return flat.reshape(3, table_x.shape[0], table_y.shape[0], table_z.shape[0])


def relax_kernel(e_ref, below_ref, above_ref, mask_ref, out_ref, rhs, one, two):
    span_x, span_y = out_ref.shape[1], out_ref.shape[2]
    wide_x, wide_y = span_x + 2 * ITERS, span_y + 2 * ITERS
    rim = below_ref.shape[2]
    mask = mask_ref[...]
    extent_z = mask.shape[1]

    def build(x, carry):
        one[x] = jnp.zeros((wide_y, extent_z), jnp.float32)
        one[x, 2 : wide_y - 2] = e_ref[0, x]
        one[x, 0:rim] = one[x, 0:rim] + below_ref[0, x]
        one[x, wide_y - rim : wide_y] = one[x, wide_y - rim : wide_y] + above_ref[0, x]
        rhs[x] = one[x] * mask
        return carry

    lax.fori_loop(0, wide_x, build, 0)
    inverse = 1.0 / (1.0 + 6.0 * DIFFUSION)

    def row(source, x):
        here = source[x]
        beside = source[x - 1] + source[x + 1]
        beside = beside + pltpu.roll(here, 1, 0) + pltpu.roll(here, wide_y - 1, 0)
        beside = beside + pltpu.roll(here, 1, 1) + pltpu.roll(here, extent_z - 1, 1)
        return (rhs[x] + DIFFUSION * beside) * (inverse * mask)

    source = rhs
    for sweep in range(ITERS - 1):
        target = one if sweep % 2 == 0 else two

        def step(pair, carry, source=source, target=target, first=sweep + 1):
            x = first + 2 * pair
            new = (row(source, x), row(source, x + 1))
            target[x] = new[0]
            target[x + 1] = new[1]
            return carry

        lax.fori_loop(0, wide_x // 2 - sweep - 1, step, 0)
        source = target

    def last(pair, carry, source=source):
        x = 2 * pair
        new = (row(source, x + ITERS), row(source, x + ITERS + 1))
        out_ref[0, x] = new[0][ITERS : ITERS + span_y]
        out_ref[0, x + 1] = new[1][ITERS : ITERS + span_y]
        return carry

    lax.fori_loop(0, span_x // 2, last, 0)


def relax_all(grown, below, above, mask, span_x, span_y):
    extent_z = grown.shape[3]
    wide = (span_x + 2 * ITERS, span_y + 2 * ITERS, extent_z)

    def block(array):
        return pl.BlockSpec((1,) + array.shape[1:], lambda c: (c, 0, 0, 0))

    return pl.pallas_call(
        relax_kernel,
        grid=(grown.shape[0],),
        out_shape=jax.ShapeDtypeStruct((grown.shape[0], span_x, span_y, extent_z), jnp.float32),
        in_specs=[
            block(grown),
            block(below),
            block(above),
            pl.BlockSpec(mask.shape, lambda c: (0, 0)),
        ],
        out_specs=pl.BlockSpec((1, span_x, span_y, extent_z), lambda c: (c, 0, 0, 0)),
        scratch_shapes=[pltpu.VMEM(wide, jnp.float32)] * 3,
        cost_estimate=pl.CostEstimate(
            flops=40 * grown.size, bytes_accessed=12 * grown.size, transcendentals=0
        ),
        name="relax",
    )(grown, below, above, mask)


def gather_kernel(columns, rows, x_ref, out_ref, held, local_sem, row_send, row_recv, col_send, col_recv):
    column = lax.axis_index("gx")
    row = lax.axis_index("gy")
    row_peers = [lax.rem(row + k, rows) for k in range(1, rows)]
    column_peers = [lax.rem(column + k, columns) for k in range(1, columns)]
    barrier = pltpu.get_barrier_semaphore()
    mesh = pl.DeviceIdType.MESH
    for peer in row_peers:
        pl.semaphore_signal(barrier, inc=1, device_id=(column, peer), device_id_type=mesh)
    for peer in column_peers:
        pl.semaphore_signal(barrier, inc=1, device_id=(peer, row), device_id_type=mesh)
    own = pltpu.make_async_copy(x_ref, held.at[column, row], local_sem)
    own.start()
    pl.semaphore_wait(barrier, rows + columns - 2)
    first = []
    for k, peer in enumerate(row_peers):
        copy = pltpu.make_async_remote_copy(
            src_ref=x_ref,
            dst_ref=held.at[column, row],
            send_sem=row_send.at[k],
            recv_sem=row_recv.at[k],
            device_id=(column, peer),
            device_id_type=mesh,
        )
        copy.start()
        first.append(copy)
    own.wait()
    for copy in first:
        copy.wait()
    second = []
    for k, peer in enumerate(column_peers):
        copy = pltpu.make_async_remote_copy(
            src_ref=held.at[column],
            dst_ref=held.at[column],
            send_sem=col_send.at[k],
            recv_sem=col_recv.at[k],
            device_id=(peer, row),
            device_id_type=mesh,
        )
        copy.start()
        second.append(copy)
    for copy in second:
        copy.wait()
    out_ref[...] = held[...]


def gather_tiles(tile):
    columns, rows = lax.axis_size("gx"), lax.axis_size("gy")
    shape = (columns, rows) + tile.shape
    return pl.pallas_call(
        functools.partial(gather_kernel, columns, rows),
        out_shape=jax.ShapeDtypeStruct(shape, jnp.float32),
        in_specs=[pl.BlockSpec(memory_space=pltpu.VMEM)],
        out_specs=pl.BlockSpec(memory_space=pltpu.VMEM),
        scratch_shapes=[
            pltpu.VMEM(shape, jnp.float32),
            pltpu.SemaphoreType.DMA,
            pltpu.SemaphoreType.DMA((rows - 1,)),
            pltpu.SemaphoreType.DMA((rows - 1,)),
            pltpu.SemaphoreType.DMA((columns - 1,)),
            pltpu.SemaphoreType.DMA((columns - 1,)),
        ],
        compiler_params=pltpu.CompilerParams(collective_id=0, has_side_effects=True),
        cost_estimate=pl.CostEstimate(flops=0, bytes_accessed=40_000_000, transcendentals=0),
        name="gather_tiles",
    )(tile)


ARRIVALS = ((0, 0), (1, 0), (2, 0), (0, 1), (2, 1), (0, 2), (1, 2), (2, 2), (1, 1))


def combine_matrix(columns, rows, per_sphere):
    matrix = np.zeros((columns, rows, columns, rows, TILE_ROWS), np.float32)
    for i in range(columns):
        for j in range(rows):
            for slot, (a, b) in enumerate(ARRIVALS):
                target_row = j + b - 1
                if 0 <= target_row < rows:
                    matrix[(i + a - 1) % columns, target_row, i, j, slot] -= RESPONSE / per_sphere
            matrix[i, j, i, j, len(ARRIVALS)] = 1.0
    return matrix.reshape(columns * rows, -1)


def moments(forces, offsets):
    return jnp.concatenate([forces, jnp.cross(offsets, forces, axis=0)], axis=0)


def on_device(
    velocity,
    owner_block,
    base_x,
    base_y,
    base_z,
    delta_weights,
    marker_offset,
    sphere_motion,
    contact_sphere,
    contact_partner,
):
    span_x = velocity.shape[1]
    span_y = velocity.shape[2]
    extent_z = velocity.shape[3]
    row_count = lax.axis_size("gy")
    column_count = lax.axis_size("gx")
    here = lax.axis_index(("gx", "gy"))
    row_index = lax.axis_index("gy")
    column_index = lax.axis_index("gx")
    grown_field = with_halo(velocity, "gx", 1, 2, True)
    grown_field = with_halo(grown_field, "gy", 2, 2, False)
    markers = base_x.shape[0]
    spheres_here = sphere_motion.shape[1]
    per_sphere = markers // spheres_here
    capacity = markers // 8
    owner = owner_block[:, 0]
    at_home = owner == here
    home_weight = at_home.astype(jnp.float32)
    lanes = 8
    step_x = (owner // row_count - column_index + 1 + column_count) % column_count
    step_y = owner % row_count - row_index + 1
    lane = step_x * 3 + step_y
    lane = lane - (lane > 4).astype(jnp.int32)
    hits = (lane[:, None] == jnp.arange(lanes, dtype=jnp.int32)[None, :]).astype(jnp.int32)
    hits = hits * (1 - at_home.astype(jnp.int32))[:, None]
    ranked = jnp.sum((jnp.cumsum(hits, axis=0) - hits) * hits, axis=1)
    total_slots = lanes * capacity
    slots = jnp.where(at_home, total_slots, lane * capacity + ranked)
    marker_motion = jnp.broadcast_to(
        sphere_motion[:, :, None], (6, spheres_here, per_sphere)
    ).reshape(6, markers)
    target = marker_motion[0:3] + jnp.cross(marker_motion[3:6], marker_offset, axis=0)
    coords = jnp.stack([base_x, base_y, base_z]).astype(jnp.float32)
    sphere_of = (jnp.arange(markers, dtype=jnp.int32) // per_sphere).astype(jnp.float32)
    payload = jnp.concatenate(
        [delta_weights, coords, target, marker_offset, sphere_of[None, :]], axis=0
    )
    outgoing = (
        jnp.zeros((payload.shape[0], total_slots), jnp.float32)
        .at[:, slots]
        .set(payload, mode="drop")
    )
    c = capacity
    from_left = shift(outgoing[:, 5 * c :], "gx", 1, True)
    from_right = shift(outgoing[:, : 3 * c], "gx", -1, True)
    down = [from_left[:, :c], outgoing[:, 3 * c : 4 * c], from_right[:, :c]]
    up = [from_left[:, 2 * c :], outgoing[:, 4 * c : 5 * c], from_right[:, 2 * c :]]
    from_above = shift(jnp.concatenate(down, axis=1), "gy", -1, False)
    from_below = shift(jnp.concatenate(up, axis=1), "gy", 1, False)
    arrived = jnp.concatenate(
        [from_below, from_left[:, c : 2 * c], from_right[:, c : 2 * c], from_above], axis=1
    )

    home_tables = tables(base_x, base_y, base_z, delta_weights, span_x, span_y, extent_z)
    sampled_home = sample_field(grown_field, *home_tables)
    home_force = (target - sampled_home) * home_weight[None, :]
    cell_start = arrived[12:15].astype(jnp.int32)
    slot_tables = tables(
        cell_start[0], cell_start[1], cell_start[2], arrived[0:12], span_x, span_y, extent_z
    )
    slot_force = arrived[15:18] - sample_field(grown_field, *slot_tables)
    forces_all = jnp.concatenate([home_force, slot_force], axis=1)
    all_tables = [jnp.concatenate(pair, axis=1) for pair in zip(home_tables, slot_tables)]
    spread = deposit_field(forces_all, *all_tables)

    spread = spread + jnp.pad(velocity, ((0, 0), (2, 2), (2, 2), (0, 0)))
    reach = ITERS + 2
    left = shift(spread[:, span_x + 4 - reach :], "gx", 1, True)
    right = shift(spread[:, :reach], "gx", -1, True)
    grown = jnp.concatenate(
        [
            left[:, :2],
            spread[:, : reach - 2] + left[:, 2:],
            spread[:, reach - 2 : span_x + 6 - reach],
            spread[:, span_x + 6 - reach :] + right[:, : reach - 2],
            right[:, reach - 2 :],
        ],
        axis=1,
    )
    below = shift(grown[:, :, span_y + 4 - reach :], "gy", 1, False)
    above = shift(grown[:, :, :reach], "gy", -1, False)
    global_row = row_index * span_y - ITERS + jnp.arange(span_y + 2 * ITERS, dtype=jnp.int32)
    inside = jnp.logical_and(global_row >= 0, global_row < span_y * row_count)
    mask = jnp.broadcast_to(inside.astype(jnp.float32)[:, None], (span_y + 2 * ITERS, extent_z))
    state = relax_all(grown, below, above, mask, span_x, span_y)

    home_sums = jnp.sum(
        moments(home_force, marker_offset).reshape(6, spheres_here, per_sphere), axis=-1
    )
    slot_moments = moments(slot_force, arrived[18:21])
    chosen = arrived[21][None, :] == jnp.arange(spheres_here, dtype=jnp.float32)[:, None]
    picked = jnp.where(chosen[None], slot_moments[:, None], 0.0)
    slot_sums = jnp.sum(picked.reshape(6, spheres_here, lanes, capacity), axis=-1)
    columns = jnp.concatenate(
        [slot_sums, home_sums[:, :, None], sphere_motion[:, :, None]], axis=2
    )
    tile = columns.transpose(2, 1, 0).reshape(lanes + 2, spheres_here * 6)
    tile = jnp.pad(tile, ((0, TILE_ROWS - tile.shape[0]), (0, TILE_LANES - tile.shape[1])))
    gathered = gather_tiles(tile).reshape(-1, TILE_LANES)
    matrix = jnp.asarray(combine_matrix(column_count, row_count, per_sphere))
    moved = jnp.dot(matrix, gathered, precision=lax.Precision.HIGHEST)
    moved = moved[:, : spheres_here * 6].reshape(-1, 6)
    all_spheres = jnp.arange(moved.shape[0], dtype=jnp.int32)
    mine = here * spheres_here + jnp.arange(spheres_here, dtype=jnp.int32)
    own = (mine[:, None] == all_spheres[None, :]).astype(jnp.float32)
    acts = (contact_sphere[None, :] == mine[:, None]).astype(jnp.float32)
    partner = (contact_partner[:, None] == all_spheres[None, :]).astype(jnp.float32)
    linked = jnp.sum(acts[:, :, None] * partner[None], axis=1)
    linked = linked - jnp.sum(acts, axis=1)[:, None] * own
    linear_part = jnp.dot(own + DASHPOT * linked, moved[:, :3], precision=lax.Precision.HIGHEST)
    angular_part = jnp.dot(own, moved[:, 3:], precision=lax.Precision.HIGHEST)
    new_motion = jnp.concatenate([linear_part, angular_part], axis=1).T
    return (state, new_motion)


def solution(mesh):
    placed = (
        P(None, "gx", "gy", None),
        P(("gx", "gy"), None),
        P(("gx", "gy")),
        P(("gx", "gy")),
        P(("gx", "gy")),
        P(None, ("gx", "gy")),
        P(None, ("gx", "gy")),
        P(None, ("gx", "gy")),
        P(("gx", "gy")),
        P(("gx", "gy")),
    )
    return jax.shard_map(
        on_device,
        mesh=mesh,
        in_specs=placed,
        out_specs=(P(None, "gx", "gy", None), P(None, ("gx", "gy"))),
        check_vma=False,
    )
```

profile of v0, /device:TPU:1, one launch (start us, length us, event | category | flops | bytes accessed | tf_op | source)
XLA Modules:
  0.0 186.9 jit_solution(17616555549506087838)
XLA Ops:
  0.7 1.2 fusion.58
  1.8 2.1 %collective-permute-start = (f32[3,2,32,256]{3,2,1,0:T(8,128)S(1)}, f32[3,2,32,256]{3,2,1,0:T(8,128)S(1)}, u32[]{:S(2)}, u32[]{:S(2)}) collective-permute-start(f32[3,2,32,256]{3,2,1,0:T(8,128)S(1)} %get-tuple-element.12), channel_id=1, source_target_pairs={{0,4},{4,8},{8,12},{12,16},{16,20},{20,24},{24,28},{28,0},{1,5},{5... | collective-permute-start | bytes 589832 | tf_op jit(solution)/shard_map/ppermute | solution.py:24
  3.9 3.1 %collective-permute-start.1 = (f32[3,2,32,256]{3,2,1,0:T(8,128)S(1)}, f32[3,2,32,256]{3,2,1,0:T(8,128)S(1)}, u32[]{:S(2)}, u32[]{:S(2)}) collective-permute-start(f32[3,2,32,256]{3,2,1,0:T(8,128)S(1)} %get-tuple-element.11), channel_id=1, source_target_pairs={{0,28},{4,0},{8,4},{12,8},{16,12},{20,16},{24,20},{28,24},{1,29},{... | collective-permute-start | bytes 589832 | tf_op jit(solution)/shard_map/ppermute | solution.py:24
  7.0 0.7 fusion.53
  7.8 0.8 fusion.22
  8.6 1.5 fusion.63
  10.0 0.7 broadcast_add_fusion.11
  10.7 0.7 add_select_fusion.3
  11.5 0.7 broadcast_add_fusion.10
  12.2 0.8 fusion.65
  13.4 2.3 %reduce-window.6 = s32[8,16,128]{2,1,0:T(8,128)S(1)} reduce-window(s32[8,16,128]{2,1,0:T(8,128)S(1)} %fusion.17, s32[]{:T(128)} %constant.143.clone.1), window={size=1x1x128 pad=0_0x0_0x127_0}, to_apply=%region_2.4 | reduce-window | flops 2080768 | bytes 131076 | tf_op jit(solution)/shard_map/reduce-window
  16.2 0.7 compare_select_fusion
  17.0 0.7 fusion.37
  17.7 0.9 subtract_bitcast_fusion.8
  18.6 0.8 fusion.54
  19.5 0.8 add_convert_fusion
  20.2 0.8 select_add_fusion.3
  21.6 4.1 %collective-permute-start.2 = (f32[3,20,2,256]{3,2,1,0:T(2,128)S(1)}, f32[3,20,2,256]{3,2,1,0:T(2,128)S(1)}, u32[]{:S(2)}, u32[]{:S(2)}) collective-permute-start(f32[3,20,2,256]{3,2,1,0:T(2,128)S(1)} %get-tuple-element.9), channel_id=1, source_target_pairs={{0,1},{1,2},{2,3},{4,5},{5,6},{6,7},{8,9},{9,10},{10,11},{12,13},{... | collective-permute-start | bytes 368648 | tf_op jit(solution)/shard_map/ppermute | solution.py:24
  25.7 1.9 %collective-permute-start.3 = (f32[3,20,2,256]{3,2,1,0:T(2,128)S(1)}, f32[3,20,2,256]{3,2,1,0:T(2,128)S(1)}, u32[]{:S(2)}, u32[]{:S(2)}) collective-permute-start(f32[3,20,2,256]{3,2,1,0:T(2,128)S(1)} %get-tuple-element.10), channel_id=1, source_target_pairs={{1,0},{2,1},{3,2},{5,4},{6,5},{7,6},{9,8},{10,9},{11,10},{13,12},{... | collective-permute-start | bytes 368648 | tf_op jit(solution)/shard_map/ppermute | solution.py:24
  27.9 4.0 %collective-permute-done.3 = f32[3,20,2,256]{3,2,1,0:T(2,128)S(1)} collective-permute-done((f32[3,20,2,256]{3,2,1,0:T(2,128)S(1)}, f32[3,20,2,256]{3,2,1,0:T(2,128)S(1)}, u32[]{:S(2)}, u32[]{:S(2)}) %collective-permute-start.3) | collective-permute-done | bytes 122912 | tf_op jit(solution)/shard_map/ppermute | solution.py:24
  31.9 12.3 %multiply_reduce_fusion.1 = f32[3,20,2048]{2,1,0:T(8,128)S(1)} fusion(f32[36,2048]{1,0:T(8,128)S(1)} %select_add_fusion.3, f32[3,20,2,256]{3,2,1,0:T(2,128)S(1)} %collective-permute-done.3, f32[3,20,32,256]{3,2,1,0:T(8,128)} %copy-done.4, f32[3,20,2,256]{3,2,1,0:T(2,128)S(1)} %collective-permute-done.2, f32[2048]{0:T(1024)S(1)} %bitcast.135, ...), kind=kOutput, calls=%fused_computation.6 | convolution fusion | flops 6810370048 | bytes 3063808 | tf_op jit(solution)/shard_map/dot_general | solution.py:59
  45.0 5.8 %scatter_custom_fusion = f32[22,2048]{0,1:T(8,128)S(1)} fusion(s32[2048]{0:T(1024)S(1)} %bitcast.189, f32[2048,22]{1,0:T(8,128)S(1)} %copy.78, f32[]{:T(128)} %constant.146.clone.1), kind=kCustom, calls=%fused_computation.29 | custom fusion | bytes 180228 | tf_op jit(solution)/shard_map/scatter | solution.py:290
  50.9 0.9 fusion.60
  51.8 4.2 %collective-permute-start.5 = (f32[22,768]{0,1:T(8,128)}, f32[22,768]{0,1:T(8,128)S(1)}, u32[]{:S(2)}, u32[]{:S(2)}) collective-permute-start(f32[22,768]{0,1:T(8,128)} %get-tuple-element.16), channel_id=1, source_target_pairs={{0,28},{4,0},{8,4},{12,8},{16,12},{20,16},{24,20},{28,24},{1,29},{... | collective-permute-start | bytes 202760 | tf_op jit(solution)/shard_map/ppermute | solution.py:24
  56.2 10.5 %collective-permute-done.4 = f32[22,768]{0,1:T(8,128)S(1)} collective-permute-done((f32[22,768]{0,1:T(8,128)}, f32[22,768]{0,1:T(8,128)S(1)}, u32[]{:S(2)}, u32[]{:S(2)}) %collective-permute-start.4) | collective-permute-done | bytes 67616 | tf_op jit(solution)/shard_map/ppermute | solution.py:24
  66.8 2.0 %collective-permute-done.5 = f32[22,768]{0,1:T(8,128)S(1)} collective-permute-done((f32[22,768]{0,1:T(8,128)}, f32[22,768]{0,1:T(8,128)S(1)}, u32[]{:S(2)}, u32[]{:S(2)}) %collective-permute-start.5) | collective-permute-done | bytes 67616 | tf_op jit(solution)/shard_map/ppermute | solution.py:24
  68.9 1.9 %collective-permute-start.6 = (f32[22,768]{1,0:T(8,128)S(1)}, f32[22,768]{1,0:T(8,128)S(1)}, u32[]{:S(2)}, u32[]{:S(2)}) collective-permute-start(f32[22,768]{1,0:T(8,128)S(1)} %pad_maximum_fusion.6), channel_id=1, source_target_pairs={{0,1},{1,2},{2,3},{4,5},{5,6},{6,7},{8,9},{9,10},{10,11},{12,13},{... | collective-permute-start | bytes 202760 | tf_op jit(solution)/shard_map/ppermute | solution.py:24
  71.0 2.6 %collective-permute-start.7 = (f32[22,768]{1,0:T(8,128)S(1)}, f32[22,768]{1,0:T(8,128)S(1)}, u32[]{:S(2)}, u32[]{:S(2)}) collective-permute-start(f32[22,768]{1,0:T(8,128)S(1)} %pad_maximum_fusion.7), channel_id=1, source_target_pairs={{1,0},{2,1},{3,2},{5,4},{6,5},{7,6},{9,8},{10,9},{11,10},{13,12},{... | collective-permute-start | bytes 202760 | tf_op jit(solution)/shard_map/ppermute | solution.py:24
  74.1 2.6 %collective-permute-done.7 = f32[22,768]{1,0:T(8,128)S(1)} collective-permute-done((f32[22,768]{1,0:T(8,128)S(1)}, f32[22,768]{1,0:T(8,128)S(1)}, u32[]{:S(2)}, u32[]{:S(2)}) %collective-permute-start.7) | collective-permute-done | bytes 67616 | tf_op jit(solution)/shard_map/ppermute | solution.py:24
  77.4 3.4 %select_add_fusion = (f32[256,2048]{1,0:T(8,128)}, f32[256,2048]{1,0:T(8,128)}) fusion(f32[2048]{0:T(1024)S(1)} %bitcast.143, s32[2048]{0:T(1024)S(1)} %bitcast.151, f32[2048]{0:T(1024)S(1)} %bitcast.145, s32[2048]{0:T(1024)S(1)} %bitcast.153, f32[2048]{0:T(1024)S(1)} %bitcast.147, s32[2048]{0:T(1024)S(1)} %bitcast.155, f32[2048]{0:T(1024)S(1)} %bitcast.149, ...), kind=kLoop, calls=%fused_computation.14 | loop fusion | flops 11534336 | bytes 4325376 | tf_op jit(solution)/shard_map/add | solution.py:43
  80.8 12.0 %multiply_reduce_fusion = f32[3,20,2048]{2,1,0:T(8,128)S(1)} fusion(f32[36,2048]{1,0:T(8,128)S(1)} %select_add_fusion.2, f32[3,20,2,256]{3,2,1,0:T(2,128)S(1)} %copy-done.11, f32[3,20,32,256]{3,2,1,0:T(8,128)S(1)} %copy-done.5, f32[3,20,2,256]{3,2,1,0:T(2,128)S(1)} %collective-permute-done.2, f32[2048]{0:T(1024)S(1)} %bitcast.144, s32[2048]{0:T(1024)S(1)} %bitcast.152, ...), kind=kOutput, calls=%fused_computation.5 | convolution fusion | flops 6810370048 | bytes 3063808 | tf_op jit(solution)/shard_map/dot_general | solution.py:59
  93.2 19.0 %pad_add_fusion = f32[3,20,36,256]{3,2,1,0:T(8,128)S(1)} fusion(f32[3,16,32,256]{3,2,1,0:T(8,128)} %param.13, f32[256,2048]{1,0:T(8,128)} %get-tuple-element.82, f32[256,2048]{1,0:T(8,128)} %get-tuple-element.83, f32[36,4096]{1,0:T(8,128)S(1)} %pad_maximum_fusion.3, f32[3,20,4096]{2,1,0:T(8,128)S(1)} %broadcast_multiply_fusion), kind=kOutput, calls=%fused_computation.11 | convolution fusion | flops 13599993856 | bytes 9551872 | tf_op jit(solution)/shard_map/dot_general | solution.py:68
  112.3 1.0 fusion.56
  114.3 22.5 %gather_tiles.1 = f32[8,4,16,128]{3,2,1,0:T(8,128)} custom-call(f32[16,128]{1,0:T(8,128)} %pad.9.x_ref), custom_call_target="tpu_custom_call" | custom-call | bytes 40000000 | tf_op jit(solution)/shard_map/gather_tiles/pallas_call | solution.py:201
  136.8 1.2 fusion.14
  138.1 3.3 %collective-permute-start.9 = (f32[3,6,36,256]{3,2,1,0:T(8,128)S(1)}, f32[3,6,36,256]{3,2,1,0:T(8,128)S(1)}, u32[]{:S(2)}, u32[]{:S(2)}) collective-permute-start(f32[3,6,36,256]{3,2,1,0:T(8,128)S(1)} %get-tuple-element.7), channel_id=1, source_target_pairs={{0,28},{4,0},{8,4},{12,8},{16,12},{20,16},{24,20},{28,24},{1,29},{... | collective-permute-start | bytes 1990664 | tf_op jit(solution)/shard_map/ppermute | solution.py:24
  141.4 1.0 slice_dynamic-update-slice_fusion.2
  142.4 1.1 fusion.13
  143.6 12.7 %collective-permute-done.9 = f32[3,6,36,256]{3,2,1,0:T(8,128)S(1)} collective-permute-done((f32[3,6,36,256]{3,2,1,0:T(8,128)S(1)}, f32[3,6,36,256]{3,2,1,0:T(8,128)S(1)}, u32[]{:S(2)}, u32[]{:S(2)}) %collective-permute-start.9) | collective-permute-done | bytes 663584 | tf_op jit(solution)/shard_map/ppermute | solution.py:24
  156.7 1.9 %collective-permute-start.10 = (f32[3,24,6,256]{3,1,2,0:T(8,128)S(1)}, f32[3,24,6,256]{3,1,2,0:T(8,128)S(1)}, u32[]{:S(2)}, u32[]{:S(2)}) collective-permute-start(f32[3,24,6,256]{3,1,2,0:T(8,128)S(1)} %copy.87), channel_id=1, source_target_pairs={{0,1},{1,2},{2,3},{4,5},{5,6},{6,7},{8,9},{9,10},{10,11},{12,13},{... | collective-permute-start | bytes 1327112 | tf_op jit(solution)/shard_map/ppermute | solution.py:24
  158.8 2.4 %collective-permute-start.11 = (f32[3,24,6,256]{3,1,2,0:T(8,128)S(1)}, f32[3,24,6,256]{3,1,2,0:T(8,128)S(1)}, u32[]{:S(2)}, u32[]{:S(2)}) collective-permute-start(f32[3,24,6,256]{3,1,2,0:T(8,128)S(1)} %copy.88), channel_id=1, source_target_pairs={{1,0},{2,1},{3,2},{5,4},{6,5},{7,6},{9,8},{10,9},{11,10},{13,12},{... | collective-permute-start | bytes 1327112 | tf_op jit(solution)/shard_map/ppermute | solution.py:24
  161.6 0.7 maximum_bitcast_fusion.6
  162.3 1.6 collective-permute-done.10
  163.8 1.0 copy.89.below_ref
  164.8 3.6 %collective-permute-done.11 = f32[3,24,6,256]{3,1,2,0:T(8,128)S(1)} collective-permute-done((f32[3,24,6,256]{3,1,2,0:T(8,128)S(1)}, f32[3,24,6,256]{3,1,2,0:T(8,128)S(1)}, u32[]{:S(2)}, u32[]{:S(2)}) %collective-permute-start.11) | collective-permute-done | bytes 442400 | tf_op jit(solution)/shard_map/ppermute | solution.py:24
  168.4 1.0 copy.90.above_ref
  169.4 0.7 broadcast_in_dim.44.mask_ref
  170.0 16.8 %relax.1 = f32[3,16,32,256]{3,2,1,0:T(8,128)} custom-call(f32[3,24,36,256]{3,2,1,0:T(8,128)} %copy-done, f32[3,24,6,256]{3,2,1,0:T(8,128)} %copy.89.below_ref, f32[3,24,6,256]{3,2,1,0:T(8,128)} %copy.90.above_ref, f32[40,256]{1,0:T(8,128)} %broadcast_in_dim.44.mask_ref), custom_call_target="tpu_custom_call" | custom-call | flops 26542080 | bytes 7962624 | tf_op jit(solution)/shard_map/relax/pallas_call | solution.py:133
  (110 shorter events, 6.5 us)
Async XLA Ops:
  0.6 20.6 %copy-start.1 = (f32[3,16,32,256]{3,2,1,0:T(8,128)S(1)}, f32[3,16,32,256]{3,2,1,0:T(8,128)}, u32[]{:S(2)}) copy-start(f32[3,16,32,256]{3,2,1,0:T(8,128)} %param.13) | copy-start | bytes 4718596
  0.6 20.4 %copy-start.6 = (s32[2048]{0:T(1024)S(1)}, s32[2048]{0:T(1024)}, u32[]{:S(2)}) copy-start(s32[2048]{0:T(1024)} %param.15) | copy-start | bytes 24580
  0.7 20.5 %copy-start.9 = (s32[4]{0:T(128)S(1)}, s32[4]{0:T(128)}, u32[]{:S(2)}) copy-start(s32[4]{0:T(128)} %param.21) | copy-start | bytes 52
  1.8 19.4 %collective-permute-start = (f32[3,2,32,256]{3,2,1,0:T(8,128)S(1)}, f32[3,2,32,256]{3,2,1,0:T(8,128)S(1)}, u32[]{:S(2)}, u32[]{:S(2)}) collective-permute-start(f32[3,2,32,256]{3,2,1,0:T(8,128)S(1)} %get-tuple-element.12), channel_id=1, source_target_pairs={{0,4},{4,8},{8,12},{12,16},{16,20},{20,24},{24,28},{28,0},{1,5},{5... | collective-permute-start | bytes 589832 | tf_op jit(solution)/shard_map/ppermute | solution.py:24
  3.9 17.5 %collective-permute-start.1 = (f32[3,2,32,256]{3,2,1,0:T(8,128)S(1)}, f32[3,2,32,256]{3,2,1,0:T(8,128)S(1)}, u32[]{:S(2)}, u32[]{:S(2)}) collective-permute-start(f32[3,2,32,256]{3,2,1,0:T(8,128)S(1)} %get-tuple-element.11), channel_id=1, source_target_pairs={{0,28},{4,0},{8,4},{12,8},{16,12},{20,16},{24,20},{28,24},{1,29},{... | collective-permute-start | bytes 589832 | tf_op jit(solution)/shard_map/ppermute | solution.py:24
  21.3 6.4 %copy-start.8 = (f32[6,2]{0,1:T(2,128)S(1)}, f32[6,2]{0,1:T(2,128)}, u32[]{:S(2)}) copy-start(f32[6,2]{0,1:T(2,128)} %param.20) | copy-start | bytes 148
  21.5 6.2 %copy-start.4 = (f32[3,20,32,256]{3,2,1,0:T(8,128)}, f32[3,20,32,256]{3,2,1,0:T(8,128)S(1)}, u32[]{:S(2)}) copy-start(f32[3,20,32,256]{3,2,1,0:T(8,128)S(1)} %constant_dynamic-update-slice_fusion) | copy-start | bytes 5898244
  21.6 6.3 %collective-permute-start.2 = (f32[3,20,2,256]{3,2,1,0:T(2,128)S(1)}, f32[3,20,2,256]{3,2,1,0:T(2,128)S(1)}, u32[]{:S(2)}, u32[]{:S(2)}) collective-permute-start(f32[3,20,2,256]{3,2,1,0:T(2,128)S(1)} %get-tuple-element.9), channel_id=1, source_target_pairs={{0,1},{1,2},{2,3},{4,5},{5,6},{6,7},{8,9},{9,10},{10,11},{12,13},{... | collective-permute-start | bytes 368648 | tf_op jit(solution)/shard_map/ppermute | solution.py:24
  25.7 6.2 %collective-permute-start.3 = (f32[3,20,2,256]{3,2,1,0:T(2,128)S(1)}, f32[3,20,2,256]{3,2,1,0:T(2,128)S(1)}, u32[]{:S(2)}, u32[]{:S(2)}) collective-permute-start(f32[3,20,2,256]{3,2,1,0:T(2,128)S(1)} %get-tuple-element.10), channel_id=1, source_target_pairs={{1,0},{2,1},{3,2},{5,4},{6,5},{7,6},{9,8},{10,9},{11,10},{13,12},{... | collective-permute-start | bytes 368648 | tf_op jit(solution)/shard_map/ppermute | solution.py:24
  31.9 12.3 %copy-start.10 = (f32[3,20,2,256]{3,2,1,0:T(2,128)}, f32[3,20,2,256]{3,2,1,0:T(2,128)S(1)}, u32[]{:S(2)}) copy-start(f32[3,20,2,256]{3,2,1,0:T(2,128)S(1)} %collective-permute-done.3) | copy-start | bytes 368644
  31.9 12.5 %copy-start.2 = (f32[12,2048]{1,0:T(8,128)S(1)}, f32[12,2048]{1,0:T(8,128)}, u32[]{:S(2)}) copy-start(f32[12,2048]{1,0:T(8,128)} %param.18) | copy-start | bytes 294916
  31.9 12.5 %copy-start.3 = (f32[3,2048]{1,0:T(4,128)S(1)}, f32[3,2048]{1,0:T(4,128)}, u32[]{:S(2)}) copy-start(f32[3,2048]{1,0:T(4,128)} %param.19) | copy-start | bytes 73732
  51.8 14.9 %collective-permute-start.4 = (f32[22,768]{0,1:T(8,128)}, f32[22,768]{0,1:T(8,128)S(1)}, u32[]{:S(2)}, u32[]{:S(2)}) collective-permute-start(f32[22,768]{0,1:T(8,128)} %get-tuple-element.15), channel_id=1, source_target_pairs={{0,4},{4,8},{8,12},{12,16},{16,20},{20,24},{24,28},{28,0},{1,5},{5... | collective-permute-start | bytes 202760 | tf_op jit(solution)/shard_map/ppermute | solution.py:24
  51.8 17.0 %collective-permute-start.5 = (f32[22,768]{0,1:T(8,128)}, f32[22,768]{0,1:T(8,128)S(1)}, u32[]{:S(2)}, u32[]{:S(2)}) collective-permute-start(f32[22,768]{0,1:T(8,128)} %get-tuple-element.16), channel_id=1, source_target_pairs={{0,28},{4,0},{8,4},{12,8},{16,12},{20,16},{24,20},{28,24},{1,29},{... | collective-permute-start | bytes 202760 | tf_op jit(solution)/shard_map/ppermute | solution.py:24
  68.9 5.2 %collective-permute-start.6 = (f32[22,768]{1,0:T(8,128)S(1)}, f32[22,768]{1,0:T(8,128)S(1)}, u32[]{:S(2)}, u32[]{:S(2)}) collective-permute-start(f32[22,768]{1,0:T(8,128)S(1)} %pad_maximum_fusion.6), channel_id=1, source_target_pairs={{0,1},{1,2},{2,3},{4,5},{5,6},{6,7},{8,9},{9,10},{10,11},{12,13},{... | collective-permute-start | bytes 202760 | tf_op jit(solution)/shard_map/ppermute | solution.py:24
  71.0 5.7 %collective-permute-start.7 = (f32[22,768]{1,0:T(8,128)S(1)}, f32[22,768]{1,0:T(8,128)S(1)}, u32[]{:S(2)}, u32[]{:S(2)}) collective-permute-start(f32[22,768]{1,0:T(8,128)S(1)} %pad_maximum_fusion.7), channel_id=1, source_target_pairs={{1,0},{2,1},{3,2},{5,4},{6,5},{7,6},{9,8},{10,9},{11,10},{13,12},{... | collective-permute-start | bytes 202760 | tf_op jit(solution)/shard_map/ppermute | solution.py:24
  77.3 3.5 %copy-start.5 = (f32[3,20,32,256]{3,2,1,0:T(8,128)S(1)}, f32[3,20,32,256]{3,2,1,0:T(8,128)}, u32[]{:S(2)}) copy-start(f32[3,20,32,256]{3,2,1,0:T(8,128)} %copy-done.4) | copy-start | bytes 5898244
  77.3 3.5 %copy-start.11 = (f32[3,20,2,256]{3,2,1,0:T(2,128)S(1)}, f32[3,20,2,256]{3,2,1,0:T(2,128)}, u32[]{:S(2)}) copy-start(f32[3,20,2,256]{3,2,1,0:T(2,128)} %copy-done.10) | copy-start | bytes 368644
  112.3 24.5 %copy-start.7 = (f32[32,512]{1,0:T(8,128)S(1)}, f32[32,512]{1,0:T(8,128)}, u32[]{:S(2)}) copy-start(f32[32,512]{1,0:T(8,128)} %constant.165.clone) | copy-start | bytes 196612
  113.3 28.1 %collective-permute-start.8 = (f32[3,6,36,256]{3,2,1,0:T(8,128)}, f32[3,6,36,256]{3,2,1,0:T(8,128)}, u32[]{:S(2)}, u32[]{:S(2)}) collective-permute-start(f32[3,6,36,256]{3,2,1,0:T(8,128)} %get-tuple-element.8), channel_id=1, source_target_pairs={{0,4},{4,8},{8,12},{12,16},{16,20},{20,24},{24,28},{28,0},{1,5},{5... | collective-permute-start | bytes 1990664 | tf_op jit(solution)/shard_map/ppermute | solution.py:24
  138.1 18.2 %collective-permute-start.9 = (f32[3,6,36,256]{3,2,1,0:T(8,128)S(1)}, f32[3,6,36,256]{3,2,1,0:T(8,128)S(1)}, u32[]{:S(2)}, u32[]{:S(2)}) collective-permute-start(f32[3,6,36,256]{3,2,1,0:T(8,128)S(1)} %get-tuple-element.7), channel_id=1, source_target_pairs={{0,28},{4,0},{8,4},{12,8},{16,12},{20,16},{24,20},{28,24},{1,29},{... | collective-permute-start | bytes 1990664 | tf_op jit(solution)/shard_map/ppermute | solution.py:24
  156.4 2.4 %copy-start = (f32[3,24,36,256]{3,2,1,0:T(8,128)}, f32[3,24,36,256]{3,2,1,0:T(8,128)S(1)}, u32[]{:S(2)}) copy-start(f32[3,24,36,256]{3,2,1,0:T(8,128)S(1)} %slice_dynamic-update-slice_fusion.1.e_ref) | copy-start | bytes 7962628
  156.7 7.2 %collective-permute-start.10 = (f32[3,24,6,256]{3,1,2,0:T(8,128)S(1)}, f32[3,24,6,256]{3,1,2,0:T(8,128)S(1)}, u32[]{:S(2)}, u32[]{:S(2)}) collective-permute-start(f32[3,24,6,256]{3,1,2,0:T(8,128)S(1)} %copy.87), channel_id=1, source_target_pairs={{0,1},{1,2},{2,3},{4,5},{5,6},{6,7},{8,9},{9,10},{10,11},{12,13},{... | collective-permute-start | bytes 1327112 | tf_op jit(solution)/shard_map/ppermute | solution.py:24
  158.8 9.6 %collective-permute-start.11 = (f32[3,24,6,256]{3,1,2,0:T(8,128)S(1)}, f32[3,24,6,256]{3,1,2,0:T(8,128)S(1)}, u32[]{:S(2)}, u32[]{:S(2)}) collective-permute-start(f32[3,24,6,256]{3,1,2,0:T(8,128)S(1)} %copy.88), channel_id=1, source_target_pairs={{1,0},{2,1},{3,2},{5,4},{6,5},{7,6},{9,8},{10,9},{11,10},{13,12},{... | collective-permute-start | bytes 1327112 | tf_op jit(solution)/shard_map/ppermute | solution.py:24
where the time goes:
time: 188 us; the launch traced here: 187 us
  matrix products  45 us (24%)
  Pallas kernels  39.3 us (21%)
  waiting for transfers between devices  36.9 us (20%)
  starting transfers between devices  27.5 us (15%)
  local copies, waits for them, and re-layouts  18.9 us (10%)
  other arithmetic  17.9 us (10%)
    ppermute x12, waiting for transfers between devices, shift(): return lax.ppermute(array, axis, pairs)  36.9 us
    ppermute x12, starting transfers between devices, shift(): return lax.ppermute(array, axis, pairs)  27.5 us
    dot_general x2, matrix products, sample_field(): jnp.dot(field.reshape(-1, extent_z), table_z, precision=lax.Precision.HIGH)  24.3 us
    pallas_call x1, Pallas kernels, gather_tiles(): pl.pallas_call(functools.partial(gather_kernel, columns, rows), out_shape...  22.5 us
    dot_general x1, matrix products, deposit_field(): lax.dot_general(spread_xy.reshape(-1, count), table_z, (((1,), (1,)), (()...  19 us
    pallas_call x1, Pallas kernels, relax_all(): pl.pallas_call(relax_kernel, grid=(grown.shape[0],), out_shape=jax.ShapeD...  16.8 us
    scatter x1, local copies, waits for them, and re-layouts, on_device(): outgoing = jnp.zeros((payload.shape[0], total_slots), jnp.float32).at[:,...  5.85 us
    add x5, other arithmetic, weight_table(): table + weights[offset][None, :] * (positions == target_cell[None, :]).as...  4.54 us
  transfers between devices with their start and end apart: 12, of which 7 were waited for; matrix products, arithmetic and copies ran while one was open for 12% of the time, Pallas kernels for 12%

commit v1 on v0

v1 whole, which is shorter than its diff:
```python
import functools

import jax
import jax.numpy as jnp
import numpy as np
from jax import lax
from jax.experimental import pallas as pl
from jax.experimental.pallas import tpu as pltpu
from jax.sharding import PartitionSpec as P

ITERS = 4
DIFFUSION = 1.0
RESPONSE = 0.5
DASHPOT = 0.1

MESH = pl.DeviceIdType.MESH
TILE_ROWS = 16
TILE_LANES = 128
CHUNK = 256
WINDOW = 8
GROUP = 6
RECORD = 24
X_ROW, Y_ROW, Z_ROW, TARGET, OFFSET, SPHERE, LIVE = 12, 13, 14, 15, 18, 21, 22
DIRECTIONS = ((-1, -1), (-1, 0), (-1, 1), (0, -1), (0, 1), (1, -1), (1, 0), (1, 1))
HALO = 2
RIM = 8


def when(condition, body):
    if condition is True:
        body()
    else:
        pl.when(condition)(body)


def exists(row, rows, dy):
    if dy == 0:
        return True
    return row + dy < rows if dy > 0 else row + dy >= 0


def greet(columns, rows, column, row):
    barrier = pltpu.get_barrier_semaphore()
    for dx, dy in DIRECTIONS:
        peer = (lax.rem(column + dx + columns, columns), row + dy)
        when(
            exists(row, rows, dy),
            lambda peer=peer: pl.semaphore_signal(
                barrier, inc=1, device_id=peer, device_id_type=MESH
            ),
        )
    return barrier


def greeted(rows, row):
    inner = lax.min(row, 1) + lax.min(rows - 1 - row, 1)
    return 2 + 3 * inner


def remote(src, dst, send, recv, k, peer):
    return pltpu.make_async_remote_copy(
        src_ref=src,
        dst_ref=dst,
        send_sem=send.at[k],
        recv_sem=recv.at[k],
        device_id=peer,
        device_id_type=MESH,
    )


def split(value):
    high = value.astype(jnp.bfloat16).astype(jnp.float32)
    return high, value - high


def upper_triangle():
    rows = lax.broadcasted_iota(jnp.int32, (CHUNK, CHUNK), 0)
    lanes = lax.broadcasted_iota(jnp.int32, (CHUNK, CHUNK), 1)
    return (rows <= lanes).astype(jnp.float32).astype(jnp.bfloat16)


def ranks(categories, count):
    rows = lax.broadcasted_iota(jnp.int32, (count, CHUNK), 0).astype(jnp.float32)
    hot = [(rows == block).astype(jnp.float32) for block in categories]
    stacked = jnp.concatenate(hot, axis=0).astype(jnp.bfloat16)
    inside = jnp.dot(stacked, upper_triangle(), preferred_element_type=jnp.float32)
    carry = jnp.zeros((count, 1), jnp.float32)
    upto = []
    for b in range(len(hot)):
        block = inside[b * count : (b + 1) * count]
        upto.append(block + carry)
        carry = carry + block[:, CHUNK - 1 : CHUNK]
    return hot, upto, carry


def place(parts, where_to, groups):
    group = jnp.floor(where_to * (1.0 / CHUNK))
    slot = where_to - group * CHUNK
    rows = lax.broadcasted_iota(jnp.int32, (CHUNK, where_to.shape[1]), 0).astype(jnp.float32)
    hot = (rows == slot).astype(jnp.float32).astype(jnp.bfloat16)
    masked = [parts * (group == g).astype(jnp.float32) for g in groups]
    masked = jnp.concatenate(masked, axis=0).astype(jnp.bfloat16)
    moved = lax.dot_general(
        masked, hot, (((1,), (1,)), ((), ())), preferred_element_type=jnp.float32
    )
    result = []
    for n in range(len(groups)):
        piece = moved[2 * RECORD * n : 2 * RECORD * (n + 1)]
        result.append(piece[:RECORD] + piece[RECORD:])
    return result


def front_kernel(
    columns, rows, ids, weights, offsets, motion, velocity,
    home, arrived, left, right, below, above, corners, slots, send, recv,
):
    column = lax.axis_index("gx")
    row = lax.axis_index("gy")
    span_x, span_y = velocity.shape[1], velocity.shape[2]
    barrier = greet(columns, rows, column, row)

    def peer(dx, dy):
        return (lax.rem(column + dx + columns, columns), row + dy)

    edge = [
        (velocity.at[:, 0:HALO], right, -1, 0),
        (velocity.at[:, span_x - HALO : span_x], left, 1, 0),
        (velocity.at[:, :, 0:RIM], above, 0, -1),
        (velocity.at[:, :, span_y - RIM : span_y], below, 0, 1),
    ]
    for side, halo in enumerate((left, right)):
        edge.append((halo.at[:, :, 0:RIM], corners.at[2 + side], 0, -1))
        edge.append((halo.at[:, :, span_y - RIM : span_y], corners.at[side], 0, 1))
    for g, (dx, dy) in enumerate(DIRECTIONS):
        edge.append((slots.at[g], arrived.at[g], dx, dy))

    def start(k):
        src, dst, dx, dy = edge[k]
        when(
            exists(row, rows, dy),
            lambda: remote(src, dst, send, recv, k, peer(dx, dy)).start(),
        )

    def arrive(k):
        src, dst, dx, dy = edge[k]
        when(
            exists(row, rows, -dy),
            lambda: remote(src, dst, send, recv, k, peer(dx, dy)).wait_recv(),
        )

    def sent(k):
        src, dst, dx, dy = edge[k]
        when(
            exists(row, rows, dy),
            lambda: remote(src, dst, send, recv, k, peer(dx, dy)).wait_send(),
        )

    @pl.when(row == 0)
    def _():
        below[...] = jnp.zeros(below.shape, jnp.float32)
        for n in (0, 1):
            corners[n] = jnp.zeros(corners.shape[1:], jnp.float32)
        for g, (dx, dy) in enumerate(DIRECTIONS):
            if dy > 0:
                arrived[g] = jnp.zeros(arrived.shape[1:], jnp.float32)

    @pl.when(row == rows - 1)
    def _():
        above[...] = jnp.zeros(above.shape, jnp.float32)
        for n in (2, 3):
            corners[n] = jnp.zeros(corners.shape[1:], jnp.float32)
        for g, (dx, dy) in enumerate(DIRECTIONS):
            if dy < 0:
                arrived[g] = jnp.zeros(arrived.shape[1:], jnp.float32)

    pl.semaphore_wait(barrier, greeted(rows, row))
    for k in range(4):
        start(k)

    markers = ids.shape[1]
    spheres = motion.shape[1]
    per_sphere = markers // spheres
    owner = ids[0:1]
    owner_x = jnp.floor((owner + 0.5) * (1.0 / rows))
    owner_y = owner - owner_x * rows
    step_x = owner_x - column.astype(jnp.float32)
    step_x = jnp.where(step_x > 1.5, step_x - columns, step_x)
    step_x = jnp.where(step_x < -1.5, step_x + columns, step_x)
    step_y = owner_y - row.astype(jnp.float32)
    lane = (step_x + 1.0) * 3.0 + step_y + 1.0
    at_home = lane == 4.0
    lane = jnp.where(at_home, -1.0, jnp.where(lane > 4.0, lane - 1.0, lane))
    offset = offsets[...]
    targets = []
    for s in range(spheres):
        o = offset[:, s * per_sphere : (s + 1) * per_sphere]
        m = [motion[c : c + 1, s : s + 1] for c in range(6)]
        targets.append(
            jnp.concatenate(
                [
                    m[0] + (m[4] * o[2:3] - m[5] * o[1:2]),
                    m[1] + (m[5] * o[0:1] - m[3] * o[2:3]),
                    m[2] + (m[3] * o[1:2] - m[4] * o[0:1]),
                ],
                axis=0,
            )
        )
    home[0:12] = weights[...]
    home[X_ROW : Z_ROW + 1] = ids[1:4]
    home[TARGET : TARGET + 3] = jnp.concatenate(targets, axis=1)
    home[OFFSET : OFFSET + 3] = offset
    position = lax.broadcasted_iota(jnp.int32, (1, markers), 1)
    sphere = jnp.zeros((1, markers), jnp.float32)
    for s in range(1, spheres):
        sphere = sphere + (position >= s * per_sphere).astype(jnp.float32)
    home[SPHERE : SPHERE + 1] = sphere
    home[LIVE : LIVE + 1] = jnp.ones((1, markers), jnp.float32)
    home[LIVE + 1 : LIVE + 2] = jnp.zeros((1, markers), jnp.float32)

    lanes = len(DIRECTIONS)
    blocks = markers // CHUNK
    hot, upto, totals = ranks([lane[:, b * CHUNK : (b + 1) * CHUNK] for b in range(blocks)], lanes)
    rank = [jnp.sum(h * (u - 1.0), axis=0, keepdims=True) for h, u in zip(hot, upto)]
    where_to = jnp.concatenate(rank, axis=1) + lane * CHUNK
    where_to = jnp.where(at_home, -1.0, where_to)
    parts = jnp.concatenate(split(home[...]), axis=0)
    for g, piece in enumerate(place(parts, where_to, range(lanes))):
        slots[g] = piece
    home[LIVE : LIVE + 1] = at_home.astype(jnp.float32)

    arrive(0)
    arrive(1)
    for k in range(8, 8 + lanes):
        start(k)
    for k in range(4, 8):
        start(k)
    for k in range(2, 8 + lanes):
        arrive(k)
    for k in range(8 + lanes):
        sent(k)


def front(ids, weights, offsets, motion, velocity):
    columns, rows = lax.axis_size("gx"), lax.axis_size("gy")
    span_x, span_y, extent_z = velocity.shape[1:]
    markers = ids.shape[1]
    lanes = len(DIRECTIONS)
    f32 = jnp.float32
    copies = 8 + lanes
    vmem = pl.BlockSpec(memory_space=pltpu.VMEM)
    out = [
        (RECORD, markers),
        (lanes, RECORD, CHUNK),
        (3, HALO, span_y, extent_z),
        (3, HALO, span_y, extent_z),
        (3, span_x, RIM, extent_z),
        (3, span_x, RIM, extent_z),
        (4, 3, HALO, RIM, extent_z),
    ]
    return pl.pallas_call(
        functools.partial(front_kernel, columns, rows),
        out_shape=[jax.ShapeDtypeStruct(shape, f32) for shape in out],
        in_specs=[vmem] * 5,
        out_specs=[vmem] * len(out),
        scratch_shapes=[
            pltpu.VMEM((lanes, RECORD, CHUNK), f32),
            pltpu.SemaphoreType.DMA((copies,)),
            pltpu.SemaphoreType.DMA((copies,)),
        ],
        compiler_params=pltpu.CompilerParams(collective_id=0, has_side_effects=True),
        name="front",
    )(ids, weights, offsets, motion, velocity)


def four(distance, weights):
    value = jnp.where(distance == 3.0, weights[3:4], 0.0)
    for n in (2, 1, 0):
        value = jnp.where(distance == float(n), weights[n : n + 1], value)
    return value


def markers_kernel(
    spheres, velocity, left, right, below, above, corners, home, arrived, motion,
    spread, tile, high, low, sorted_refs, parts, sums,
):
    span_x, span_y, extent_z = velocity.shape[1:]
    wide_y = span_y + 2 * ITERS
    lanes = len(DIRECTIONS)
    bf16, f32 = jnp.bfloat16, jnp.float32
    layers = span_x + 2 * HALO

    def layer(x, row_source, below_source, above_source, own):
        for c in range(3):
            rows = row_source(c)
            edge = jnp.zeros((HALO, extent_z), f32)
            value = jnp.concatenate(
                [
                    edge,
                    below_source(c)[RIM - HALO : RIM],
                    rows,
                    above_source(c)[0:HALO],
                    edge,
                ],
                axis=0,
            )
            at = slice(wide_y * c, wide_y * (c + 1))
            first, rest = split(value)
            high[x, at] = first.astype(bf16)
            low[x, at] = rest.astype(bf16)
            if own:
                wide = jnp.zeros((ITERS, extent_z), f32)
                spread[x + HALO, at] = jnp.concatenate([wide, rows, wide], axis=0)
        end = jnp.zeros((high.shape[1] - 3 * wide_y, extent_z), bf16)
        high[x, 3 * wide_y :] = end
        low[x, 3 * wide_y :] = end

    def inner(x, carry):
        layer(
            x + HALO,
            lambda c: velocity[c, x],
            lambda c: below[c, x],
            lambda c: above[c, x],
            True,
        )
        return carry

    lax.fori_loop(0, span_x, inner, 0)
    for side, halo in enumerate((left, right)):
        for x in range(HALO):
            layer(
                x + side * (span_x + HALO),
                lambda c: halo[c, x],
                lambda c: corners[side, c, x],
                lambda c: corners[2 + side, c, x],
                False,
            )
    for x in range(ITERS):
        spread[x] = jnp.zeros(spread.shape[1:], f32)
        spread[span_x + ITERS + x] = jnp.zeros(spread.shape[1:], f32)

    markers = home.shape[1]
    blocks = markers // CHUNK
    total = blocks + lanes
    count = -(-(span_x + 1) // 8) * 8
    categories = []
    live = []
    for b in range(total):
        at = slice(b * CHUNK, (b + 1) * CHUNK)
        if b < blocks:
            record = home[:, at]
            group = lanes * spheres + record[SPHERE : SPHERE + 1]
        else:
            record = arrived[b - blocks]
            group = (b - blocks) * spheres + record[SPHERE : SPHERE + 1]
        alive = record[LIVE : LIVE + 1] > 0.5
        live.append(alive)
        categories.append(jnp.where(alive, record[X_ROW : X_ROW + 1], -1.0))
        first, rest = split(record)
        parts[0:RECORD, at] = first
        parts[RECORD : 2 * RECORD, at] = rest
        parts[SPHERE : SPHERE + 1, at] = group
    hot, upto, totals = ranks(categories, count)
    lower_rows = lax.broadcasted_iota(jnp.int32, (count, count), 0)
    lower_lanes = lax.broadcasted_iota(jnp.int32, (count, count), 1)
    before = (lower_lanes < lower_rows).astype(f32)
    starts = jnp.dot(
        before,
        jnp.broadcast_to(totals, (count, TILE_LANES)),
        precision=lax.Precision.HIGHEST,
        preferred_element_type=f32,
    )[:, 0:1]
    places = []
    for b in range(total):
        rank = jnp.sum(hot[b] * (upto[b] + (starts - 1.0)), axis=0, keepdims=True)
        places.append(jnp.where(live[b], rank, -1.0))
    where_to = jnp.concatenate(places, axis=1)
    alive_count = jnp.sum(totals).astype(jnp.int32)
    for first in range(0, total, GROUP):
        groups = range(first, min(first + GROUP, total))

        @pl.when(alive_count > first * CHUNK)
        def _(groups=groups):
            for g, piece in zip(groups, place(parts[...], where_to, groups)):
                sorted_refs[g] = piece

    sums[...] = jnp.zeros(sums.shape, f32)
    z_cells = lax.broadcasted_iota(jnp.int32, (extent_z, CHUNK), 0).astype(f32)
    y_cells = lax.broadcasted_iota(jnp.int32, (wide_y, CHUNK), 0).astype(f32) - HALO
    x_cells = lax.broadcasted_iota(jnp.int32, (WINDOW, CHUNK), 0).astype(f32)

    def chunk(j, carry):
        record = sorted_refs[j]
        alive = record[LIVE : LIVE + 1]
        cell_x = record[X_ROW : X_ROW + 1]
        distance = z_cells - record[Z_ROW : Z_ROW + 1]
        distance = jnp.where(distance < 0.0, distance + extent_z, distance)
        z_high, z_low = split(four(distance, record[8:12]))
        z_high = z_high.astype(bf16)
        z_low = z_low.astype(bf16)
        y_table = four(y_cells - record[Y_ROW : Y_ROW + 1], record[4:8])
        least = jnp.min(jnp.where(alive > 0.5, cell_x, 1e4)).astype(jnp.int32)
        most = jnp.max(jnp.where(alive > 0.5, cell_x, -1.0)).astype(jnp.int32)
        windows = (most + 4 - least + WINDOW - 1) // WINDOW

        def x_table(k):
            fresh = least + WINDOW * k
            base = jnp.minimum(fresh, layers - WINDOW)
            cells = x_cells + base.astype(f32)
            table = four(cells - cell_x, record[0:4])
            return base, jnp.where(cells >= fresh.astype(f32), table, 0.0)

        z_stack = jnp.concatenate([z_high, z_high, z_low], axis=0)

        def sample(k, total):
            base, table = x_table(k)
            rows = high.shape[1]
            first = high[pl.ds(base, WINDOW)].reshape(WINDOW * rows, extent_z)
            rest = low[pl.ds(base, WINDOW)].reshape(WINDOW * rows, extent_z)
            lines = jnp.dot(
                jnp.concatenate([first, rest, first], axis=1),
                z_stack,
                preferred_element_type=f32,
            )
            for x in range(WINDOW):
                total = total + lines[x * rows : x * rows + 3 * wide_y] * table[x : x + 1]
            return total

        plane = lax.fori_loop(0, windows, sample, jnp.zeros((3 * wide_y, CHUNK), f32))
        forces = []
        for c in range(3):
            got = jnp.sum(plane[c * wide_y : (c + 1) * wide_y] * y_table, axis=0, keepdims=True)
            forces.append((record[TARGET + c : TARGET + c + 1] - got) * alive)
        sheet = jnp.concatenate([force * y_table for force in forces], axis=0)
        z_wide = jnp.concatenate([z_high, z_high, z_low], axis=1)

        def deposit(k, carry):
            base, table = x_table(k)
            value = jnp.concatenate([sheet * table[x : x + 1] for x in range(WINDOW)], axis=0)
            first, rest = split(value)
            first = first.astype(bf16)
            rest = rest.astype(bf16)
            added = lax.dot_general(
                jnp.concatenate([first, rest, first], axis=1),
                z_wide,
                (((1,), (1,)), ((), ())),
                preferred_element_type=f32,
            )
            at = pl.ds(base + HALO, WINDOW)
            spread[at] = spread[at] + added.reshape(WINDOW, 3 * wide_y, extent_z)
            return carry

        lax.fori_loop(0, windows, deposit, 0)
        o = [record[OFFSET + c : OFFSET + c + 1] for c in range(3)]
        f = forces
        moments = jnp.concatenate(
            f
            + [
                o[1] * f[2] - o[2] * f[1],
                o[2] * f[0] - o[0] * f[2],
                o[0] * f[1] - o[1] * f[0],
                jnp.zeros((2, CHUNK), f32),
            ],
            axis=0,
        )
        group = record[SPHERE : SPHERE + 1]
        for g in range((lanes + 1) * spheres):
            sums[g] = sums[g] + jnp.where(group == float(g), moments, 0.0)
        return carry

    chunks = (alive_count + (CHUNK - 1)) // CHUNK
    lax.fori_loop(0, chunks, chunk, 0)
    tile[...] = jnp.sum(sums[...], axis=2)


def markers_stage(spheres, velocity, halos, home, arrived, motion):
    span_x, span_y, extent_z = velocity.shape[1:]
    wide_y = span_y + 2 * ITERS
    lanes = len(DIRECTIONS)
    f32 = jnp.float32
    total = home.shape[1] // CHUNK + lanes
    groups = (lanes + 1) * spheres
    field_rows = -(-3 * wide_y // 16) * 16
    field = (span_x + 2 * HALO, field_rows, extent_z)
    vmem = pl.BlockSpec(memory_space=pltpu.VMEM)
    return pl.pallas_call(
        functools.partial(markers_kernel, spheres),
        out_shape=[
            jax.ShapeDtypeStruct((span_x + 2 * ITERS, 3 * wide_y, extent_z), f32),
            jax.ShapeDtypeStruct((groups, 8), f32),
        ],
        in_specs=[vmem] * 9,
        out_specs=[vmem] * 2,
        scratch_shapes=[
            pltpu.VMEM(field, jnp.bfloat16),
            pltpu.VMEM(field, jnp.bfloat16),
            pltpu.VMEM((total, RECORD, CHUNK), f32),
            pltpu.VMEM((2 * RECORD, total * CHUNK), f32),
            pltpu.VMEM((groups, 8, CHUNK), f32),
        ],
        compiler_params=pltpu.CompilerParams(vmem_limit_bytes=56 * 2**20),
        name="markers",
    )(velocity, *halos, home, arrived, motion)


def combine_matrix(columns, rows, per_sphere):
    matrix = np.zeros((columns, rows, columns, rows, TILE_ROWS), np.float32)
    for i in range(columns):
        for j in range(rows):
            for slot, (dx, dy) in enumerate(DIRECTIONS):
                if 0 <= j - dy < rows:
                    matrix[(i - dx) % columns, j - dy, i, j, slot] -= RESPONSE / per_sphere
            matrix[i, j, i, j, len(DIRECTIONS)] -= RESPONSE / per_sphere
            matrix[i, j, i, j, len(DIRECTIONS) + 1] = 1.0
    return matrix.reshape(columns * rows, -1)


def tail_kernel(
    columns, rows, spread, tile, matrix, links,
    out, motion_out, from_left, from_right, from_below, from_above, corners, held,
    rhs, one, two, mask_ref, own_sem, send, recv, row_send, row_recv, col_send, col_recv,
):
    column = lax.axis_index("gx")
    row = lax.axis_index("gy")
    span_x, span_y, extent_z = out.shape[1:]
    wide_x, wide_y = span_x + 2 * ITERS, span_y + 2 * ITERS
    reach = ITERS + HALO
    row_peers = [lax.rem(row + k, rows) for k in range(1, rows)]
    column_peers = [lax.rem(column + k, columns) for k in range(1, columns)]
    barrier = pltpu.get_barrier_semaphore()
    for other in row_peers:
        pl.semaphore_signal(barrier, inc=1, device_id=(column, other), device_id_type=MESH)
    for other in column_peers:
        pl.semaphore_signal(barrier, inc=1, device_id=(other, row), device_id_type=MESH)
    own = pltpu.make_async_copy(tile, held.at[column, row], own_sem)
    own.start()

    def peer(dx, dy):
        return (lax.rem(column + dx + columns, columns), row + dy)

    edge = []
    for c in range(3):
        low, high = wide_y * c, wide_y * (c + 1)
        inner = slice(HALO, wide_x - HALO)
        edge += [
            (spread.at[span_x : span_x + reach, low:high], from_left.at[c], 1, 0),
            (spread.at[HALO : HALO + reach, low:high], from_right.at[c], -1, 0),
            (spread.at[inner, high - RIM : high], from_below.at[c], 0, 1),
            (spread.at[inner, low : low + RIM], from_above.at[c], 0, -1),
            (from_left.at[c, :, wide_y - RIM :], corners.at[c, 0], 0, 1),
            (from_right.at[c, :, wide_y - RIM :], corners.at[c, 1], 0, 1),
            (from_left.at[c, :, 0:RIM], corners.at[c, 2], 0, -1),
            (from_right.at[c, :, 0:RIM], corners.at[c, 3], 0, -1),
        ]

    def start(k):
        src, dst, dx, dy = edge[k]
        when(
            exists(row, rows, dy),
            lambda: remote(src, dst, send, recv, k, peer(dx, dy)).start(),
        )

    def arrive(k):
        src, dst, dx, dy = edge[k]
        when(
            exists(row, rows, -dy),
            lambda: remote(src, dst, send, recv, k, peer(dx, dy)).wait_recv(),
        )

    def sent(k):
        src, dst, dx, dy = edge[k]
        when(
            exists(row, rows, dy),
            lambda: remote(src, dst, send, recv, k, peer(dx, dy)).wait_send(),
        )

    @pl.when(row == 0)
    def _():
        from_below[...] = jnp.zeros(from_below.shape, jnp.float32)
        for c in range(3):
            corners[c, 0:2] = jnp.zeros((2,) + corners.shape[2:], jnp.float32)

    @pl.when(row == rows - 1)
    def _():
        from_above[...] = jnp.zeros(from_above.shape, jnp.float32)
        for c in range(3):
            corners[c, 2:4] = jnp.zeros((2,) + corners.shape[2:], jnp.float32)

    pl.semaphore_wait(barrier, rows + columns - 2)
    first = [
        pltpu.make_async_remote_copy(
            src_ref=tile,
            dst_ref=held.at[column, row],
            send_sem=row_send.at[k],
            recv_sem=row_recv.at[k],
            device_id=(column, other),
            device_id_type=MESH,
        )
        for k, other in enumerate(row_peers)
    ]
    for copy in first:
        copy.start()
    for k in range(4):
        start(k)
    for c in range(1, 3):
        for k in range(2, 4):
            start(8 * c + k)
    own.wait()
    for copy in first:
        copy.wait()
    second = [
        pltpu.make_async_remote_copy(
            src_ref=held.at[column],
            dst_ref=held.at[column],
            send_sem=col_send.at[k],
            recv_sem=col_recv.at[k],
            device_id=(other, row),
            device_id_type=MESH,
        )
        for k, other in enumerate(column_peers)
    ]
    for copy in second:
        copy.start()
    for c in range(1, 3):
        for k in range(2):
            start(8 * c + k)

    cells = lax.broadcasted_iota(jnp.int32, (wide_y, extent_z), 0) + (row * span_y - ITERS)
    inside = jnp.logical_and(cells >= 0, cells < span_y * rows)
    mask_ref[...] = inside.astype(jnp.float32)
    inverse = 1.0 / (1.0 + 6.0 * DIFFUSION)

    def relaxed(source, x):
        here = source[x]
        beside = source[x - 1] + source[x + 1]
        beside = beside + pltpu.roll(here, 1, 0) + pltpu.roll(here, wide_y - 1, 0)
        beside = beside + pltpu.roll(here, 1, 1) + pltpu.roll(here, extent_z - 1, 1)
        return (rhs[x] + DIFFUSION * beside) * (inverse * mask_ref[...])

    for c in range(3):
        at = slice(wide_y * c, wide_y * (c + 1))
        for k in range(4):
            arrive(8 * c + k)
        for k in range(4, 8):
            start(8 * c + k)

        def build(x, carry, at=at, c=c):
            rhs[x] = spread[x, at]
            return carry

        lax.fori_loop(0, wide_x, build, 0)
        for x in range(reach):
            rhs[x] = rhs[x] + from_left[c, x]
            rhs[x + span_x + HALO] = rhs[x + span_x + HALO] + from_right[c, x]

        def rims(x, carry, c=c):
            y = x + HALO
            rhs[y, 0:RIM] = rhs[y, 0:RIM] + from_below[c, x]
            rhs[y, wide_y - RIM :] = rhs[y, wide_y - RIM :] + from_above[c, x]
            return carry

        lax.fori_loop(0, wide_x - 2 * HALO, rims, 0)
        for k in range(4, 8):
            arrive(8 * c + k)
        for x in range(reach):
            for side, y in enumerate((x, x + span_x + HALO)):
                rhs[y, 0:RIM] = rhs[y, 0:RIM] + corners[c, side, x]
                rhs[y, wide_y - RIM :] = rhs[y, wide_y - RIM :] + corners[c, 2 + side, x]

        def masked(x, carry):
            rhs[x] = rhs[x] * mask_ref[...]
            return carry

        lax.fori_loop(0, wide_x, masked, 0)
        source = rhs
        for sweep in range(ITERS - 1):
            target = one if sweep % 2 == 0 else two

            def step(pair, carry, source=source, target=target, first=sweep + 1):
                x = first + 2 * pair
                new = (relaxed(source, x), relaxed(source, x + 1))
                target[x] = new[0]
                target[x + 1] = new[1]
                return carry

            lax.fori_loop(0, wide_x // 2 - sweep - 1, step, 0)
            source = target

        def last(pair, carry, source=source, c=c):
            x = 2 * pair
            new = (relaxed(source, x + ITERS), relaxed(source, x + ITERS + 1))
            out[c, x] = new[0][ITERS : ITERS + span_y]
            out[c, x + 1] = new[1][ITERS : ITERS + span_y]
            return carry

        lax.fori_loop(0, span_x // 2, last, 0)

    for copy in second:
        copy.wait()
    gathered = held[...].reshape(-1, TILE_LANES)
    moved = jnp.dot(
        matrix[...],
        gathered,
        precision=lax.Precision.HIGHEST,
        preferred_element_type=jnp.float32,
    )
    motion_out[...] = jnp.dot(
        links[...],
        moved,
        precision=lax.Precision.HIGHEST,
        preferred_element_type=jnp.float32,
    )
    for k in range(len(edge)):
        sent(k)


def tail(spread, tile, matrix, links, span_y):
    columns, rows = lax.axis_size("gx"), lax.axis_size("gy")
    wide_x, _, extent_z = spread.shape
    span_x = wide_x - 2 * ITERS
    wide_y = span_y + 2 * ITERS
    reach = ITERS + HALO
    f32 = jnp.float32
    vmem = pl.BlockSpec(memory_space=pltpu.VMEM)
    dma = pltpu.SemaphoreType.DMA
    return pl.pallas_call(
        functools.partial(tail_kernel, columns, rows),
        out_shape=[
            jax.ShapeDtypeStruct((3, span_x, span_y, extent_z), f32),
            jax.ShapeDtypeStruct((links.shape[0], TILE_LANES), f32),
        ],
        in_specs=[vmem] * 4,
        out_specs=[vmem] * 2,
        scratch_shapes=[
            pltpu.VMEM((3, reach, wide_y, extent_z), f32),
            pltpu.VMEM((3, reach, wide_y, extent_z), f32),
            pltpu.VMEM((3, wide_x - 2 * HALO, RIM, extent_z), f32),
            pltpu.VMEM((3, wide_x - 2 * HALO, RIM, extent_z), f32),
            pltpu.VMEM((3, 4, reach, RIM, extent_z), f32),
            pltpu.VMEM((columns, rows) + tile.shape, f32),
            pltpu.VMEM((wide_x, wide_y, extent_z), f32),
            pltpu.VMEM((wide_x, wide_y, extent_z), f32),
            pltpu.VMEM((wide_x, wide_y, extent_z), f32),
            pltpu.VMEM((wide_y, extent_z), f32),
            dma,
            dma((24,)),
            dma((24,)),
            dma((rows - 1,)),
            dma((rows - 1,)),
            dma((columns - 1,)),
            dma((columns - 1,)),
        ],
        compiler_params=pltpu.CompilerParams(
            collective_id=1, has_side_effects=True, vmem_limit_bytes=56 * 2**20
        ),
        name="tail",
    )(spread, tile, matrix, links)


def on_device(
    velocity,
    owner_block,
    base_x,
    base_y,
    base_z,
    delta_weights,
    marker_offset,
    sphere_motion,
    contact_sphere,
    contact_partner,
):
    span_y = velocity.shape[2]
    row_count = lax.axis_size("gy")
    column_count = lax.axis_size("gx")
    here = lax.axis_index(("gx", "gy"))
    devices = row_count * column_count
    spheres = sphere_motion.shape[1]
    per_sphere = base_x.shape[0] // spheres
    lanes = len(DIRECTIONS)
    ids = jnp.stack([owner_block[:, 0], base_x, base_y, base_z]).astype(jnp.float32)
    home, arrived, *halos = front(ids, delta_weights, marker_offset, sphere_motion, velocity)
    spread, sums = markers_stage(spheres, velocity, halos, home, arrived, sphere_motion)
    sums = sums[:, :6].reshape(lanes + 1, spheres * 6)
    tile = jnp.concatenate([sums, sphere_motion.T.reshape(1, spheres * 6)], axis=0)
    tile = jnp.pad(tile, ((0, TILE_ROWS - tile.shape[0]), (0, TILE_LANES - tile.shape[1])))
    mine = here * spheres + jnp.arange(spheres, dtype=jnp.int32)
    known = jnp.arange(devices * spheres, dtype=jnp.int32)
    own = (mine[:, None] == known[None, :]).astype(jnp.float32)
    acts = (contact_sphere[None, :] == mine[:, None]).astype(jnp.float32)
    partner = (contact_partner[:, None] == known[None, :]).astype(jnp.float32)
    linked = jnp.sum(acts[:, :, None] * partner[None], axis=1)
    linked = own + DASHPOT * (linked - jnp.sum(acts, axis=1)[:, None] * own)
    both = jnp.concatenate([linked, own], axis=0)
    links = both.reshape(2 * spheres, devices, spheres).transpose(0, 2, 1)
    links = links.reshape(2 * spheres * spheres, devices)
    matrix = jnp.asarray(combine_matrix(column_count, row_count, per_sphere))
    state, motion = tail(spread, tile, matrix, links, span_y)
    motion = motion.reshape(2, spheres, spheres, TILE_LANES)
    linear = sum(motion[0, :, s, 6 * s : 6 * s + 3] for s in range(spheres))
    angular = sum(motion[1, :, s, 6 * s + 3 : 6 * s + 6] for s in range(spheres))
    return state, jnp.concatenate([linear, angular], axis=1).T


def solution(mesh):
    placed = (
        P(None, "gx", "gy", None),
        P(("gx", "gy"), None),
        P(("gx", "gy")),
        P(("gx", "gy")),
        P(("gx", "gy")),
        P(None, ("gx", "gy")),
        P(None, ("gx", "gy")),
        P(None, ("gx", "gy")),
        P(("gx", "gy")),
        P(("gx", "gy")),
    )
    return jax.shard_map(
        on_device,
        mesh=mesh,
        in_specs=placed,
        out_specs=(P(None, "gx", "gy", None), P(None, ("gx", "gy"))),
        check_vma=False,
    )
```

time: 188 us -> 110 us (0.59)
  Pallas kernels: 39.3 us -> 98.8 us
  matrix products: 45 us -> 0 us
  waiting for transfers between devices: 36.9 us -> 0 us
  starting transfers between devices: 27.5 us -> 0 us
  other arithmetic: 17.9 us -> 3.24 us
  local copies, waits for them, and re-layouts: 18.9 us -> 6.67 us
    pallas_call x2 -> x3, Pallas kernels: 39.3 us -> 98.8 us  [the longest x1 53.3 us: tail(): pl.pallas_call(functools.partial(tail_kernel, columns, rows), out_shape=[...]
    dot_general x5 -> x0, matrix products: 43.8 us -> none  [the longest x2 24.3 us: sample_field(): jnp.dot(field.reshape(-1, extent_z), table_z, precision=lax.Precision.HIGH)]
    ppermute x12 -> x0, waiting for transfers between devices: 36.9 us -> none  [shift(): return lax.ppermute(array, axis, pairs)]
    ppermute x12 -> x0, starting transfers between devices: 27.5 us -> none  [shift(): return lax.ppermute(array, axis, pairs)]
    slice x23 -> x1, local copies, waits for them, and re-layouts: 7.08 us -> 0.84 us  [on_device(): linear = sum((motion[0, :, s, 6 * s:6 * s + 3] for s in range(spheres)))]
    add x8 -> x3, other arithmetic: 5.95 us -> 0.09 us  [the longest x1 0.08 us: on_device(): linked = own + DASHPOT * (linked - jnp.sum(acts, axis=1)[:, None] * own)]
    scatter x1 -> x0, local copies, waits for them, and re-layouts: 5.85 us -> none  [on_device(): outgoing = jnp.zeros((payload.shape[0], total_slots), jnp.float32).at[:,...]
    unnamed x33 -> x8, local copies, waits for them, and re-layouts: 1.54 us -> 4.1 us
  transfers between devices with their start and end apart: 12 -> 0, of which waited for: 7 -> 0; matrix products, arithmetic and copies ran while one was open for 12% -> 0% of each run, Pallas kernels for 12% -> 0%
where the time goes in v1:
time: 110 us; the launch traced here: 109 us
  Pallas kernels  98.8 us (90%)
  local copies, waits for them, and re-layouts  6.67 us (6%)
  other arithmetic  3.24 us (3%)
    pallas_call x1, Pallas kernels, tail(): pl.pallas_call(functools.partial(tail_kernel, columns, rows), out_shape=[...  53.3 us
    pallas_call x1, Pallas kernels, markers_stage(): pl.pallas_call(functools.partial(markers_kernel, spheres), out_shape=[jax...  22.9 us
    pallas_call x1, Pallas kernels, front(): pl.pallas_call(functools.partial(front_kernel, columns, rows), out_shape=...  22.6 us
    unnamed x8, local copies, waits for them, and re-layouts  4.1 us

profile of v1, /device:TPU:1, one launch (start us, length us, event | category | flops | bytes accessed | tf_op | source)
XLA Modules:
  0.0 109.4 jit_solution(7356515838659664687)
XLA Ops:
  0.6 1.4 %copy.36.motion = f32[6,2]{1,0:T(8,128)} copy(f32[6,2]{0,1:T(2,128)} %param.18) | data formatting | bytes 96 | tf_op args[7]
  2.0 1.4 %add_convert_fusion.ids = f32[4,2048]{1,0:T(4,128)} fusion(s32[1,2048]{1,0:T(1,128)} %bitcast.22, s32[1,2048]{1,0:T(1,128)} %bitcast.23, s32[1,2048]{1,0:T(1,128)} %bitcast.24, s32[1,2048]{1,0:T(1,128)} %bitcast.25), kind=kLoop, calls=%fused_computation.5 | loop fusion | flops 32768 | bytes 65536 | tf_op jit(solution)/shard_map/convert_element_type | solution.py:779
  3.4 22.6 %front.1 = (f32[24,2048]{1,0:T(8,128)}, f32[8,24,256]{2,1,0:T(8,128)}, f32[3,2,32,256]{3,2,1,0:T(8,128)}, f32[3,2,32,256]{3,2,1,0:T(8,128)}, f32[3,16,8,256]{3,2...) custom-call(f32[4,2048]{1,0:T(4,128)} %add_convert_fusion.ids, f32[12,2048]{1,0:T(8,128)} %weights.1, ...), custom_call_target="tpu_custom_call" | custom-call | tf_op jit(solution)/shard_map/front/pallas_call | solution.py:260
  26.0 0.0 copy-start
  26.0 0.0 copy-start.2
  26.0 0.0 copy-start.1
  26.0 22.9 %markers.1 = (f32[24,120,256]{2,1,0:T(8,128)}, f32[18,8]{1,0:T(8,128)}) custom-call(f32[3,16,32,256]{3,2,1,0:T(8,128)} %velocity.3, f32[3,2,32,256]{3,2,1,0:T(8,128)} %get-tuple-element.13.left, f32[3,2,32,256]{3,2,1,0:T(8,128)} %get-tuple-element.14.right, f32[3,16,8,256]{3,2,1,0:T(8,128)} %get-tuple-element.15.below, ...), custom_call_target="tpu_custom_call" | custom-call | tf_op jit(solution)/shard_map/markers/pallas_call | solution.py:485
  48.9 0.8 reshape.100
  49.7 0.0 copy-done
  49.7 0.1 reshape.101
  49.8 0.6 select_maximum_fusion.tile
  50.4 0.0 copy-done.2
  50.4 0.1 compare_convert_fusion.1
  50.5 0.0 copy-done.1
  50.5 0.1 fusion.3
  50.6 0.1 multiply_reduce_fusion
  50.6 0.1 reduce_sum.21
  50.8 0.2 fusion.4
  50.9 0.1 fusion.2
  51.0 0.1 copy.38
  51.1 0.1 compare_convert_fusion
  51.2 0.1 copy.39
  51.3 0.6 copy.40
  51.9 53.3 %tail.1 = (f32[3,16,32,256]{3,2,1,0:T(8,128)}, f32[8,128]{1,0:T(8,128)}) custom-call(f32[24,120,256]{2,1,0:T(8,128)} %get-tuple-element.20.spread, f32[16,128]{1,0:T(8,128)} %select_maximum_fusion.tile, f32[32,512]{1,0:T(8,128)} %constant.24.clone.matrix, f32[8,32]{1,0:T(8,128)} %bitcast.20), custom_call_target="tpu_custom_call" | custom-call | tf_op jit(solution)/shard_map/tail/pallas_call | solution.py:725
  105.2 0.8 fusion.5
  106.0 0.6 maximum_bitcast_fusion.1
  106.7 2.7 %copy.50 = f32[3,16,32,256]{3,2,1,0:T(8,128)} copy(f32[3,16,32,256]{3,2,1,0:T(8,128)} %get-tuple-element.32) | data formatting | bytes 3145728
  (4 shorter events, 0.0 us)
Async XLA Ops:
  26.0 23.7 %copy-start = (f32[6,2]{0,1:T(2,128)S(1)}, f32[6,2]{0,1:T(2,128)}, u32[]{:S(2)}) copy-start(f32[6,2]{0,1:T(2,128)} %param.18) | copy-start | bytes 148
  26.0 24.4 %copy-start.2 = (s32[4]{0:T(128)S(1)}, s32[4]{0:T(128)}, u32[]{:S(2)}) copy-start(s32[4]{0:T(128)} %param.19) | copy-start | bytes 52
  26.0 24.5 %copy-start.1 = (s32[4]{0:T(128)S(1)}, s32[4]{0:T(128)}, u32[]{:S(2)}) copy-start(s32[4]{0:T(128)} %param.20) | copy-start | bytes 52

commit v2 on v1

--- a/solution.py
+++ b/solution.py
@@ -111,7 +111,7 @@
 
 
 def front_kernel(
-    columns, rows, ids, weights, offsets, motion, velocity,
+    columns, rows, owners, base_x, base_y, base_z, weights, offsets, motion, velocity,
     home, arrived, left, right, below, above, corners, slots, send, recv,
 ):
     column = lax.axis_index("gx")
@@ -177,10 +177,10 @@
     for k in range(4):
         start(k)
 
-    markers = ids.shape[1]
-    spheres = motion.shape[1]
+    markers = owners.shape[1]
+    spheres = motion.shape[0]
     per_sphere = markers // spheres
-    owner = ids[0:1]
+    owner = owners[...].astype(jnp.float32)
     owner_x = jnp.floor((owner + 0.5) * (1.0 / rows))
     owner_y = owner - owner_x * rows
     step_x = owner_x - column.astype(jnp.float32)
@@ -194,7 +194,7 @@
     targets = []
     for s in range(spheres):
         o = offset[:, s * per_sphere : (s + 1) * per_sphere]
-        m = [motion[c : c + 1, s : s + 1] for c in range(6)]
+        m = [motion[s : s + 1, c : c + 1] for c in range(6)]
         targets.append(
             jnp.concatenate(
                 [
@@ -206,7 +206,8 @@
             )
         )
     home[0:12] = weights[...]
-    home[X_ROW : Z_ROW + 1] = ids[1:4]
+    for line, base in ((X_ROW, base_x), (Y_ROW, base_y), (Z_ROW, base_z)):
+        home[line : line + 1] = base[...].astype(jnp.float32)
     home[TARGET : TARGET + 3] = jnp.concatenate(targets, axis=1)
     home[OFFSET : OFFSET + 3] = offset
     position = lax.broadcasted_iota(jnp.int32, (1, markers), 1)
@@ -228,10 +229,10 @@
         slots[g] = piece
     home[LIVE : LIVE + 1] = at_home.astype(jnp.float32)
 
+    for k in range(8, 8 + lanes):
+        start(k)
     arrive(0)
     arrive(1)
-    for k in range(8, 8 + lanes):
-        start(k)
     for k in range(4, 8):
         start(k)
     for k in range(2, 8 + lanes):
@@ -240,10 +241,10 @@
         sent(k)
 
 
-def front(ids, weights, offsets, motion, velocity):
+def front(owners, bases, weights, offsets, motion, velocity):
     columns, rows = lax.axis_size("gx"), lax.axis_size("gy")
     span_x, span_y, extent_z = velocity.shape[1:]
-    markers = ids.shape[1]
+    markers = owners.shape[1]
     lanes = len(DIRECTIONS)
     f32 = jnp.float32
     copies = 8 + lanes
@@ -260,7 +261,7 @@
     return pl.pallas_call(
         functools.partial(front_kernel, columns, rows),
         out_shape=[jax.ShapeDtypeStruct(shape, f32) for shape in out],
-        in_specs=[vmem] * 5,
+        in_specs=[vmem] * 8,
         out_specs=[vmem] * len(out),
         scratch_shapes=[
             pltpu.VMEM((lanes, RECORD, CHUNK), f32),
@@ -269,7 +270,7 @@
         ],
         compiler_params=pltpu.CompilerParams(collective_id=0, has_side_effects=True),
         name="front",
-    )(ids, weights, offsets, motion, velocity)
+    )(owners, *bases, weights, offsets, motion, velocity)
 
 
 def four(distance, weights):
@@ -281,7 +282,7 @@
 
 def markers_kernel(
     spheres, velocity, left, right, below, above, corners, home, arrived, motion,
-    spread, tile, high, low, sorted_refs, parts, sums,
+    spread, edges, tile, high, low, sorted_refs, parts, sums,
 ):
     span_x, span_y, extent_z = velocity.shape[1:]
     wide_y = span_y + 2 * ITERS
@@ -348,10 +349,10 @@
         at = slice(b * CHUNK, (b + 1) * CHUNK)
         if b < blocks:
             record = home[:, at]
-            group = lanes * spheres + record[SPHERE : SPHERE + 1]
+            group = lanes + record[SPHERE : SPHERE + 1] * (lanes + 1)
         else:
             record = arrived[b - blocks]
-            group = (b - blocks) * spheres + record[SPHERE : SPHERE + 1]
+            group = (b - blocks) + record[SPHERE : SPHERE + 1] * (lanes + 1)
         alive = record[LIVE : LIVE + 1] > 0.5
         live.append(alive)
         categories.append(jnp.where(alive, record[X_ROW : X_ROW + 1], -1.0))
@@ -469,7 +470,20 @@
 
     chunks = (alive_count + (CHUNK - 1)) // CHUNK
     lax.fori_loop(0, chunks, chunk, 0)
-    tile[...] = jnp.sum(sums[...], axis=2)
+    columns = jnp.sum(sums[...], axis=2)
+    tile[...] = jnp.zeros(tile.shape, f32)
+    for s in range(spheres):
+        at = slice(6 * s, 6 * (s + 1))
+        tile[0 : lanes + 1, at] = columns[(lanes + 1) * s : (lanes + 1) * (s + 1), 0:6]
+        tile[lanes + 1 : lanes + 2, at] = motion[s : s + 1]
+    reach = ITERS + HALO
+    depth = span_y + 2 * HALO
+    for side, first in enumerate((span_x, HALO)):
+        for c in range(3):
+            for x in range(reach):
+                edges[side, c, depth * x : depth * (x + 1)] = spread[
+                    first + x, wide_y * c + HALO : wide_y * (c + 1) - HALO
+                ]
 
 
 def markers_stage(spheres, velocity, halos, home, arrived, motion):
@@ -486,10 +500,11 @@
         functools.partial(markers_kernel, spheres),
         out_shape=[
             jax.ShapeDtypeStruct((span_x + 2 * ITERS, 3 * wide_y, extent_z), f32),
-            jax.ShapeDtypeStruct((groups, 8), f32),
+            jax.ShapeDtypeStruct((2, 3, (ITERS + HALO) * (span_y + 2 * HALO), extent_z), f32),
+            jax.ShapeDtypeStruct((TILE_ROWS, TILE_LANES), f32),
         ],
         in_specs=[vmem] * 9,
-        out_specs=[vmem] * 2,
+        out_specs=[vmem] * 3,
         scratch_shapes=[
             pltpu.VMEM(field, jnp.bfloat16),
             pltpu.VMEM(field, jnp.bfloat16),
@@ -515,8 +530,8 @@
 
 
 def tail_kernel(
-    columns, rows, spread, tile, matrix, links,
-    out, motion_out, from_left, from_right, from_below, from_above, corners, held,
+    columns, rows, spread, edges, tile, matrix, contact_sphere, contact_partner,
+    out, motion_out, from_left, from_right, from_below, from_above, given, corners, held,
     rhs, one, two, mask_ref, own_sem, send, recv, row_send, row_recv, col_send, col_recv,
 ):
     column = lax.axis_index("gx")
@@ -524,6 +539,7 @@
     span_x, span_y, extent_z = out.shape[1:]
     wide_x, wide_y = span_x + 2 * ITERS, span_y + 2 * ITERS
     reach = ITERS + HALO
+    depth = span_y + 2 * HALO
     row_peers = [lax.rem(row + k, rows) for k in range(1, rows)]
     column_peers = [lax.rem(column + k, columns) for k in range(1, columns)]
     barrier = pltpu.get_barrier_semaphore()
@@ -542,14 +558,14 @@
         low, high = wide_y * c, wide_y * (c + 1)
         inner = slice(HALO, wide_x - HALO)
         edge += [
-            (spread.at[span_x : span_x + reach, low:high], from_left.at[c], 1, 0),
-            (spread.at[HALO : HALO + reach, low:high], from_right.at[c], -1, 0),
+            (edges.at[0, c], from_left.at[c], 1, 0),
+            (edges.at[1, c], from_right.at[c], -1, 0),
             (spread.at[inner, high - RIM : high], from_below.at[c], 0, 1),
             (spread.at[inner, low : low + RIM], from_above.at[c], 0, -1),
-            (from_left.at[c, :, wide_y - RIM :], corners.at[c, 0], 0, 1),
-            (from_right.at[c, :, wide_y - RIM :], corners.at[c, 1], 0, 1),
-            (from_left.at[c, :, 0:RIM], corners.at[c, 2], 0, -1),
-            (from_right.at[c, :, 0:RIM], corners.at[c, 3], 0, -1),
+            (given.at[c, 0], corners.at[c, 0], 0, 1),
+            (given.at[c, 1], corners.at[c, 1], 0, 1),
+            (given.at[c, 2], corners.at[c, 2], 0, -1),
+            (given.at[c, 3], corners.at[c, 3], 0, -1),
         ]
 
     def start(k):
@@ -604,6 +620,13 @@
     for c in range(1, 3):
         for k in range(2, 4):
             start(8 * c + k)
+
+    cells = lax.broadcasted_iota(jnp.int32, (wide_y, extent_z), 0) + (row * span_y - ITERS)
+    inside = jnp.logical_and(cells >= 0, cells < span_y * rows)
+    inverse = 1.0 / (1.0 + 6.0 * DIFFUSION)
+    mask_ref[0] = inside.astype(jnp.float32)
+    mask_ref[1] = inside.astype(jnp.float32) * inverse
+
     own.wait()
     for copy in first:
         copy.wait()
@@ -624,75 +647,72 @@
         for k in range(2):
             start(8 * c + k)
 
-    cells = lax.broadcasted_iota(jnp.int32, (wide_y, extent_z), 0) + (row * span_y - ITERS)
-    inside = jnp.logical_and(cells >= 0, cells < span_y * rows)
-    mask_ref[...] = inside.astype(jnp.float32)
-    inverse = 1.0 / (1.0 + 6.0 * DIFFUSION)
-
-    def relaxed(source, x):
-        here = source[x]
-        beside = source[x - 1] + source[x + 1]
+    def relaxed(c, source, x):
+        here = source[c, x]
+        beside = source[c, x - 1] + source[c, x + 1]
         beside = beside + pltpu.roll(here, 1, 0) + pltpu.roll(here, wide_y - 1, 0)
         beside = beside + pltpu.roll(here, 1, 1) + pltpu.roll(here, extent_z - 1, 1)
-        return (rhs[x] + DIFFUSION * beside) * (inverse * mask_ref[...])
+        return (rhs[c, x] + DIFFUSION * beside) * mask_ref[1]
+
+    buffers = (rhs, one, two, one)
+
+    def sweeps(c, starts, length):
+        for sweep in range(ITERS):
+            source = buffers[sweep]
+            for first, shift in starts:
+                begin = first + sweep * shift
+                for x in range(begin, begin + length(sweep)):
+                    new = relaxed(c, source, x)
+                    if sweep == ITERS - 1:
+                        out[c, x - ITERS] = new[ITERS : ITERS + span_y]
+                    else:
+                        buffers[sweep + 1][c, x] = new
+
+    def base(c, carry):
+        for x in range(wide_x):
+            rhs[c, x] = spread[x, pl.ds(pl.multiple_of(wide_y * c, 8), wide_y)]
+        for x in range(wide_x - 2 * HALO):
+            y = x + HALO
+            rhs[c, y, 0:RIM] = rhs[c, y, 0:RIM] + from_below[c, x]
+            rhs[c, y, wide_y - RIM :] = rhs[c, y, wide_y - RIM :] + from_above[c, x]
+        for x in range(reach, wide_x - reach):
+            rhs[c, x] = rhs[c, x] * mask_ref[0]
+        sweeps(c, ((reach + 1, 1),), lambda sweep: span_x - 2 * HALO - 2 - 2 * sweep)
+        return carry
 
     for c in range(3):
-        at = slice(wide_y * c, wide_y * (c + 1))
-        for k in range(4):
-            arrive(8 * c + k)
+        arrive(8 * c + 2)
+        arrive(8 * c + 3)
+    lax.fori_loop(0, 3, base, 0)
+
+    def outer(c):
+        for x in range(reach):
+            for side, y in enumerate((x, x + span_x + HALO)):
+                at = slice(6 * x, 6 * (x + 1))
+                rhs[c, y, 0:6] = rhs[c, y, 0:6] + corners[c, side, at]
+                rhs[c, y, wide_y - 6 :] = rhs[c, y, wide_y - 6 :] + corners[c, 2 + side, at]
+                rhs[c, y] = rhs[c, y] * mask_ref[0]
+        sweeps(c, ((1, 1), (span_x + 1, -1)), lambda sweep: reach)
+
+    for c in range(3):
+        arrive(8 * c)
+        arrive(8 * c + 1)
+        for side, halo in enumerate((from_left, from_right)):
+            for up, first in ((0, depth - reach), (2, 0)):
+                pieces = [
+                    halo[c, depth * x + first : depth * x + first + reach] for x in range(reach)
+                ]
+                given[c, up + side, 0 : reach * reach] = jnp.concatenate(pieces, axis=0)
+        for x in range(reach):
+            for halo, y in ((from_left, x), (from_right, x + span_x + HALO)):
+                rhs[c, y, HALO : wide_y - HALO] = (
+                    rhs[c, y, HALO : wide_y - HALO] + halo[c, depth * x : depth * (x + 1)]
+                )
         for k in range(4, 8):
             start(8 * c + k)
-
-        def build(x, carry, at=at, c=c):
-            rhs[x] = spread[x, at]
-            return carry
-
-        lax.fori_loop(0, wide_x, build, 0)
-        for x in range(reach):
-            rhs[x] = rhs[x] + from_left[c, x]
-            rhs[x + span_x + HALO] = rhs[x + span_x + HALO] + from_right[c, x]
-
-        def rims(x, carry, c=c):
-            y = x + HALO
-            rhs[y, 0:RIM] = rhs[y, 0:RIM] + from_below[c, x]
-            rhs[y, wide_y - RIM :] = rhs[y, wide_y - RIM :] + from_above[c, x]
-            return carry
-
-        lax.fori_loop(0, wide_x - 2 * HALO, rims, 0)
         for k in range(4, 8):
             arrive(8 * c + k)
-        for x in range(reach):
-            for side, y in enumerate((x, x + span_x + HALO)):
-                rhs[y, 0:RIM] = rhs[y, 0:RIM] + corners[c, side, x]
-                rhs[y, wide_y - RIM :] = rhs[y, wide_y - RIM :] + corners[c, 2 + side, x]
-
-        def masked(x, carry):
-            rhs[x] = rhs[x] * mask_ref[...]
-            return carry
-
-        lax.fori_loop(0, wide_x, masked, 0)
-        source = rhs
-        for sweep in range(ITERS - 1):
-            target = one if sweep % 2 == 0 else two
-
-            def step(pair, carry, source=source, target=target, first=sweep + 1):
-                x = first + 2 * pair
-                new = (relaxed(source, x), relaxed(source, x + 1))
-                target[x] = new[0]
-                target[x + 1] = new[1]
-                return carry
-
-            lax.fori_loop(0, wide_x // 2 - sweep - 1, step, 0)
-            source = target
-
-        def last(pair, carry, source=source, c=c):
-            x = 2 * pair
-            new = (relaxed(source, x + ITERS), relaxed(source, x + ITERS + 1))
-            out[c, x] = new[0][ITERS : ITERS + span_y]
-            out[c, x + 1] = new[1][ITERS : ITERS + span_y]
-            return carry
-
-        lax.fori_loop(0, span_x // 2, last, 0)
+        outer(c)
 
     for copy in second:
         copy.wait()
@@ -703,17 +723,38 @@
         precision=lax.Precision.HIGHEST,
         preferred_element_type=jnp.float32,
     )
-    motion_out[...] = jnp.dot(
-        links[...],
-        moved,
-        precision=lax.Precision.HIGHEST,
-        preferred_element_type=jnp.float32,
+    spheres = motion_out.shape[0]
+    device = lax.broadcasted_iota(jnp.int32, (1, columns * rows), 1)
+    here = column * rows + row
+    linked, owned = [], []
+    for s in range(spheres):
+        mine = here * spheres + s
+        for other in range(spheres):
+            own_row = (device * spheres + other == mine).astype(jnp.float32)
+            line = own_row
+            for k in range(contact_sphere.shape[0]):
+                acts = contact_sphere[k] == mine
+                partner = (device * spheres + other == contact_partner[k]).astype(jnp.float32)
+                line = line + jnp.where(acts, DASHPOT * (partner - own_row), 0.0)
+            linked.append(line)
+            owned.append(own_row)
+    links = jnp.concatenate(linked + owned, axis=0)
+    result = jnp.dot(
+        links, moved, precision=lax.Precision.HIGHEST, preferred_element_type=jnp.float32
     )
+    for s in range(spheres):
+        for part in range(2):
+            total = 0.0
+            for other in range(spheres):
+                line = (part * spheres + s) * spheres + other
+                at = 6 * other + 3 * part
+                total = total + result[line : line + 1, at : at + 3]
+            motion_out[s : s + 1, 3 * part : 3 * part + 3] = total
     for k in range(len(edge)):
         sent(k)
 
 
-def tail(spread, tile, matrix, links, span_y):
+def tail(spread, edges, tile, matrix, contact_sphere, contact_partner, span_y, spheres):
     columns, rows = lax.axis_size("gx"), lax.axis_size("gy")
     wide_x, _, extent_z = spread.shape
     span_x = wide_x - 2 * ITERS
@@ -721,26 +762,30 @@
     reach = ITERS + HALO
     f32 = jnp.float32
     vmem = pl.BlockSpec(memory_space=pltpu.VMEM)
+    smem = pl.BlockSpec(memory_space=pltpu.SMEM)
     dma = pltpu.SemaphoreType.DMA
+    corner = (3, 4, -(-reach * reach // 8) * 8, extent_z)
+    frame = (3, wide_x, wide_y, extent_z)
     return pl.pallas_call(
         functools.partial(tail_kernel, columns, rows),
         out_shape=[
             jax.ShapeDtypeStruct((3, span_x, span_y, extent_z), f32),
-            jax.ShapeDtypeStruct((links.shape[0], TILE_LANES), f32),
+            jax.ShapeDtypeStruct((spheres, 6), f32),
         ],
-        in_specs=[vmem] * 4,
+        in_specs=[vmem] * 4 + [smem] * 2,
         out_specs=[vmem] * 2,
         scratch_shapes=[
-            pltpu.VMEM((3, reach, wide_y, extent_z), f32),
-            pltpu.VMEM((3, reach, wide_y, extent_z), f32),
+            pltpu.VMEM(edges.shape[1:], f32),
+            pltpu.VMEM(edges.shape[1:], f32),
             pltpu.VMEM((3, wide_x - 2 * HALO, RIM, extent_z), f32),
             pltpu.VMEM((3, wide_x - 2 * HALO, RIM, extent_z), f32),
-            pltpu.VMEM((3, 4, reach, RIM, extent_z), f32),
+            pltpu.VMEM(corner, f32),
+            pltpu.VMEM(corner, f32),
             pltpu.VMEM((columns, rows) + tile.shape, f32),
-            pltpu.VMEM((wide_x, wide_y, extent_z), f32),
-            pltpu.VMEM((wide_x, wide_y, extent_z), f32),
-            pltpu.VMEM((wide_x, wide_y, extent_z), f32),
-            pltpu.VMEM((wide_y, extent_z), f32),
+            pltpu.VMEM(frame, f32),
+            pltpu.VMEM(frame, f32),
+            pltpu.VMEM(frame, f32),
+            pltpu.VMEM((2, wide_y, extent_z), f32),
             dma,
             dma((24,)),
             dma((24,)),
@@ -753,7 +798,7 @@
             collective_id=1, has_side_effects=True, vmem_limit_bytes=56 * 2**20
         ),
         name="tail",
-    )(spread, tile, matrix, links)
+    )(spread, edges, tile, matrix, contact_sphere, contact_partner)
 
 
 def on_device(
@@ -769,35 +814,19 @@
     contact_partner,
 ):
     span_y = velocity.shape[2]
-    row_count = lax.axis_size("gy")
-    column_count = lax.axis_size("gx")
-    here = lax.axis_index(("gx", "gy"))
-    devices = row_count * column_count
+    markers = base_x.shape[0]
     spheres = sphere_motion.shape[1]
-    per_sphere = base_x.shape[0] // spheres
-    lanes = len(DIRECTIONS)
-    ids = jnp.stack([owner_block[:, 0], base_x, base_y, base_z]).astype(jnp.float32)
-    home, arrived, *halos = front(ids, delta_weights, marker_offset, sphere_motion, velocity)
-    spread, sums = markers_stage(spheres, velocity, halos, home, arrived, sphere_motion)
-    sums = sums[:, :6].reshape(lanes + 1, spheres * 6)
-    tile = jnp.concatenate([sums, sphere_motion.T.reshape(1, spheres * 6)], axis=0)
-    tile = jnp.pad(tile, ((0, TILE_ROWS - tile.shape[0]), (0, TILE_LANES - tile.shape[1])))
-    mine = here * spheres + jnp.arange(spheres, dtype=jnp.int32)
-    known = jnp.arange(devices * spheres, dtype=jnp.int32)
-    own = (mine[:, None] == known[None, :]).astype(jnp.float32)
-    acts = (contact_sphere[None, :] == mine[:, None]).astype(jnp.float32)
-    partner = (contact_partner[:, None] == known[None, :]).astype(jnp.float32)
-    linked = jnp.sum(acts[:, :, None] * partner[None], axis=1)
-    linked = own + DASHPOT * (linked - jnp.sum(acts, axis=1)[:, None] * own)
-    both = jnp.concatenate([linked, own], axis=0)
-    links = both.reshape(2 * spheres, devices, spheres).transpose(0, 2, 1)
-    links = links.reshape(2 * spheres * spheres, devices)
-    matrix = jnp.asarray(combine_matrix(column_count, row_count, per_sphere))
-    state, motion = tail(spread, tile, matrix, links, span_y)
-    motion = motion.reshape(2, spheres, spheres, TILE_LANES)
-    linear = sum(motion[0, :, s, 6 * s : 6 * s + 3] for s in range(spheres))
-    angular = sum(motion[1, :, s, 6 * s + 3 : 6 * s + 6] for s in range(spheres))
-    return state, jnp.concatenate([linear, angular], axis=1).T
+    bases = [base.reshape(1, markers) for base in (base_x, base_y, base_z)]
+    owners = owner_block.reshape(1, markers)
+    motion = sphere_motion.T
+    home, arrived, *halos = front(owners, bases, delta_weights, marker_offset, motion, velocity)
+    spread, edges, tile = markers_stage(spheres, velocity, halos, home, arrived, motion)
+    columns, rows = lax.axis_size("gx"), lax.axis_size("gy")
+    matrix = jnp.asarray(combine_matrix(columns, rows, markers // spheres))
+    state, moved = tail(
+        spread, edges, tile, matrix, contact_sphere, contact_partner, span_y, spheres
+    )
+    return state, moved.T
 
 
 def solution(mesh):

time: 110 us -> 92 us (0.84)
  Pallas kernels: 98.8 us -> 88 us
  local copies, waits for them, and re-layouts: 6.67 us -> 3.29 us
  other arithmetic: 3.24 us -> 0 us
    pallas_call x1, Pallas kernels: 53.3 us -> 47 us  [tail(): pl.pallas_call(functools.partial(tail_kernel, columns, rows), out_shape=[...]
    pallas_call x1, Pallas kernels: 22.9 us -> 18.7 us  [markers_stage(): pl.pallas_call(functools.partial(markers_kernel, spheres), out_shape=[jax...]
    convert_element_type x4 -> x0, other arithmetic: 1.61 us -> none  [the longest x1 1.4 us: on_device(): jnp.stack([owner_block[:, 0], base_x, base_y, base_z]).astype(jnp.float32)]
    unnamed x8 -> x4, local copies, waits for them, and re-layouts: 4.1 us -> 3.29 us
where the time goes in v2:
time: 92 us
  Pallas kernels  88 us (96%)
  local copies, waits for them, and re-layouts  3.29 us (4%)
    pallas_call x1, Pallas kernels, tail(): pl.pallas_call(functools.partial(tail_kernel, columns, rows), out_shape=[...  47 us
    pallas_call x1, Pallas kernels, front(): pl.pallas_call(functools.partial(front_kernel, columns, rows), out_shape=...  22.4 us
    pallas_call x1, Pallas kernels, markers_stage(): pl.pallas_call(functools.partial(markers_kernel, spheres), out_shape=[jax...  18.7 us
    unnamed x4, local copies, waits for them, and re-layouts  3.29 us

profile of v2, /device:TPU:1, one launch (start us, length us, event | category | flops | bytes accessed | tf_op | source)
XLA Modules:
  0.0 92.0 jit_solution(3460259169715443841)
XLA Ops:
  0.6 22.4 %front.1 = (f32[24,2048]{1,0:T(8,128)}, f32[8,24,256]{2,1,0:T(8,128)}, f32[3,2,32,256]{3,2,1,0:T(8,128)}, f32[3,2,32,256]{3,2,1,0:T(8,128)}, f32[3,16,8,256]{3,2...) custom-call(s32[1,2048]{1,0:T(1,128)} %bitcast.6, s32[1,2048]{1,0:T(1,128)} %bitcast.7, ...), custom_call_target="tpu_custom_call" | custom-call | tf_op jit(solution)/shard_map/front/pallas_call | solution.py:261
  23.0 18.7 %markers.1 = (f32[24,120,256]{2,1,0:T(8,128)}, f32[2,3,216,256]{3,2,1,0:T(8,128)}, f32[16,128]{1,0:T(8,128)}) custom-call(f32[3,16,32,256]{3,2,1,0:T(8,128)} %velocity.3, f32[3,2,32,256]{3,2,1,0:T(8,128)} %get-tuple-element.14.left, f32[3,2,32,256]{3,2,1,0:T(8,128)} %get-tuple-element.15.right, f32[3,16,8,256]{3,2,1,0:T(8,128)} %get-tuple-element.16.below, ...), custom_call_target="tpu_custom_call" | custom-call | tf_op jit(solution)/shard_map/markers/pallas_call | solution.py:499
  41.7 47.0 %tail.1 = (f32[3,16,32,256]{3,2,1,0:T(8,128)}, f32[2,6]{1,0:T(2,128)}) custom-call(f32[24,120,256]{2,1,0:T(8,128)} %get-tuple-element.21.spread, f32[2,3,216,256]{3,2,1,0:T(8,128)} %get-tuple-element.22.edges, f32[16,128]{1,0:T(8,128)} %get-tuple-element.23.tile, f32[32,512]{1,0:T(8,128)} %constant.2.clone.matrix, s32[4]{0:T(128)} %contact_sphere.1, ...), custom_call_target="tpu_custom_call" | custom-call | tf_op jit(solution)/shard_map/tail/pallas_call | solution.py:769
  88.7 0.0 copy-start
  88.7 2.7 %copy.15 = f32[3,16,32,256]{3,2,1,0:T(8,128)} copy(f32[3,16,32,256]{3,2,1,0:T(8,128)} %get-tuple-element.28) | data formatting | bytes 3145728
  91.4 0.0 copy-done
  91.4 0.6 copy.16
Async XLA Ops:
  88.7 2.7 %copy-start = (f32[2,6]{1,0:T(2,128)S(1)}, f32[2,6]{1,0:T(2,128)}, u32[]{:S(2)}) copy-start(f32[2,6]{1,0:T(2,128)} %get-tuple-element.25) | copy-start | bytes 148

commit v3 on v2

--- a/solution.py
+++ b/solution.py
@@ -1,4 +1,5 @@
 import functools
+import math
 
 import jax
 import jax.numpy as jnp
@@ -111,28 +112,45 @@
 
 
 def front_kernel(
-    columns, rows, owners, base_x, base_y, base_z, weights, offsets, motion, velocity,
-    home, arrived, left, right, below, above, corners, slots, send, recv,
+    columns, rows, *refs
+):
+    inputs, refs = refs[:8], refs[8:]
+    staged, load = refs[-9:-1], refs[-1]
+    loads = [
+        pltpu.make_async_copy(src, dst, load.at[n])
+        for n, (src, dst) in enumerate(zip(inputs, staged))
+    ]
+    for copy in loads:
+        copy.start()
+    front_body(columns, rows, loads, *staged, *refs[:-9])
+
+
+def front_body(
+    columns, rows, loads, owners, base_x, base_y, base_z, weights, offsets, motion, velocity,
+    placed, alive, high, low, spread,
+    home, slots, arrived, left, right, below, above, corners, parts, send, recv,
 ):
     column = lax.axis_index("gx")
     row = lax.axis_index("gy")
-    span_x, span_y = velocity.shape[1], velocity.shape[2]
+    span_x, span_y, extent_z = velocity.shape[1:]
+    wide_y = span_y + 2 * ITERS
+    lanes = len(DIRECTIONS)
+    f32, bf16 = jnp.float32, jnp.bfloat16
     barrier = greet(columns, rows, column, row)
 
     def peer(dx, dy):
         return (lax.rem(column + dx + columns, columns), row + dy)
 
-    edge = [
-        (velocity.at[:, 0:HALO], right, -1, 0),
-        (velocity.at[:, span_x - HALO : span_x], left, 1, 0),
-        (velocity.at[:, :, 0:RIM], above, 0, -1),
-        (velocity.at[:, :, span_y - RIM : span_y], below, 0, 1),
-    ]
+    edge = [(slots.at[g], arrived.at[g], dx, dy) for g, (dx, dy) in enumerate(DIRECTIONS)]
+    rims = (slice(0, RIM), slice(span_y - RIM, span_y))
+    for at in rims + (slice(RIM, span_y - RIM),):
+        edge.append((velocity.at[:, 0:HALO, at], right.at[:, :, at], -1, 0))
+        edge.append((velocity.at[:, span_x - HALO : span_x, at], left.at[:, :, at], 1, 0))
+    edge.append((velocity.at[:, :, rims[0]], above, 0, -1))
+    edge.append((velocity.at[:, :, rims[1]], below, 0, 1))
     for side, halo in enumerate((left, right)):
-        edge.append((halo.at[:, :, 0:RIM], corners.at[2 + side], 0, -1))
-        edge.append((halo.at[:, :, span_y - RIM : span_y], corners.at[side], 0, 1))
-    for g, (dx, dy) in enumerate(DIRECTIONS):
-        edge.append((slots.at[g], arrived.at[g], dx, dy))
+        edge.append((halo.at[:, :, rims[0]], corners.at[2 + side], 0, -1))
+        edge.append((halo.at[:, :, rims[1]], corners.at[side], 0, 1))
 
     def start(k):
         src, dst, dx, dy = edge[k]
@@ -157,36 +175,34 @@
 
     @pl.when(row == 0)
     def _():
-        below[...] = jnp.zeros(below.shape, jnp.float32)
+        below[...] = jnp.zeros(below.shape, f32)
         for n in (0, 1):
-            corners[n] = jnp.zeros(corners.shape[1:], jnp.float32)
+            corners[n] = jnp.zeros(corners.shape[1:], f32)
         for g, (dx, dy) in enumerate(DIRECTIONS):
             if dy > 0:
-                arrived[g] = jnp.zeros(arrived.shape[1:], jnp.float32)
+                arrived[g] = jnp.zeros(arrived.shape[1:], f32)
 
     @pl.when(row == rows - 1)
     def _():
-        above[...] = jnp.zeros(above.shape, jnp.float32)
+        above[...] = jnp.zeros(above.shape, f32)
         for n in (2, 3):
-            corners[n] = jnp.zeros(corners.shape[1:], jnp.float32)
+            corners[n] = jnp.zeros(corners.shape[1:], f32)
         for g, (dx, dy) in enumerate(DIRECTIONS):
             if dy < 0:
-                arrived[g] = jnp.zeros(arrived.shape[1:], jnp.float32)
-
-    pl.semaphore_wait(barrier, greeted(rows, row))
-    for k in range(4):
-        start(k)
-
+                arrived[g] = jnp.zeros(arrived.shape[1:], f32)
+
+    for copy in loads[:7]:
+        copy.wait()
     markers = owners.shape[1]
     spheres = motion.shape[0]
     per_sphere = markers // spheres
-    owner = owners[...].astype(jnp.float32)
+    owner = owners[...].astype(f32)
     owner_x = jnp.floor((owner + 0.5) * (1.0 / rows))
     owner_y = owner - owner_x * rows
-    step_x = owner_x - column.astype(jnp.float32)
+    step_x = owner_x - column.astype(f32)
     step_x = jnp.where(step_x > 1.5, step_x - columns, step_x)
     step_x = jnp.where(step_x < -1.5, step_x + columns, step_x)
-    step_y = owner_y - row.astype(jnp.float32)
+    step_y = owner_y - row.astype(f32)
     lane = (step_x + 1.0) * 3.0 + step_y + 1.0
     at_home = lane == 4.0
     lane = jnp.where(at_home, -1.0, jnp.where(lane > 4.0, lane - 1.0, lane))
@@ -207,100 +223,83 @@
         )
     home[0:12] = weights[...]
     for line, base in ((X_ROW, base_x), (Y_ROW, base_y), (Z_ROW, base_z)):
-        home[line : line + 1] = base[...].astype(jnp.float32)
+        home[line : line + 1] = base[...].astype(f32)
     home[TARGET : TARGET + 3] = jnp.concatenate(targets, axis=1)
     home[OFFSET : OFFSET + 3] = offset
     position = lax.broadcasted_iota(jnp.int32, (1, markers), 1)
-    sphere = jnp.zeros((1, markers), jnp.float32)
+    sphere = jnp.zeros((1, markers), f32)
     for s in range(1, spheres):
-        sphere = sphere + (position >= s * per_sphere).astype(jnp.float32)
+        sphere = sphere + (position >= s * per_sphere).astype(f32)
     home[SPHERE : SPHERE + 1] = sphere
-    home[LIVE : LIVE + 1] = jnp.ones((1, markers), jnp.float32)
-    home[LIVE + 1 : LIVE + 2] = jnp.zeros((1, markers), jnp.float32)
-
-    lanes = len(DIRECTIONS)
+    home[LIVE : LIVE + 1] = jnp.ones((1, markers), f32)
+    home[LIVE + 1 : LIVE + 2] = jnp.zeros((1, markers), f32)
+
     blocks = markers // CHUNK
     hot, upto, totals = ranks([lane[:, b * CHUNK : (b + 1) * CHUNK] for b in range(blocks)], lanes)
     rank = [jnp.sum(h * (u - 1.0), axis=0, keepdims=True) for h, u in zip(hot, upto)]
     where_to = jnp.concatenate(rank, axis=1) + lane * CHUNK
     where_to = jnp.where(at_home, -1.0, where_to)
-    parts = jnp.concatenate(split(home[...]), axis=0)
-    for g, piece in enumerate(place(parts, where_to, range(lanes))):
+    pair = jnp.concatenate(split(home[...]), axis=0)
+    for g, piece in enumerate(place(pair, where_to, range(lanes))):
         slots[g] = piece
-    home[LIVE : LIVE + 1] = at_home.astype(jnp.float32)
-
-    for k in range(8, 8 + lanes):
+    home[LIVE : LIVE + 1] = at_home.astype(f32)
+
+    loads[7].wait()
+    pl.semaphore_wait(barrier, greeted(rows, row))
+    for k in range(len(edge) - 4):
         start(k)
-    arrive(0)
-    arrive(1)
-    for k in range(4, 8):
-        start(k)
-    for k in range(2, 8 + lanes):
+
+    for k in range(lanes):
         arrive(k)
-    for k in range(8 + lanes):
-        sent(k)
-
-
-def front(owners, bases, weights, offsets, motion, velocity):
-    columns, rows = lax.axis_size("gx"), lax.axis_size("gy")
-    span_x, span_y, extent_z = velocity.shape[1:]
-    markers = owners.shape[1]
-    lanes = len(DIRECTIONS)
-    f32 = jnp.float32
-    copies = 8 + lanes
-    vmem = pl.BlockSpec(memory_space=pltpu.VMEM)
-    out = [
-        (RECORD, markers),
-        (lanes, RECORD, CHUNK),
-        (3, HALO, span_y, extent_z),
-        (3, HALO, span_y, extent_z),
-        (3, span_x, RIM, extent_z),
-        (3, span_x, RIM, extent_z),
-        (4, 3, HALO, RIM, extent_z),
-    ]
-    return pl.pallas_call(
-        functools.partial(front_kernel, columns, rows),
-        out_shape=[jax.ShapeDtypeStruct(shape, f32) for shape in out],
-        in_specs=[vmem] * 8,
-        out_specs=[vmem] * len(out),
-        scratch_shapes=[
-            pltpu.VMEM((lanes, RECORD, CHUNK), f32),
-            pltpu.SemaphoreType.DMA((copies,)),
-            pltpu.SemaphoreType.DMA((copies,)),
-        ],
-        compiler_params=pltpu.CompilerParams(collective_id=0, has_side_effects=True),
-        name="front",
-    )(owners, *bases, weights, offsets, motion, velocity)
-
-
-def four(distance, weights):
-    value = jnp.where(distance == 3.0, weights[3:4], 0.0)
-    for n in (2, 1, 0):
-        value = jnp.where(distance == float(n), weights[n : n + 1], value)
-    return value
-
-
-def markers_kernel(
-    spheres, velocity, left, right, below, above, corners, home, arrived, motion,
-    spread, edges, tile, high, low, sorted_refs, parts, sums,
-):
-    span_x, span_y, extent_z = velocity.shape[1:]
-    wide_y = span_y + 2 * ITERS
-    lanes = len(DIRECTIONS)
-    bf16, f32 = jnp.bfloat16, jnp.float32
-    layers = span_x + 2 * HALO
+    total = blocks + lanes
+    count = -(-(span_x + 1) // 8) * 8
+    categories = []
+    living = []
+    for b in range(total):
+        at = slice(b * CHUNK, (b + 1) * CHUNK)
+        if b < blocks:
+            record = home[:, at]
+            group = lanes + record[SPHERE : SPHERE + 1] * (lanes + 1)
+        else:
+            record = arrived[b - blocks]
+            group = (b - blocks) + record[SPHERE : SPHERE + 1] * (lanes + 1)
+        lives = record[LIVE : LIVE + 1] > 0.5
+        living.append(lives)
+        categories.append(jnp.where(lives, record[X_ROW : X_ROW + 1], -1.0))
+        first, rest = split(record)
+        parts[0:RECORD, at] = first
+        parts[RECORD : 2 * RECORD, at] = rest
+        parts[SPHERE : SPHERE + 1, at] = group
+    hot, upto, totals = ranks(categories, count)
+    lower_rows = lax.broadcasted_iota(jnp.int32, (count, count), 0)
+    lower_lanes = lax.broadcasted_iota(jnp.int32, (count, count), 1)
+    before = (lower_lanes < lower_rows).astype(f32)
+    wide = jnp.broadcast_to(totals, (count, TILE_LANES))
+    starts = jnp.dot(
+        before, wide, precision=lax.Precision.HIGHEST, preferred_element_type=f32
+    )[:, 0:1]
+    places = []
+    for b in range(total):
+        rank = jnp.sum(hot[b] * (upto[b] + (starts - 1.0)), axis=0, keepdims=True)
+        places.append(jnp.where(living[b], rank, -1.0))
+    where_to = jnp.concatenate(places, axis=1)
+    alive[...] = jnp.broadcast_to(jnp.sum(wide, axis=0, keepdims=True), alive.shape)
+    for first in range(0, total, GROUP):
+        groups = range(first, min(first + GROUP, total))
+        for g, piece in zip(groups, place(parts[...], where_to, groups)):
+            placed[g] = piece
 
     def layer(x, row_source, below_source, above_source, own):
         for c in range(3):
-            rows = row_source(c)
-            edge = jnp.zeros((HALO, extent_z), f32)
+            lines = row_source(c)
+            margin = jnp.zeros((HALO, extent_z), f32)
             value = jnp.concatenate(
                 [
-                    edge,
+                    margin,
                     below_source(c)[RIM - HALO : RIM],
-                    rows,
+                    lines,
                     above_source(c)[0:HALO],
-                    edge,
+                    margin,
                 ],
                 axis=0,
             )
@@ -309,11 +308,14 @@
             high[x, at] = first.astype(bf16)
             low[x, at] = rest.astype(bf16)
             if own:
-                wide = jnp.zeros((ITERS, extent_z), f32)
-                spread[x + HALO, at] = jnp.concatenate([wide, rows, wide], axis=0)
+                margin = jnp.zeros((ITERS, extent_z), f32)
+                spread[x + HALO, at] = jnp.concatenate([margin, lines, margin], axis=0)
         end = jnp.zeros((high.shape[1] - 3 * wide_y, extent_z), bf16)
         high[x, 3 * wide_y :] = end
         low[x, 3 * wide_y :] = end
+
+    arrive(len(edge) - 6)
+    arrive(len(edge) - 5)
 
     def inner(x, carry):
         layer(
@@ -325,7 +327,18 @@
         )
         return carry
 
+    for k in range(lanes, lanes + 4):
+        arrive(k)
+    for k in range(len(edge) - 4, len(edge)):
+        start(k)
     lax.fori_loop(0, span_x, inner, 0)
+    for x in range(ITERS):
+        spread[x] = jnp.zeros(spread.shape[1:], f32)
+        spread[span_x + ITERS + x] = jnp.zeros(spread.shape[1:], f32)
+    arrive(lanes + 4)
+    arrive(lanes + 5)
+    for k in range(len(edge) - 4, len(edge)):
+        arrive(k)
     for side, halo in enumerate((left, right)):
         for x in range(HALO):
             layer(
@@ -335,54 +348,73 @@
                 lambda c: corners[2 + side, c, x],
                 False,
             )
-    for x in range(ITERS):
-        spread[x] = jnp.zeros(spread.shape[1:], f32)
-        spread[span_x + ITERS + x] = jnp.zeros(spread.shape[1:], f32)
-
-    markers = home.shape[1]
-    blocks = markers // CHUNK
-    total = blocks + lanes
-    count = -(-(span_x + 1) // 8) * 8
-    categories = []
-    live = []
-    for b in range(total):
-        at = slice(b * CHUNK, (b + 1) * CHUNK)
-        if b < blocks:
-            record = home[:, at]
-            group = lanes + record[SPHERE : SPHERE + 1] * (lanes + 1)
-        else:
-            record = arrived[b - blocks]
-            group = (b - blocks) + record[SPHERE : SPHERE + 1] * (lanes + 1)
-        alive = record[LIVE : LIVE + 1] > 0.5
-        live.append(alive)
-        categories.append(jnp.where(alive, record[X_ROW : X_ROW + 1], -1.0))
-        first, rest = split(record)
-        parts[0:RECORD, at] = first
-        parts[RECORD : 2 * RECORD, at] = rest
-        parts[SPHERE : SPHERE + 1, at] = group
-    hot, upto, totals = ranks(categories, count)
-    lower_rows = lax.broadcasted_iota(jnp.int32, (count, count), 0)
-    lower_lanes = lax.broadcasted_iota(jnp.int32, (count, count), 1)
-    before = (lower_lanes < lower_rows).astype(f32)
-    starts = jnp.dot(
-        before,
-        jnp.broadcast_to(totals, (count, TILE_LANES)),
-        precision=lax.Precision.HIGHEST,
-        preferred_element_type=f32,
-    )[:, 0:1]
-    places = []
-    for b in range(total):
-        rank = jnp.sum(hot[b] * (upto[b] + (starts - 1.0)), axis=0, keepdims=True)
-        places.append(jnp.where(live[b], rank, -1.0))
-    where_to = jnp.concatenate(places, axis=1)
-    alive_count = jnp.sum(totals).astype(jnp.int32)
-    for first in range(0, total, GROUP):
-        groups = range(first, min(first + GROUP, total))
-
-        @pl.when(alive_count > first * CHUNK)
-        def _(groups=groups):
-            for g, piece in zip(groups, place(parts[...], where_to, groups)):
-                sorted_refs[g] = piece
+    for k in range(len(edge)):
+        sent(k)
+
+
+def front(owners, bases, weights, offsets, motion, velocity):
+    columns, rows = lax.axis_size("gx"), lax.axis_size("gy")
+    span_x, span_y, extent_z = velocity.shape[1:]
+    wide_y = span_y + 2 * ITERS
+    markers = owners.shape[1]
+    lanes = len(DIRECTIONS)
+    f32, bf16 = jnp.float32, jnp.bfloat16
+    copies = lanes + 12
+    inputs = (owners, *bases, weights, offsets, motion, velocity)
+    total = markers // CHUNK + lanes
+    field = (span_x + 2 * HALO, -(-3 * wide_y // 16) * 16, extent_z)
+    vmem = pl.BlockSpec(memory_space=pltpu.VMEM)
+    out = [
+        pltpu.VMEM((total, RECORD, CHUNK), f32),
+        pltpu.VMEM((8, TILE_LANES), f32),
+        pltpu.VMEM(field, bf16),
+        pltpu.VMEM(field, bf16),
+        pltpu.VMEM((span_x + 2 * ITERS, 3 * wide_y, extent_z), f32),
+    ]
+    room = 67_043_328 - sum(math.prod(ref.shape) * ref.dtype.itemsize for ref in out) - 2**15
+    return pl.pallas_call(
+        functools.partial(front_kernel, columns, rows),
+        out_shape=out,
+        in_specs=[pl.BlockSpec(memory_space=pltpu.HBM)] * 8,
+        out_specs=[vmem] * len(out),
+        scratch_shapes=[
+            pltpu.VMEM((RECORD, markers), f32),
+            pltpu.VMEM((lanes, RECORD, CHUNK), f32),
+            pltpu.VMEM((lanes, RECORD, CHUNK), f32),
+            pltpu.VMEM((3, HALO, span_y, extent_z), f32),
+            pltpu.VMEM((3, HALO, span_y, extent_z), f32),
+            pltpu.VMEM((3, span_x, RIM, extent_z), f32),
+            pltpu.VMEM((3, span_x, RIM, extent_z), f32),
+            pltpu.VMEM((4, 3, HALO, RIM, extent_z), f32),
+            pltpu.VMEM((2 * RECORD, total * CHUNK), f32),
+            pltpu.SemaphoreType.DMA((copies,)),
+            pltpu.SemaphoreType.DMA((copies,)),
+        ]
+        + [pltpu.VMEM(array.shape, array.dtype) for array in inputs]
+        + [pltpu.SemaphoreType.DMA((len(inputs),))],
+        compiler_params=pltpu.CompilerParams(
+            collective_id=0, has_side_effects=True, vmem_limit_bytes=room
+        ),
+        name="front",
+    )(*inputs)
+
+
+def four(distance, weights):
+    value = jnp.where(distance == 3.0, weights[3:4], 0.0)
+    for n in (2, 1, 0):
+        value = jnp.where(distance == float(n), weights[n : n + 1], value)
+    return value
+
+
+def markers_kernel(
+    spheres, span_y, sorted_refs, alive_ref, high, low, frame, motion, spread, edges, tile, sums
+):
+    layers, _, extent_z = high.shape
+    span_x = layers - 2 * HALO
+    wide_y = span_y + 2 * ITERS
+    lanes = len(DIRECTIONS)
+    bf16, f32 = jnp.bfloat16, jnp.float32
+    alive_count = jnp.max(alive_ref[0:1, :]).astype(jnp.int32)
 
     sums[...] = jnp.zeros(sums.shape, f32)
     z_cells = lax.broadcasted_iota(jnp.int32, (extent_z, CHUNK), 0).astype(f32)
@@ -486,35 +518,26 @@
                 ]
 
 
-def markers_stage(spheres, velocity, halos, home, arrived, motion):
-    span_x, span_y, extent_z = velocity.shape[1:]
-    wide_y = span_y + 2 * ITERS
+def markers_stage(spheres, span_y, placed, alive, high, low, frame, motion):
+    wide_x, lines, extent_z = frame.shape
     lanes = len(DIRECTIONS)
     f32 = jnp.float32
-    total = home.shape[1] // CHUNK + lanes
     groups = (lanes + 1) * spheres
-    field_rows = -(-3 * wide_y // 16) * 16
-    field = (span_x + 2 * HALO, field_rows, extent_z)
     vmem = pl.BlockSpec(memory_space=pltpu.VMEM)
     return pl.pallas_call(
-        functools.partial(markers_kernel, spheres),
+        functools.partial(markers_kernel, spheres, span_y),
         out_shape=[
-            jax.ShapeDtypeStruct((span_x + 2 * ITERS, 3 * wide_y, extent_z), f32),
-            jax.ShapeDtypeStruct((2, 3, (ITERS + HALO) * (span_y + 2 * HALO), extent_z), f32),
+            pltpu.VMEM(frame.shape, f32),
+            pltpu.VMEM((2, 3, (ITERS + HALO) * (span_y + 2 * HALO), extent_z), f32),
             jax.ShapeDtypeStruct((TILE_ROWS, TILE_LANES), f32),
         ],
-        in_specs=[vmem] * 9,
+        in_specs=[vmem] * 6,
         out_specs=[vmem] * 3,
-        scratch_shapes=[
-            pltpu.VMEM(field, jnp.bfloat16),
-            pltpu.VMEM(field, jnp.bfloat16),
-            pltpu.VMEM((total, RECORD, CHUNK), f32),
-            pltpu.VMEM((2 * RECORD, total * CHUNK), f32),
-            pltpu.VMEM((groups, 8, CHUNK), f32),
-        ],
-        compiler_params=pltpu.CompilerParams(vmem_limit_bytes=56 * 2**20),
+        scratch_shapes=[pltpu.VMEM((groups, 8, CHUNK), f32)],
+        input_output_aliases={4: 0},
+        compiler_params=pltpu.CompilerParams(vmem_limit_bytes=40 * 2**20),
         name="markers",
-    )(velocity, *halos, home, arrived, motion)
+    )(placed, alive, high, low, frame, motion)
 
 
 def combine_matrix(columns, rows, per_sphere):
@@ -769,7 +792,7 @@
     return pl.pallas_call(
         functools.partial(tail_kernel, columns, rows),
         out_shape=[
-            jax.ShapeDtypeStruct((3, span_x, span_y, extent_z), f32),
+            pltpu.VMEM((3, span_x, span_y, extent_z), f32),
             jax.ShapeDtypeStruct((spheres, 6), f32),
         ],
         in_specs=[vmem] * 4 + [smem] * 2,
@@ -795,7 +818,7 @@
             dma((columns - 1,)),
         ],
         compiler_params=pltpu.CompilerParams(
-            collective_id=1, has_side_effects=True, vmem_limit_bytes=56 * 2**20
+            collective_id=1, has_side_effects=True, vmem_limit_bytes=40 * 2**20
         ),
         name="tail",
     )(spread, edges, tile, matrix, contact_sphere, contact_partner)
@@ -819,8 +842,8 @@
     bases = [base.reshape(1, markers) for base in (base_x, base_y, base_z)]
     owners = owner_block.reshape(1, markers)
     motion = sphere_motion.T
-    home, arrived, *halos = front(owners, bases, delta_weights, marker_offset, motion, velocity)
-    spread, edges, tile = markers_stage(spheres, velocity, halos, home, arrived, motion)
+    staged = front(owners, bases, delta_weights, marker_offset, motion, velocity)
+    spread, edges, tile = markers_stage(spheres, span_y, *staged, motion)
     columns, rows = lax.axis_size("gx"), lax.axis_size("gy")
     matrix = jnp.asarray(combine_matrix(columns, rows, markers // spheres))
     state, moved = tail(

time: 92 us -> 78.2 us (0.85)
  Pallas kernels: 88 us -> 75.6 us
  local copies, waits for them, and re-layouts: 3.29 us -> 1.73 us
    pallas_call x1, Pallas kernels: 18.7 us -> 12.1 us  [markers_stage(): pl.pallas_call(functools.partial(markers_kernel, spheres, span_y), out_sh...]
    pallas_call x1, Pallas kernels: 47 us -> 43.6 us  [tail(): pl.pallas_call(functools.partial(tail_kernel, columns, rows), out_shape=[...]
    pallas_call x1, Pallas kernels: 22.4 us -> 19.9 us  [front(): pl.pallas_call(functools.partial(front_kernel, columns, rows), out_shape=...]
    unnamed x4 -> x10, local copies, waits for them, and re-layouts: 3.29 us -> 1.73 us
where the time goes in v3:
time: 78.2 us; the launch traced here: 78.1 us
  Pallas kernels  75.6 us (97%)
  local copies, waits for them, and re-layouts  1.73 us (2%)
    pallas_call x1, Pallas kernels, tail(): pl.pallas_call(functools.partial(tail_kernel, columns, rows), out_shape=[...  43.6 us
    pallas_call x1, Pallas kernels, front(): pl.pallas_call(functools.partial(front_kernel, columns, rows), out_shape=...  19.9 us
    pallas_call x1, Pallas kernels, markers_stage(): pl.pallas_call(functools.partial(markers_kernel, spheres, span_y), out_sh...  12.1 us
    unnamed x10, local copies, waits for them, and re-layouts  1.73 us

profile of v3, /device:TPU:1, one launch (start us, length us, event | category | flops | bytes accessed | tf_op | source)
XLA Modules:
  0.0 78.1 jit_solution(4092573115739365004)
XLA Ops:
  0.6 0.0 copy-start.1
  0.6 19.9 %front.1 = (f32[16,24,256]{2,1,0:T(8,128)S(1)}, f32[8,128]{1,0:T(8,128)S(1)}, bf16[20,128,256]{2,1,0:T(8,128)(2,1)S(1)}, bf16[20,128,256]{2,1,0:T(8,128)(2,1)S(1)}, f32[24,120,256]{2,1,0:T(8,128)S(1)}) custom-call(s32[1,2048]{1,0:T(1,128)} %bitcast.9, s32[1,2048]{1,0:T(1,128)} %bitcast.10, s32[1,2048]{1,0:T(1,128)} %bitcast.11, s32[1,2048]{1,0:T(1,128)} %bitcast.12, ...), custom_call_target="tpu_custom_call" | custom-call | tf_op jit(solution)/shard_map/front/pallas_call | solution.py:375
  20.6 0.0 copy-done.1
  20.6 0.0 copy-start
  20.6 0.0 copy-start.2
  20.6 0.0 copy-start.3
  20.6 12.1 %markers.1 = (f32[24,120,256]{2,1,0:T(8,128)S(1)}, f32[2,3,216,256]{3,2,1,0:T(8,128)S(1)}, f32[16,128]{1,0:T(8,128)S(1)}) custom-call(f32[16,24,256]{2,1,0:T(8,128)S(1)} %get-tuple-element.12.sorted_refs, f32[8,128]{1,0:T(8,128)S(1)} %get-tuple-element.13.alive_ref, ...), custom_call_target="tpu_custom_call", output_to_operand_aliasing={{0}: (4, {})} | custom-call | tf_op jit(solution)/shard_map/markers/pallas_call | solution.py:527
  32.7 0.0 copy-done
  32.7 0.0 copy-done.2
  32.8 0.0 copy-done.3
  32.8 43.6 %tail.1 = (f32[3,16,32,256]{3,2,1,0:T(8,128)S(1)}, f32[2,6]{1,0:T(2,128)S(1)}) custom-call(f32[24,120,256]{2,1,0:T(8,128)S(1)} %get-tuple-element.17.spread, f32[2,3,216,256]{3,2,1,0:T(8,128)S(1)} %get-tuple-element.18.edges, f32[16,128]{1,0:T(8,128)S(1)} %get-tuple-element.19.tile, f32[32,512]{1,0:T(8,128)S(1)} %copy-done, s32[4]{0:T(128)S(1)} %copy-done.2, ...), custom_call_target="tpu_custom_call" | custom-call | tf_op jit(solution)/shard_map/tail/pallas_call | solution.py:792
  76.4 1.1 %copy.17 = f32[3,16,32,256]{3,2,1,0:T(8,128)} copy(f32[3,16,32,256]{3,2,1,0:T(8,128)S(1)} %get-tuple-element.22) | data formatting | bytes 3145728
  77.5 0.6 copy.18
Async XLA Ops:
  0.6 20.0 %copy-start.1 = (f32[6,2]{0,1:T(2,128)S(1)}, f32[6,2]{0,1:T(2,128)}, u32[]{:S(2)}) copy-start(f32[6,2]{0,1:T(2,128)} %param.18) | copy-start | bytes 148
  20.6 12.1 %copy-start = (f32[32,512]{1,0:T(8,128)S(1)}, f32[32,512]{1,0:T(8,128)}, u32[]{:S(2)}) copy-start(f32[32,512]{1,0:T(8,128)} %constant.2.clone.matrix) | copy-start | bytes 196612
  20.6 12.1 %copy-start.2 = (s32[4]{0:T(128)S(1)}, s32[4]{0:T(128)}, u32[]{:S(2)}) copy-start(s32[4]{0:T(128)} %contact_sphere.1) | copy-start | bytes 52
  20.6 12.1 %copy-start.3 = (s32[4]{0:T(128)S(1)}, s32[4]{0:T(128)}, u32[]{:S(2)}) copy-start(s32[4]{0:T(128)} %contact_partner.1) | copy-start | bytes 52

commit v4 on v3

--- a/solution.py
+++ b/solution.py
@@ -15,7 +15,6 @@
 DASHPOT = 0.1
 
 MESH = pl.DeviceIdType.MESH
-TILE_ROWS = 16
 TILE_LANES = 128
 CHUNK = 256
 WINDOW = 8
@@ -505,17 +504,28 @@
     columns = jnp.sum(sums[...], axis=2)
     tile[...] = jnp.zeros(tile.shape, f32)
     for s in range(spheres):
-        at = slice(6 * s, 6 * (s + 1))
-        tile[0 : lanes + 1, at] = columns[(lanes + 1) * s : (lanes + 1) * (s + 1), 0:6]
-        tile[lanes + 1 : lanes + 2, at] = motion[s : s + 1]
+        for slot in range(lanes + 1):
+            at = 6 * (slot * spheres + s)
+            line = (lanes + 1) * s + slot
+            tile[0:1, at : at + 6] = columns[line : line + 1, 0:6]
+        at = 6 * ((lanes + 1) * spheres + s)
+        tile[0:1, at : at + 6] = motion[s : s + 1]
     reach = ITERS + HALO
-    depth = span_y + 2 * HALO
+    middle = span_y + 2 * HALO - 2 * reach
     for side, first in enumerate((span_x, HALO)):
         for c in range(3):
             for x in range(reach):
-                edges[side, c, depth * x : depth * (x + 1)] = spread[
-                    first + x, wide_y * c + HALO : wide_y * (c + 1) - HALO
-                ]
+                low_rim = wide_y * c + HALO
+                high_rim = wide_y * (c + 1) - HALO - reach
+                done = 0
+                for start, length in (
+                    (low_rim, reach),
+                    (high_rim, reach),
+                    (low_rim + reach, middle),
+                ):
+                    to = done + length * x
+                    edges[side, c, to : to + length] = spread[first + x, start : start + length]
+                    done += length * reach
 
 
 def markers_stage(spheres, span_y, placed, alive, high, low, frame, motion):
@@ -529,7 +539,7 @@
         out_shape=[
             pltpu.VMEM(frame.shape, f32),
             pltpu.VMEM((2, 3, (ITERS + HALO) * (span_y + 2 * HALO), extent_z), f32),
-            jax.ShapeDtypeStruct((TILE_ROWS, TILE_LANES), f32),
+            jax.ShapeDtypeStruct((1, TILE_LANES), f32),
         ],
         in_specs=[vmem] * 6,
         out_specs=[vmem] * 3,
@@ -541,20 +551,21 @@
 
 
 def combine_matrix(columns, rows, per_sphere):
-    matrix = np.zeros((columns, rows, columns, rows, TILE_ROWS), np.float32)
+    slots = len(DIRECTIONS) + 2
+    matrix = np.zeros((slots, columns, rows, columns, rows), np.float32)
     for i in range(columns):
         for j in range(rows):
             for slot, (dx, dy) in enumerate(DIRECTIONS):
                 if 0 <= j - dy < rows:
-                    matrix[(i - dx) % columns, j - dy, i, j, slot] -= RESPONSE / per_sphere
-            matrix[i, j, i, j, len(DIRECTIONS)] -= RESPONSE / per_sphere
-            matrix[i, j, i, j, len(DIRECTIONS) + 1] = 1.0
-    return matrix.reshape(columns * rows, -1)
+                    matrix[slot, (i - dx) % columns, j - dy, i, j] -= RESPONSE / per_sphere
+            matrix[slots - 2, i, j, i, j] -= RESPONSE / per_sphere
+            matrix[slots - 1, i, j, i, j] = 1.0
+    return matrix.reshape(slots * columns * rows, -1)
 
 
 def tail_kernel(
     columns, rows, spread, edges, tile, matrix, contact_sphere, contact_partner,
-    out, motion_out, from_left, from_right, from_below, from_above, given, corners, held,
+    out, motion_out, from_left, from_right, from_below, from_above, corners, held,
     rhs, one, two, mask_ref, own_sem, send, recv, row_send, row_recv, col_send, col_recv,
 ):
     column = lax.axis_index("gx")
@@ -577,19 +588,24 @@
         return (lax.rem(column + dx + columns, columns), row + dy)
 
     edge = []
+    rim = 2 * reach * reach
+    part = corners.shape[2]
     for c in range(3):
         low, high = wide_y * c, wide_y * (c + 1)
         inner = slice(HALO, wide_x - HALO)
         edge += [
-            (edges.at[0, c], from_left.at[c], 1, 0),
-            (edges.at[1, c], from_right.at[c], -1, 0),
+            (edges.at[0, c, 0:rim], from_left.at[c, 0:rim], 1, 0),
+            (edges.at[1, c, 0:rim], from_right.at[c, 0:rim], -1, 0),
+            (edges.at[0, c, rim:], from_left.at[c, rim:], 1, 0),
+            (edges.at[1, c, rim:], from_right.at[c, rim:], -1, 0),
             (spread.at[inner, high - RIM : high], from_below.at[c], 0, 1),
             (spread.at[inner, low : low + RIM], from_above.at[c], 0, -1),
-            (given.at[c, 0], corners.at[c, 0], 0, 1),
-            (given.at[c, 1], corners.at[c, 1], 0, 1),
-            (given.at[c, 2], corners.at[c, 2], 0, -1),
-            (given.at[c, 3], corners.at[c, 3], 0, -1),
+            (from_left.at[c, rim - part : rim], corners.at[c, 0], 0, 1),
+            (from_right.at[c, rim - part : rim], corners.at[c, 1], 0, 1),
+            (from_left.at[c, 0:part], corners.at[c, 2], 0, -1),
+            (from_right.at[c, 0:part], corners.at[c, 3], 0, -1),
         ]
+    each = 10
 
     def start(k):
         src, dst, dx, dy = edge[k]
@@ -638,11 +654,11 @@
     ]
     for copy in first:
         copy.start()
-    for k in range(4):
+    for k in range(6):
         start(k)
     for c in range(1, 3):
-        for k in range(2, 4):
-            start(8 * c + k)
+        for k in range(4, 6):
+            start(each * c + k)
 
     cells = lax.broadcasted_iota(jnp.int32, (wide_y, extent_z), 0) + (row * span_y - ITERS)
     inside = jnp.logical_and(cells >= 0, cells < span_y * rows)
@@ -667,8 +683,8 @@
     for copy in second:
         copy.start()
     for c in range(1, 3):
-        for k in range(2):
-            start(8 * c + k)
+        for k in range(4):
+            start(each * c + k)
 
     def relaxed(c, source, x):
         here = source[c, x]
@@ -704,75 +720,84 @@
         return carry
 
     for c in range(3):
-        arrive(8 * c + 2)
-        arrive(8 * c + 3)
+        arrive(each * c + 4)
+        arrive(each * c + 5)
     lax.fori_loop(0, 3, base, 0)
+
+    middle = depth - 2 * reach
+    upper = wide_y - HALO - reach
 
     def outer(c):
         for x in range(reach):
-            for side, y in enumerate((x, x + span_x + HALO)):
-                at = slice(6 * x, 6 * (x + 1))
-                rhs[c, y, 0:6] = rhs[c, y, 0:6] + corners[c, side, at]
-                rhs[c, y, wide_y - 6 :] = rhs[c, y, wide_y - 6 :] + corners[c, 2 + side, at]
+            for side, (halo, y) in enumerate(((from_left, x), (from_right, x + span_x + HALO))):
+                low = slice(reach * x, reach * (x + 1))
+                high = slice(reach * (reach + x), reach * (reach + x + 1))
+                late = slice(part - rim // 2 + reach * x, part - rim // 2 + reach * (x + 1))
+                inside = slice(rim + middle * x, rim + middle * (x + 1))
+                rhs[c, y, HALO : HALO + reach] = rhs[c, y, HALO : HALO + reach] + halo[c, low]
+                rhs[c, y, upper : upper + reach] = rhs[c, y, upper : upper + reach] + halo[c, high]
+                rhs[c, y, HALO + reach : upper] = rhs[c, y, HALO + reach : upper] + halo[c, inside]
+                rhs[c, y, 0:reach] = rhs[c, y, 0:reach] + corners[c, side, late]
+                rhs[c, y, wide_y - reach :] = rhs[c, y, wide_y - reach :] + corners[c, 2 + side, low]
                 rhs[c, y] = rhs[c, y] * mask_ref[0]
         sweeps(c, ((1, 1), (span_x + 1, -1)), lambda sweep: reach)
 
+    def settle():
+        for copy in second:
+            copy.wait()
+        gathered = held[...].reshape(-1, TILE_LANES)
+        devices = columns * rows
+        pieces = jnp.dot(
+            matrix[...],
+            gathered,
+            precision=lax.Precision.HIGHEST,
+            preferred_element_type=jnp.float32,
+        )
+        spheres = motion_out.shape[0]
+        moved = 0.0
+        for slot in range(len(DIRECTIONS) + 2):
+            at = 6 * spheres * slot
+            moved = moved + pieces[devices * slot : devices * (slot + 1), at : at + 6 * spheres]
+        device = lax.broadcasted_iota(jnp.int32, (1, devices), 1)
+        here = column * rows + row
+        linked, owned = [], []
+        for s in range(spheres):
+            mine = here * spheres + s
+            for other in range(spheres):
+                own_row = (device * spheres + other == mine).astype(jnp.float32)
+                line = own_row
+                for k in range(contact_sphere.shape[0]):
+                    acts = contact_sphere[k] == mine
+                    partner = (device * spheres + other == contact_partner[k]).astype(jnp.float32)
+                    line = line + jnp.where(acts, DASHPOT * (partner - own_row), 0.0)
+                linked.append(line)
+                owned.append(own_row)
+        links = jnp.concatenate(linked + owned, axis=0)
+        result = jnp.dot(
+            links, moved, precision=lax.Precision.HIGHEST, preferred_element_type=jnp.float32
+        )
+        for s in range(spheres):
+            for half in range(2):
+                total = 0.0
+                for other in range(spheres):
+                    line = (half * spheres + s) * spheres + other
+                    at = 6 * other + 3 * half
+                    total = total + result[line : line + 1, at : at + 3]
+                motion_out[s : s + 1, 3 * half : 3 * half + 3] = total
+
     for c in range(3):
-        arrive(8 * c)
-        arrive(8 * c + 1)
-        for side, halo in enumerate((from_left, from_right)):
-            for up, first in ((0, depth - reach), (2, 0)):
-                pieces = [
-                    halo[c, depth * x + first : depth * x + first + reach] for x in range(reach)
-                ]
-                given[c, up + side, 0 : reach * reach] = jnp.concatenate(pieces, axis=0)
-        for x in range(reach):
-            for halo, y in ((from_left, x), (from_right, x + span_x + HALO)):
-                rhs[c, y, HALO : wide_y - HALO] = (
-                    rhs[c, y, HALO : wide_y - HALO] + halo[c, depth * x : depth * (x + 1)]
-                )
-        for k in range(4, 8):
-            start(8 * c + k)
-        for k in range(4, 8):
-            arrive(8 * c + k)
+        arrive(each * c)
+        arrive(each * c + 1)
+        for k in range(6, each):
+            start(each * c + k)
+        if c == 2:
+            settle()
+        for k in range(2, 4):
+            arrive(each * c + k)
+        for k in range(6, each):
+            arrive(each * c + k)
         outer(c)
 
-    for copy in second:
-        copy.wait()
-    gathered = held[...].reshape(-1, TILE_LANES)
-    moved = jnp.dot(
-        matrix[...],
-        gathered,
-        precision=lax.Precision.HIGHEST,
-        preferred_element_type=jnp.float32,
-    )
-    spheres = motion_out.shape[0]
-    device = lax.broadcasted_iota(jnp.int32, (1, columns * rows), 1)
-    here = column * rows + row
-    linked, owned = [], []
-    for s in range(spheres):
-        mine = here * spheres + s
-        for other in range(spheres):
-            own_row = (device * spheres + other == mine).astype(jnp.float32)
-            line = own_row
-            for k in range(contact_sphere.shape[0]):
-                acts = contact_sphere[k] == mine
-                partner = (device * spheres + other == contact_partner[k]).astype(jnp.float32)
-                line = line + jnp.where(acts, DASHPOT * (partner - own_row), 0.0)
-            linked.append(line)
-            owned.append(own_row)
-    links = jnp.concatenate(linked + owned, axis=0)
-    result = jnp.dot(
-        links, moved, precision=lax.Precision.HIGHEST, preferred_element_type=jnp.float32
-    )
-    for s in range(spheres):
-        for part in range(2):
-            total = 0.0
-            for other in range(spheres):
-                line = (part * spheres + s) * spheres + other
-                at = 6 * other + 3 * part
-                total = total + result[line : line + 1, at : at + 3]
-            motion_out[s : s + 1, 3 * part : 3 * part + 3] = total
     for k in range(len(edge)):
         sent(k)
 
@@ -803,15 +828,14 @@
             pltpu.VMEM((3, wide_x - 2 * HALO, RIM, extent_z), f32),
             pltpu.VMEM((3, wide_x - 2 * HALO, RIM, extent_z), f32),
             pltpu.VMEM(corner, f32),
-            pltpu.VMEM(corner, f32),
             pltpu.VMEM((columns, rows) + tile.shape, f32),
             pltpu.VMEM(frame, f32),
             pltpu.VMEM(frame, f32),
             pltpu.VMEM(frame, f32),
             pltpu.VMEM((2, wide_y, extent_z), f32),
             dma,
-            dma((24,)),
-            dma((24,)),
+            dma((30,)),
+            dma((30,)),
             dma((rows - 1,)),
             dma((rows - 1,)),
             dma((columns - 1,)),

time: 78.2 us -> 72.6 us (0.928)
  Pallas kernels: 75.6 us -> 70.2 us
    pallas_call x1, Pallas kernels: 12.1 us -> 9.15 us  [markers_stage(): pl.pallas_call(functools.partial(markers_kernel, spheres, span_y), out_sh...]
    pallas_call x1, Pallas kernels: 43.6 us -> 41.1 us  [tail(): pl.pallas_call(functools.partial(tail_kernel, columns, rows), out_shape=[...]
where the time goes in v4:
time: 72.6 us
  Pallas kernels  70.2 us (97%)
  local copies, waits for them, and re-layouts  1.73 us (2%)
    pallas_call x1, Pallas kernels, tail(): pl.pallas_call(functools.partial(tail_kernel, columns, rows), out_shape=[...  41.1 us
    pallas_call x1, Pallas kernels, front(): pl.pallas_call(functools.partial(front_kernel, columns, rows), out_shape=...  19.9 us
    pallas_call x1, Pallas kernels, markers_stage(): pl.pallas_call(functools.partial(markers_kernel, spheres, span_y), out_sh...  9.15 us
    unnamed x10, local copies, waits for them, and re-layouts  1.73 us

profile of v4, /device:TPU:1, one launch (start us, length us, event | category | flops | bytes accessed | tf_op | source)
XLA Modules:
  0.0 72.6 jit_solution(14330040848640720350)
XLA Ops:
  0.6 0.0 copy-start.1
  0.6 19.9 %front.1 = (f32[16,24,256]{2,1,0:T(8,128)S(1)}, f32[8,128]{1,0:T(8,128)S(1)}, bf16[20,128,256]{2,1,0:T(8,128)(2,1)S(1)}, bf16[20,128,256]{2,1,0:T(8,128)(2,1)S(1)}, f32[24,120,256]{2,1,0:T(8,128)S(1)}) custom-call(s32[1,2048]{1,0:T(1,128)} %bitcast.9, s32[1,2048]{1,0:T(1,128)} %bitcast.10, s32[1,2048]{1,0:T(1,128)} %bitcast.11, s32[1,2048]{1,0:T(1,128)} %bitcast.12, ...), custom_call_target="tpu_custom_call" | custom-call | tf_op jit(solution)/shard_map/front/pallas_call | solution.py:374
  20.6 0.0 copy-done.1
  20.6 0.0 copy-start
  20.6 0.0 copy-start.2
  20.6 0.0 copy-start.3
  20.6 9.2 %markers.1 = (f32[24,120,256]{2,1,0:T(8,128)S(1)}, f32[2,3,216,256]{3,2,1,0:T(8,128)S(1)}, f32[1,128]{1,0:T(1,128)S(1)}) custom-call(f32[16,24,256]{2,1,0:T(8,128)S(1)} %get-tuple-element.12.sorted_refs, f32[8,128]{1,0:T(8,128)S(1)} %get-tuple-element.13.alive_ref, ...), custom_call_target="tpu_custom_call", output_to_operand_aliasing={{0}: (4, {})} | custom-call | tf_op jit(solution)/shard_map/markers/pallas_call | solution.py:537
  29.8 0.0 copy-done
  29.8 0.0 copy-done.2
  29.8 0.0 copy-done.3
  29.8 41.1 %tail.1 = (f32[3,16,32,256]{3,2,1,0:T(8,128)S(1)}, f32[2,6]{1,0:T(2,128)S(1)}) custom-call(f32[24,120,256]{2,1,0:T(8,128)S(1)} %get-tuple-element.17.spread, f32[2,3,216,256]{3,2,1,0:T(8,128)S(1)} %get-tuple-element.18.edges, f32[1,128]{1,0:T(1,128)S(1)} %get-tuple-element.19.tile, f32[320,32]{1,0:T(8,128)S(1)} %copy-done, s32[4]{0:T(128)S(1)} %copy-done.2, ...), custom_call_target="tpu_custom_call" | custom-call | tf_op jit(solution)/shard_map/tail/pallas_call | solution.py:817
  70.9 1.1 %copy.17 = f32[3,16,32,256]{3,2,1,0:T(8,128)} copy(f32[3,16,32,256]{3,2,1,0:T(8,128)S(1)} %get-tuple-element.22) | data formatting | bytes 3145728
  72.1 0.6 copy.18
Async XLA Ops:
  0.6 20.0 %copy-start.1 = (f32[6,2]{0,1:T(2,128)S(1)}, f32[6,2]{0,1:T(2,128)}, u32[]{:S(2)}) copy-start(f32[6,2]{0,1:T(2,128)} %param.18) | copy-start | bytes 148
  20.6 9.2 %copy-start = (f32[320,32]{1,0:T(8,128)S(1)}, f32[320,32]{1,0:T(8,128)}, u32[]{:S(2)}) copy-start(f32[320,32]{1,0:T(8,128)} %constant.2.clone.matrix) | copy-start | bytes 122884
  20.6 9.2 %copy-start.2 = (s32[4]{0:T(128)S(1)}, s32[4]{0:T(128)}, u32[]{:S(2)}) copy-start(s32[4]{0:T(128)} %contact_sphere.1) | copy-start | bytes 52
  20.6 9.2 %copy-start.3 = (s32[4]{0:T(128)S(1)}, s32[4]{0:T(128)}, u32[]{:S(2)}) copy-start(s32[4]{0:T(128)} %contact_partner.1) | copy-start | bytes 52

commit v5 on v4

--- a/solution.py
+++ b/solution.py
@@ -17,7 +17,8 @@
 MESH = pl.DeviceIdType.MESH
 TILE_LANES = 128
 CHUNK = 256
-WINDOW = 8
+WINDOW = 6
+TOGETHER = 2
 GROUP = 6
 RECORD = 24
 X_ROW, Y_ROW, Z_ROW, TARGET, OFFSET, SPHERE, LIVE = 12, 13, 14, 15, 18, 21, 22
@@ -126,7 +127,7 @@
 
 def front_body(
     columns, rows, loads, owners, base_x, base_y, base_z, weights, offsets, motion, velocity,
-    placed, alive, high, low, spread,
+    placed, alive, high_0, low_0, frame_0, high_1, low_1, frame_1,
     home, slots, arrived, left, right, below, above, corners, parts, send, recv,
 ):
     column = lax.axis_index("gx")
@@ -302,16 +303,19 @@
                 ],
                 axis=0,
             )
-            at = slice(wide_y * c, wide_y * (c + 1))
+            high, low, frame = (high_0, low_0, frame_0) if c == 0 else (high_1, low_1, frame_1)
+            begin = 0 if c == 0 else wide_y * (c - 1)
+            at = slice(begin, begin + wide_y)
             first, rest = split(value)
             high[x, at] = first.astype(bf16)
             low[x, at] = rest.astype(bf16)
             if own:
                 margin = jnp.zeros((ITERS, extent_z), f32)
-                spread[x + HALO, at] = jnp.concatenate([margin, lines, margin], axis=0)
-        end = jnp.zeros((high.shape[1] - 3 * wide_y, extent_z), bf16)
-        high[x, 3 * wide_y :] = end
-        low[x, 3 * wide_y :] = end
+                frame[x + HALO, at] = jnp.concatenate([margin, lines, margin], axis=0)
+        for ref, used in ((high_0, 1), (low_0, 1), (high_1, 2), (low_1, 2)):
+            used = used * wide_y
+            if ref.shape[1] > used:
+                ref[x, used:] = jnp.zeros((ref.shape[1] - used, extent_z), bf16)
 
     arrive(len(edge) - 6)
     arrive(len(edge) - 5)
@@ -332,8 +336,9 @@
         start(k)
     lax.fori_loop(0, span_x, inner, 0)
     for x in range(ITERS):
-        spread[x] = jnp.zeros(spread.shape[1:], f32)
-        spread[span_x + ITERS + x] = jnp.zeros(spread.shape[1:], f32)
+        for frame in (frame_0, frame_1):
+            frame[x] = jnp.zeros(frame.shape[1:], f32)
+            frame[span_x + ITERS + x] = jnp.zeros(frame.shape[1:], f32)
     arrive(lanes + 4)
     arrive(lanes + 5)
     for k in range(len(edge) - 4, len(edge)):
@@ -361,15 +366,15 @@
     copies = lanes + 12
     inputs = (owners, *bases, weights, offsets, motion, velocity)
     total = markers // CHUNK + lanes
-    field = (span_x + 2 * HALO, -(-3 * wide_y // 16) * 16, extent_z)
     vmem = pl.BlockSpec(memory_space=pltpu.VMEM)
     out = [
         pltpu.VMEM((total, RECORD, CHUNK), f32),
         pltpu.VMEM((8, TILE_LANES), f32),
-        pltpu.VMEM(field, bf16),
-        pltpu.VMEM(field, bf16),
-        pltpu.VMEM((span_x + 2 * ITERS, 3 * wide_y, extent_z), f32),
     ]
+    for lines in (wide_y, 2 * wide_y):
+        field = (span_x + 2 * HALO, -(-lines // 16) * 16, extent_z)
+        out += [pltpu.VMEM(field, bf16), pltpu.VMEM(field, bf16)]
+        out.append(pltpu.VMEM((span_x + 2 * ITERS, lines, extent_z), f32))
     room = 67_043_328 - sum(math.prod(ref.shape) * ref.dtype.itemsize for ref in out) - 2**15
     return pl.pallas_call(
         functools.partial(front_kernel, columns, rows),
@@ -405,85 +410,26 @@
     return value
 
 
-def markers_kernel(
-    spheres, span_y, sorted_refs, alive_ref, high, low, frame, motion, spread, edges, tile, sums
+def first_kernel(span_y, placed, alive, high, low, frame, spread, right, left, tables, forces):
+    def finish(j, record, got):
+        forces[j, 0:1] = got[0]
+
+    each_chunk(span_y, 1, 0, placed, alive, high, low, spread, tables, True, finish)
+    for edge, first in ((right, high.shape[0] - 2 * HALO), (left, HALO)):
+        pack_edge(edge, spread, first, 0, span_y)
+
+
+def rest_kernel(
+    spheres, span_y, placed, alive, high, low, frame, tables, forces, motion,
+    spread, edges, tile, sums,
 ):
-    layers, _, extent_z = high.shape
-    span_x = layers - 2 * HALO
-    wide_y = span_y + 2 * ITERS
     lanes = len(DIRECTIONS)
-    bf16, f32 = jnp.bfloat16, jnp.float32
-    alive_count = jnp.max(alive_ref[0:1, :]).astype(jnp.int32)
-
+    f32 = jnp.float32
     sums[...] = jnp.zeros(sums.shape, f32)
-    z_cells = lax.broadcasted_iota(jnp.int32, (extent_z, CHUNK), 0).astype(f32)
-    y_cells = lax.broadcasted_iota(jnp.int32, (wide_y, CHUNK), 0).astype(f32) - HALO
-    x_cells = lax.broadcasted_iota(jnp.int32, (WINDOW, CHUNK), 0).astype(f32)
-
-    def chunk(j, carry):
-        record = sorted_refs[j]
-        alive = record[LIVE : LIVE + 1]
-        cell_x = record[X_ROW : X_ROW + 1]
-        distance = z_cells - record[Z_ROW : Z_ROW + 1]
-        distance = jnp.where(distance < 0.0, distance + extent_z, distance)
-        z_high, z_low = split(four(distance, record[8:12]))
-        z_high = z_high.astype(bf16)
-        z_low = z_low.astype(bf16)
-        y_table = four(y_cells - record[Y_ROW : Y_ROW + 1], record[4:8])
-        least = jnp.min(jnp.where(alive > 0.5, cell_x, 1e4)).astype(jnp.int32)
-        most = jnp.max(jnp.where(alive > 0.5, cell_x, -1.0)).astype(jnp.int32)
-        windows = (most + 4 - least + WINDOW - 1) // WINDOW
-
-        def x_table(k):
-            fresh = least + WINDOW * k
-            base = jnp.minimum(fresh, layers - WINDOW)
-            cells = x_cells + base.astype(f32)
-            table = four(cells - cell_x, record[0:4])
-            return base, jnp.where(cells >= fresh.astype(f32), table, 0.0)
-
-        z_stack = jnp.concatenate([z_high, z_high, z_low], axis=0)
-
-        def sample(k, total):
-            base, table = x_table(k)
-            rows = high.shape[1]
-            first = high[pl.ds(base, WINDOW)].reshape(WINDOW * rows, extent_z)
-            rest = low[pl.ds(base, WINDOW)].reshape(WINDOW * rows, extent_z)
-            lines = jnp.dot(
-                jnp.concatenate([first, rest, first], axis=1),
-                z_stack,
-                preferred_element_type=f32,
-            )
-            for x in range(WINDOW):
-                total = total + lines[x * rows : x * rows + 3 * wide_y] * table[x : x + 1]
-            return total
-
-        plane = lax.fori_loop(0, windows, sample, jnp.zeros((3 * wide_y, CHUNK), f32))
-        forces = []
-        for c in range(3):
-            got = jnp.sum(plane[c * wide_y : (c + 1) * wide_y] * y_table, axis=0, keepdims=True)
-            forces.append((record[TARGET + c : TARGET + c + 1] - got) * alive)
-        sheet = jnp.concatenate([force * y_table for force in forces], axis=0)
-        z_wide = jnp.concatenate([z_high, z_high, z_low], axis=1)
-
-        def deposit(k, carry):
-            base, table = x_table(k)
-            value = jnp.concatenate([sheet * table[x : x + 1] for x in range(WINDOW)], axis=0)
-            first, rest = split(value)
-            first = first.astype(bf16)
-            rest = rest.astype(bf16)
-            added = lax.dot_general(
-                jnp.concatenate([first, rest, first], axis=1),
-                z_wide,
-                (((1,), (1,)), ((), ())),
-                preferred_element_type=f32,
-            )
-            at = pl.ds(base + HALO, WINDOW)
-            spread[at] = spread[at] + added.reshape(WINDOW, 3 * wide_y, extent_z)
-            return carry
-
-        lax.fori_loop(0, windows, deposit, 0)
+
+    def finish(j, record, got):
         o = [record[OFFSET + c : OFFSET + c + 1] for c in range(3)]
-        f = forces
+        f = [forces[j, 0:1]] + got
         moments = jnp.concatenate(
             f
             + [
@@ -497,10 +443,8 @@
         group = record[SPHERE : SPHERE + 1]
         for g in range((lanes + 1) * spheres):
             sums[g] = sums[g] + jnp.where(group == float(g), moments, 0.0)
-        return carry
-
-    chunks = (alive_count + (CHUNK - 1)) // CHUNK
-    lax.fori_loop(0, chunks, chunk, 0)
+
+    each_chunk(span_y, 2, 1, placed, alive, high, low, spread, tables, False, finish)
     columns = jnp.sum(sums[...], axis=2)
     tile[...] = jnp.zeros(tile.shape, f32)
     for s in range(spheres):
@@ -510,44 +454,186 @@
             tile[0:1, at : at + 6] = columns[line : line + 1, 0:6]
         at = 6 * ((lanes + 1) * spheres + s)
         tile[0:1, at : at + 6] = motion[s : s + 1]
+    for side, first in enumerate((high.shape[0] - 2 * HALO, HALO)):
+        for c in range(2):
+            pack_edge(edges.at[side, c], spread, first, c, span_y)
+
+
+def pack_edge(edge, spread, first, c, span_y):
+    wide_y = span_y + 2 * ITERS
     reach = ITERS + HALO
     middle = span_y + 2 * HALO - 2 * reach
-    for side, first in enumerate((span_x, HALO)):
-        for c in range(3):
-            for x in range(reach):
-                low_rim = wide_y * c + HALO
-                high_rim = wide_y * (c + 1) - HALO - reach
-                done = 0
-                for start, length in (
-                    (low_rim, reach),
-                    (high_rim, reach),
-                    (low_rim + reach, middle),
-                ):
-                    to = done + length * x
-                    edges[side, c, to : to + length] = spread[first + x, start : start + length]
-                    done += length * reach
-
-
-def markers_stage(spheres, span_y, placed, alive, high, low, frame, motion):
-    wide_x, lines, extent_z = frame.shape
-    lanes = len(DIRECTIONS)
+    low_rim = wide_y * c + HALO
+    high_rim = wide_y * (c + 1) - HALO - reach
+    for x in range(reach):
+        done = 0
+        for start, length in ((low_rim, reach), (high_rim, reach), (low_rim + reach, middle)):
+            to = done + length * x
+            edge[to : to + length] = spread[first + x, start : start + length]
+            done += length * reach
+
+
+def each_chunk(
+    span_y, components, component, placed, alive_ref, high, low, spread, tables, build, finish
+):
+    layers, rows, extent_z = high.shape
+    wide_y = span_y + 2 * ITERS
+    lines_here = components * wide_y
+    bf16, f32 = jnp.bfloat16, jnp.float32
+    alive_count = jnp.max(alive_ref[0:1, :]).astype(jnp.int32)
+    z_cells = lax.broadcasted_iota(jnp.int32, (extent_z, CHUNK), 0).astype(f32)
+    y_cells = lax.broadcasted_iota(jnp.int32, (wide_y, CHUNK), 0).astype(f32) - HALO
+    x_cells = lax.broadcasted_iota(jnp.int32, (WINDOW, CHUNK), 0).astype(f32)
+
+    def x_table(record, fresh):
+        base = jnp.minimum(fresh, layers - WINDOW)
+        cells = x_cells + base.astype(f32)
+        table = four(cells - record[X_ROW : X_ROW + 1], record[0:4])
+        return base, jnp.where(cells >= fresh.astype(f32), table, 0.0)
+
+    def sample(record, z_stack, fresh, total):
+        base, table = x_table(record, fresh)
+        first = high[pl.ds(base, WINDOW)].reshape(WINDOW * rows, extent_z)
+        rest = low[pl.ds(base, WINDOW)].reshape(WINDOW * rows, extent_z)
+        lines = jnp.dot(
+            jnp.concatenate([first, rest, first], axis=1),
+            z_stack,
+            preferred_element_type=f32,
+        )
+        for x in range(WINDOW):
+            part = lines[x * rows : x * rows + lines_here] * table[x : x + 1]
+            total = part if total is None else total + part
+        return total
+
+    def deposit(record, z_wide, sheet, fresh):
+        base, table = x_table(record, fresh)
+        value = jnp.concatenate([sheet * table[x : x + 1] for x in range(WINDOW)], axis=0)
+        first, rest = split(value)
+        first = first.astype(bf16)
+        rest = rest.astype(bf16)
+        added = lax.dot_general(
+            jnp.concatenate([first, rest, first], axis=1),
+            z_wide,
+            (((1,), (1,)), ((), ())),
+            preferred_element_type=f32,
+        )
+        at = pl.ds(base + HALO, WINDOW)
+        spread[at] = spread[at] + added.reshape(WINDOW, lines_here, extent_z)
+
+    def several(step, carry):
+        chunks = [step * TOGETHER + n for n in range(TOGETHER)]
+        records = [placed[j] for j in chunks]
+        high_z, low_z, y_tables, begins, windows, planes = [], [], [], [], [], []
+        for j, record in zip(chunks, records):
+            if build:
+                distance = z_cells - record[Z_ROW : Z_ROW + 1]
+                distance = jnp.where(distance < 0.0, distance + extent_z, distance)
+                z_high, z_low = split(four(distance, record[8:12]))
+                tables[j, 0] = z_high.astype(bf16)
+                tables[j, 1] = z_low.astype(bf16)
+            alive = record[LIVE : LIVE + 1] > 0.5
+            cell_x = record[X_ROW : X_ROW + 1]
+            least = jnp.min(jnp.where(alive, cell_x, 1e4)).astype(jnp.int32)
+            most = jnp.max(jnp.where(alive, cell_x, -1.0)).astype(jnp.int32)
+            begins.append(least)
+            windows.append((most + 4 - least + WINDOW - 1) // WINDOW)
+            y_tables.append(four(y_cells - record[Y_ROW : Y_ROW + 1], record[4:8]))
+
+        def stack(j, axis):
+            return jnp.concatenate([tables[j, 0], tables[j, 0], tables[j, 1]], axis=axis)
+
+        for n, j in enumerate(chunks):
+            planes.append(sample(records[n], stack(j, 0), begins[n], None))
+        for n, j in enumerate(chunks):
+            planes[n] = lax.fori_loop(
+                1,
+                windows[n],
+                lambda k, total, n=n, j=j: sample(
+                    placed[j], stack(j, 0), begins[n] + WINDOW * k, total
+                ),
+                planes[n],
+            )
+        sheets = []
+        for n, j in enumerate(chunks):
+            record = records[n]
+            got = []
+            for c in range(components):
+                weighted = planes[n][c * wide_y : (c + 1) * wide_y] * y_tables[n]
+                sampled = jnp.sum(weighted, axis=0, keepdims=True)
+                line = TARGET + component + c
+                got.append((record[line : line + 1] - sampled) * record[LIVE : LIVE + 1])
+            sheets.append(jnp.concatenate([force * y_tables[n] for force in got], axis=0))
+            finish(j, record, got)
+        for n, j in enumerate(chunks):
+            deposit(records[n], stack(j, 1), sheets[n], begins[n])
+        for n, j in enumerate(chunks):
+
+            @pl.when(windows[n] > 1)
+            def _(n=n, j=j):
+                def more(k, carry):
+                    deposit(placed[j], stack(j, 1), sheets[n], begins[n] + WINDOW * k)
+                    return carry
+
+                lax.fori_loop(1, windows[n], more, 0)
+
+        return carry
+
+    steps = (alive_count + (CHUNK * TOGETHER - 1)) // (CHUNK * TOGETHER)
+    lax.fori_loop(0, steps, several, 0)
+
+
+def first_stage(span_y, placed, alive, high, low, frame):
+    extent_z = frame.shape[2]
     f32 = jnp.float32
-    groups = (lanes + 1) * spheres
+    edge = jax.ShapeDtypeStruct(((ITERS + HALO) * (span_y + 2 * HALO), extent_z), f32)
     vmem = pl.BlockSpec(memory_space=pltpu.VMEM)
     return pl.pallas_call(
-        functools.partial(markers_kernel, spheres, span_y),
+        functools.partial(first_kernel, span_y),
         out_shape=[
             pltpu.VMEM(frame.shape, f32),
-            pltpu.VMEM((2, 3, (ITERS + HALO) * (span_y + 2 * HALO), extent_z), f32),
+            edge,
+            edge,
+            pltpu.VMEM((placed.shape[0], 2, extent_z, CHUNK), jnp.bfloat16),
+            pltpu.VMEM((placed.shape[0], 8, CHUNK), f32),
+        ],
+        in_specs=[vmem] * 5,
+        out_specs=[vmem] * 5,
+        input_output_aliases={4: 0},
+        compiler_params=pltpu.CompilerParams(vmem_limit_bytes=36 * 2**20),
+        cost_estimate=pl.CostEstimate(
+            flops=10_000_000_000, bytes_accessed=4_000_000, transcendentals=0
+        ),
+        name="first",
+    )(placed, alive, high, low, frame)
+
+
+def rest_stage(spheres, span_y, placed, alive, high, low, frame, tables, forces, motion):
+    extent_z = frame.shape[2]
+    f32 = jnp.float32
+    groups = (len(DIRECTIONS) + 1) * spheres
+    vmem = pl.BlockSpec(memory_space=pltpu.VMEM)
+    return pl.pallas_call(
+        functools.partial(rest_kernel, spheres, span_y),
+        out_shape=[
+            pltpu.VMEM(frame.shape, f32),
+            pltpu.VMEM((2, 2, (ITERS + HALO) * (span_y + 2 * HALO), extent_z), f32),
             jax.ShapeDtypeStruct((1, TILE_LANES), f32),
         ],
-        in_specs=[vmem] * 6,
+        in_specs=[vmem] * 8,
         out_specs=[vmem] * 3,
         scratch_shapes=[pltpu.VMEM((groups, 8, CHUNK), f32)],
         input_output_aliases={4: 0},
-        compiler_params=pltpu.CompilerParams(vmem_limit_bytes=40 * 2**20),
-        name="markers",
-    )(placed, alive, high, low, frame, motion)
+        compiler_params=pltpu.CompilerParams(vmem_limit_bytes=36 * 2**20),
+        cost_estimate=pl.CostEstimate(
+            flops=20_000_000_000, bytes_accessed=8_000_000, transcendentals=0
+        ),
+        name="rest",
+    )(placed, alive, high, low, frame, tables, forces, motion)
+
+
+def shift(array, step):
+    size = lax.axis_size("gx")
+    return lax.ppermute(array, "gx", [(i, (i + step) % size) for i in range(size)])
 
 
 def combine_matrix(columns, rows, per_sphere):
@@ -564,8 +650,8 @@
 
 
 def tail_kernel(
-    columns, rows, spread, edges, tile, matrix, contact_sphere, contact_partner,
-    out, motion_out, from_left, from_right, from_below, from_above, corners, held,
+    columns, rows, frame_0, frame_1, got_left, got_right, edges, tile, matrix,
+    contact_sphere, contact_partner, out, motion_out, from_left, from_right, from_below, from_above, corners, held,
     rhs, one, two, mask_ref, own_sem, send, recv, row_send, row_recv, col_send, col_recv,
 ):
     column = lax.axis_index("gx")
@@ -590,20 +676,33 @@
     edge = []
     rim = 2 * reach * reach
     part = corners.shape[2]
+
+    def halo(c, side):
+        if c == 0:
+            return (got_left, got_right)[side]
+        return (from_left, from_right)[side].at[c - 1]
+
     for c in range(3):
-        low, high = wide_y * c, wide_y * (c + 1)
+        frame = frame_1 if c else frame_0
+        low = wide_y * max(c - 1, 0)
+        high = low + wide_y
         inner = slice(HALO, wide_x - HALO)
+        if c:
+            edge += [
+                (edges.at[0, c - 1, 0:rim], from_left.at[c - 1, 0:rim], 1, 0),
+                (edges.at[1, c - 1, 0:rim], from_right.at[c - 1, 0:rim], -1, 0),
+                (edges.at[0, c - 1, rim:], from_left.at[c - 1, rim:], 1, 0),
+                (edges.at[1, c - 1, rim:], from_right.at[c - 1, rim:], -1, 0),
+            ]
+        else:
+            edge += [None] * 4
         edge += [
-            (edges.at[0, c, 0:rim], from_left.at[c, 0:rim], 1, 0),
-            (edges.at[1, c, 0:rim], from_right.at[c, 0:rim], -1, 0),
-            (edges.at[0, c, rim:], from_left.at[c, rim:], 1, 0),
-            (edges.at[1, c, rim:], from_right.at[c, rim:], -1, 0),
-            (spread.at[inner, high - RIM : high], from_below.at[c], 0, 1),
-            (spread.at[inner, low : low + RIM], from_above.at[c], 0, -1),
-            (from_left.at[c, rim - part : rim], corners.at[c, 0], 0, 1),
-            (from_right.at[c, rim - part : rim], corners.at[c, 1], 0, 1),
-            (from_left.at[c, 0:part], corners.at[c, 2], 0, -1),
-            (from_right.at[c, 0:part], corners.at[c, 3], 0, -1),
+            (frame.at[inner, high - RIM : high], from_below.at[c], 0, 1),
+            (frame.at[inner, low : low + RIM], from_above.at[c], 0, -1),
+            (halo(c, 0).at[rim - part : rim], corners.at[c, 0], 0, 1),
+            (halo(c, 1).at[rim - part : rim], corners.at[c, 1], 0, 1),
+            (halo(c, 0).at[0:part], corners.at[c, 2], 0, -1),
+            (halo(c, 1).at[0:part], corners.at[c, 3], 0, -1),
         ]
     each = 10
 
@@ -654,11 +753,13 @@
     ]
     for copy in first:
         copy.start()
-    for k in range(6):
-        start(k)
-    for c in range(1, 3):
+    for k in range(4):
+        start(each + k)
+    for c in range(3):
         for k in range(4, 6):
             start(each * c + k)
+    for k in range(6, each):
+        start(k)
 
     cells = lax.broadcasted_iota(jnp.int32, (wide_y, extent_z), 0) + (row * span_y - ITERS)
     inside = jnp.logical_and(cells >= 0, cells < span_y * rows)
@@ -682,9 +783,8 @@
     ]
     for copy in second:
         copy.start()
-    for c in range(1, 3):
-        for k in range(4):
-            start(each * c + k)
+    for k in range(4):
+        start(2 * each + k)
 
     def relaxed(c, source, x):
         here = source[c, x]
@@ -707,9 +807,9 @@
                     else:
                         buffers[sweep + 1][c, x] = new
 
-    def base(c, carry):
+    def base(c, load):
         for x in range(wide_x):
-            rhs[c, x] = spread[x, pl.ds(pl.multiple_of(wide_y * c, 8), wide_y)]
+            rhs[c, x] = load(x)
         for x in range(wide_x - 2 * HALO):
             y = x + HALO
             rhs[c, y, 0:RIM] = rhs[c, y, 0:RIM] + from_below[c, x]
@@ -717,26 +817,31 @@
         for x in range(reach, wide_x - reach):
             rhs[c, x] = rhs[c, x] * mask_ref[0]
         sweeps(c, ((reach + 1, 1),), lambda sweep: span_x - 2 * HALO - 2 - 2 * sweep)
+
+    def later(c, carry):
+        base(c, lambda x: frame_1[x, pl.ds(pl.multiple_of(wide_y * (c - 1), 8), wide_y)])
         return carry
 
     for c in range(3):
         arrive(each * c + 4)
         arrive(each * c + 5)
-    lax.fori_loop(0, 3, base, 0)
+    base(0, lambda x: frame_0[x])
+    lax.fori_loop(1, 3, later, 0)
 
     middle = depth - 2 * reach
     upper = wide_y - HALO - reach
 
     def outer(c):
         for x in range(reach):
-            for side, (halo, y) in enumerate(((from_left, x), (from_right, x + span_x + HALO))):
+            for side, y in enumerate((x, x + span_x + HALO)):
+                got = halo(c, side)
                 low = slice(reach * x, reach * (x + 1))
                 high = slice(reach * (reach + x), reach * (reach + x + 1))
                 late = slice(part - rim // 2 + reach * x, part - rim // 2 + reach * (x + 1))
                 inside = slice(rim + middle * x, rim + middle * (x + 1))
-                rhs[c, y, HALO : HALO + reach] = rhs[c, y, HALO : HALO + reach] + halo[c, low]
-                rhs[c, y, upper : upper + reach] = rhs[c, y, upper : upper + reach] + halo[c, high]
-                rhs[c, y, HALO + reach : upper] = rhs[c, y, HALO + reach : upper] + halo[c, inside]
+                rhs[c, y, HALO : HALO + reach] = rhs[c, y, HALO : HALO + reach] + got[low]
+                rhs[c, y, upper : upper + reach] = rhs[c, y, upper : upper + reach] + got[high]
+                rhs[c, y, HALO + reach : upper] = rhs[c, y, HALO + reach : upper] + got[inside]
                 rhs[c, y, 0:reach] = rhs[c, y, 0:reach] + corners[c, side, late]
                 rhs[c, y, wide_y - reach :] = rhs[c, y, wide_y - reach :] + corners[c, 2 + side, low]
                 rhs[c, y] = rhs[c, y] * mask_ref[0]
@@ -786,25 +891,27 @@
                 motion_out[s : s + 1, 3 * half : 3 * half + 3] = total
 
     for c in range(3):
-        arrive(each * c)
-        arrive(each * c + 1)
-        for k in range(6, each):
-            start(each * c + k)
+        if c:
+            arrive(each * c)
+            arrive(each * c + 1)
+            for k in range(6, each):
+                start(each * c + k)
         if c == 2:
             settle()
-        for k in range(2, 4):
-            arrive(each * c + k)
+        if c:
+            arrive(each * c + 2)
+            arrive(each * c + 3)
         for k in range(6, each):
             arrive(each * c + k)
         outer(c)
 
-    for k in range(len(edge)):
+    for k in range(4, len(edge)):
         sent(k)
 
 
-def tail(spread, edges, tile, matrix, contact_sphere, contact_partner, span_y, spheres):
+def tail(frames, got, edges, tile, matrix, contact_sphere, contact_partner, span_y, spheres):
     columns, rows = lax.axis_size("gx"), lax.axis_size("gy")
-    wide_x, _, extent_z = spread.shape
+    wide_x, _, extent_z = frames[0].shape
     span_x = wide_x - 2 * ITERS
     wide_y = span_y + 2 * ITERS
     reach = ITERS + HALO
@@ -820,7 +927,7 @@
             pltpu.VMEM((3, span_x, span_y, extent_z), f32),
             jax.ShapeDtypeStruct((spheres, 6), f32),
         ],
-        in_specs=[vmem] * 4 + [smem] * 2,
+        in_specs=[vmem] * 7 + [smem] * 2,
         out_specs=[vmem] * 2,
         scratch_shapes=[
             pltpu.VMEM(edges.shape[1:], f32),
@@ -842,10 +949,10 @@
             dma((columns - 1,)),
         ],
         compiler_params=pltpu.CompilerParams(
-            collective_id=1, has_side_effects=True, vmem_limit_bytes=40 * 2**20
+            collective_id=1, has_side_effects=True, vmem_limit_bytes=36 * 2**20
         ),
         name="tail",
-    )(spread, edges, tile, matrix, contact_sphere, contact_partner)
+    )(*frames, *got, edges, tile, matrix, contact_sphere, contact_partner)
 
 
 def on_device(
@@ -866,12 +973,21 @@
     bases = [base.reshape(1, markers) for base in (base_x, base_y, base_z)]
     owners = owner_block.reshape(1, markers)
     motion = sphere_motion.T
-    staged = front(owners, bases, delta_weights, marker_offset, motion, velocity)
-    spread, edges, tile = markers_stage(spheres, span_y, *staged, motion)
+    placed, alive, high_0, low_0, frame_0, high_1, low_1, frame_1 = front(
+        owners, bases, delta_weights, marker_offset, motion, velocity
+    )
+    frame_0, right, left, tables, forces = first_stage(
+        span_y, placed, alive, high_0, low_0, frame_0
+    )
+    got = (shift(right, 1), shift(left, -1))
+    frame_1, edges, tile = rest_stage(
+        spheres, span_y, placed, alive, high_1, low_1, frame_1, tables, forces, motion
+    )
     columns, rows = lax.axis_size("gx"), lax.axis_size("gy")
     matrix = jnp.asarray(combine_matrix(columns, rows, markers // spheres))
     state, moved = tail(
-        spread, edges, tile, matrix, contact_sphere, contact_partner, span_y, spheres
+        (frame_0, frame_1), got, edges, tile, matrix, contact_sphere, contact_partner,
+        span_y, spheres,
     )
     return state, moved.T
 

time: 72.6 us -> 67.7 us (0.933)
  Pallas kernels: 70.2 us -> 59.7 us
  starting transfers between devices: 0 us -> 4.22 us
  local copies, waits for them, and re-layouts: 1.73 us -> 2.88 us
    pallas_call x1, Pallas kernels: 41.1 us -> 26.7 us  [tail(): pl.pallas_call(functools.partial(tail_kernel, columns, rows), out_shape=[...]
    ppermute x0 -> x2, starting transfers between devices: none -> 4.22 us  [shift(): lax.ppermute(array, 'gx', [(i, (i + step) % size) for i in range(size)])]
    pallas_call x1 -> x2, Pallas kernels: 9.15 us -> 13 us  [the longest x1 7.21 us: rest_stage(): pl.pallas_call(functools.partial(rest_kernel, spheres, span_y), out_shape...]
    unnamed x10 -> x14, local copies, waits for them, and re-layouts: 1.73 us -> 2.88 us
  transfers between devices with their start and end apart: 0 -> 2, of which waited for: 0 -> 0; matrix products, arithmetic and copies ran while one was open for 0% -> 0% of each run, Pallas kernels for 0% -> 11%
where the time goes in v5:
time: 67.7 us; the launch traced here: 67.5 us
  Pallas kernels  59.7 us (88%)
  starting transfers between devices  4.22 us (6%)
  local copies, waits for them, and re-layouts  2.88 us (4%)
  between operations  0.73 us (1%)
    pallas_call x1, Pallas kernels, tail(): pl.pallas_call(functools.partial(tail_kernel, columns, rows), out_shape=[...  26.7 us
    pallas_call x1, Pallas kernels, front(): pl.pallas_call(functools.partial(front_kernel, columns, rows), out_shape=...  19.9 us
    pallas_call x1, Pallas kernels, rest_stage(): pl.pallas_call(functools.partial(rest_kernel, spheres, span_y), out_shape...  7.21 us
    pallas_call x1, Pallas kernels, first_stage(): pl.pallas_call(functools.partial(first_kernel, span_y), out_shape=[pltpu....  5.79 us
    ppermute x2, starting transfers between devices, shift(): lax.ppermute(array, 'gx', [(i, (i + step) % size) for i in range(size)])  4.22 us
    unnamed x14, local copies, waits for them, and re-layouts  2.88 us
  transfers between devices with their start and end apart: 2, of which 0 were waited for; matrix products, arithmetic and copies ran while one was open for 0% of the time, Pallas kernels for 11%

profile of v5, /device:TPU:1, one launch (start us, length us, event | category | flops | bytes accessed | tf_op | source)
XLA Modules:
  0.0 67.5 jit_solution(16651760164668722847)
XLA Ops:
  0.6 19.9 %front.1 = (f32[16,24,256]{2,1,0:T(8,128)S(1)}, f32[8,128]{1,0:T(8,128)S(1)}, bf16[20,48,256]{2,1,0:T(8,128)(2,1)S(1)}, bf16[20,48,256]{2,1,0:T(8,128)(2,1)S(1)}...) custom-call(s32[1,2048]{1,0:T(1,128)} %bitcast.9, ...), custom_call_target="tpu_custom_call" | custom-call | tf_op jit(solution)/shard_map/front/pallas_call | solution.py:379
  20.6 0.0 copy-start.4
  20.6 0.0 copy-start.1
  20.6 5.8 %first.1 = (f32[24,40,256]{2,1,0:T(8,128)S(1)}, f32[216,256]{1,0:T(8,128)S(1)}, f32[216,256]{1,0:T(8,128)S(1)}, bf16[16,2,256,256]{3,2,1,0:T(8,128)(2,1)S(1)}, f32[16,8,256]{2,1,0:T(8,128)S(1)}) custom-call(f32[16,24,256]{2,1,0:T(8,128)S(1)} %get-tuple-element.20.placed, f32[8,128]{1,0:T(8,128)S(1)} %get-tuple-element.21.alive, ...), custom_call_target="tpu_custom_call", output_to_operand_aliasing={{0}: (4, {})} | custom-call | flops 10000000000 | bytes 4000000 | tf_op jit(solution)/shard_map/first/pallas_call | solution.py:590
  26.4 0.0 copy-done.4
  26.4 1.9 %collective-permute-start = (f32[216,256]{1,0:T(8,128)S(1)}, f32[216,256]{1,0:T(8,128)S(1)}, u32[]{:S(2)}, u32[]{:S(2)}) collective-permute-start(f32[216,256]{1,0:T(8,128)S(1)} %get-tuple-element.32), channel_id=1, source_target_pairs={{0,4},{4,8},{8,12},{12,16},{16,20},{20,24},{24,28},{28,0},{1,5},{5... | collective-permute-start | bytes 663560 | tf_op jit(solution)/shard_map/ppermute | solution.py:636
  28.3 2.3 %collective-permute-start.1 = (f32[216,256]{1,0:T(8,128)S(1)}, f32[216,256]{1,0:T(8,128)S(1)}, u32[]{:S(2)}, u32[]{:S(2)}) collective-permute-start(f32[216,256]{1,0:T(8,128)S(1)} %get-tuple-element.33), channel_id=1, source_target_pairs={{0,28},{4,0},{8,4},{12,8},{16,12},{20,16},{24,20},{28,24},{1,29},{... | collective-permute-start | bytes 663560 | tf_op jit(solution)/shard_map/ppermute | solution.py:636
  30.6 0.0 copy-done.1
  30.6 0.0 copy-start.5
  30.6 1.1 %copy-done.5 = bf16[20,80,256]{2,1,0:T(8,128)(2,1)S(1)} copy-done((bf16[20,80,256]{2,1,0:T(8,128)(2,1)S(1)}, bf16[20,80,256]{2,1,0:T(8,128)(2,1)}, u32[]{:S(2)}) %copy-start.5) | copy-done | bytes 819224
  31.8 0.0 copy-start
  31.8 0.0 copy-start.2
  31.8 0.0 copy-start.3
  31.8 7.2 %rest.1 = (f32[24,80,256]{2,1,0:T(8,128)S(1)}, f32[2,2,216,256]{3,2,1,0:T(8,128)S(1)}, f32[1,128]{1,0:T(1,128)S(1)}) custom-call(f32[16,24,256]{2,1,0:T(8,128)S(1)} %get-tuple-element.20.placed, f32[8,128]{1,0:T(8,128)S(1)} %get-tuple-element.21.alive, bf16[20,80,256]{2,1,0:T(8,128)(2,1)S(1)} %copy-done.5, ...), custom_call_target="tpu_custom_call", output_to_operand_aliasing={{0}: (4, {})} | custom-call | flops 20000000000 | bytes 8000000 | tf_op jit(solution)/shard_map/rest/pallas_call | solution.py:615
  39.0 0.0 collective-permute-done.got_left
  39.0 0.0 collective-permute-done.1.got_right
  39.0 0.0 copy-done
  39.0 0.0 copy-done.2
  39.0 0.0 copy-done.3
  39.1 26.7 %tail.1 = (f32[3,16,32,256]{3,2,1,0:T(8,128)S(1)}, f32[2,6]{1,0:T(2,128)S(1)}) custom-call(f32[24,40,256]{2,1,0:T(8,128)S(1)} %get-tuple-element.25.frame_0, f32[24,80,256]{2,1,0:T(8,128)S(1)} %get-tuple-element.31.frame_1, f32[216,256]{1,0:T(8,128)S(1)} %collective-permute-done.got_left, f32[216,256]{1,0:T(8,128)S(1)} %collective-permute-done.1.got_right, ...), custom_call_target="tpu_custom_call" | custom-call | tf_op jit(solution)/shard_map/tail/pallas_call | solution.py:924
  65.8 1.1 %copy.19 = f32[3,16,32,256]{3,2,1,0:T(8,128)} copy(f32[3,16,32,256]{3,2,1,0:T(8,128)S(1)} %get-tuple-element.38) | data formatting | bytes 3145728
  66.9 0.6 copy.20
Async XLA Ops:
  20.6 5.8 %copy-start.4 = (bf16[20,80,256]{2,1,0:T(8,128)(2,1)}, bf16[20,80,256]{2,1,0:T(8,128)(2,1)S(1)}, u32[]{:S(2)}) copy-start(bf16[20,80,256]{2,1,0:T(8,128)(2,1)S(1)} %get-tuple-element.26.high) | copy-start | bytes 2457604
  20.6 10.0 %copy-start.1 = (f32[6,2]{0,1:T(2,128)S(1)}, f32[6,2]{0,1:T(2,128)}, u32[]{:S(2)}) copy-start(f32[6,2]{0,1:T(2,128)} %param.18) | copy-start | bytes 148
  26.4 12.6 %collective-permute-start = (f32[216,256]{1,0:T(8,128)S(1)}, f32[216,256]{1,0:T(8,128)S(1)}, u32[]{:S(2)}, u32[]{:S(2)}) collective-permute-start(f32[216,256]{1,0:T(8,128)S(1)} %get-tuple-element.32), channel_id=1, source_target_pairs={{0,4},{4,8},{8,12},{12,16},{16,20},{20,24},{24,28},{28,0},{1,5},{5... | collective-permute-start | bytes 663560 | tf_op jit(solution)/shard_map/ppermute | solution.py:636
  28.3 10.7 %collective-permute-start.1 = (f32[216,256]{1,0:T(8,128)S(1)}, f32[216,256]{1,0:T(8,128)S(1)}, u32[]{:S(2)}, u32[]{:S(2)}) collective-permute-start(f32[216,256]{1,0:T(8,128)S(1)} %get-tuple-element.33), channel_id=1, source_target_pairs={{0,28},{4,0},{8,4},{12,8},{16,12},{20,16},{24,20},{28,24},{1,29},{... | collective-permute-start | bytes 663560 | tf_op jit(solution)/shard_map/ppermute | solution.py:636
  30.6 1.1 %copy-start.5 = (bf16[20,80,256]{2,1,0:T(8,128)(2,1)S(1)}, bf16[20,80,256]{2,1,0:T(8,128)(2,1)}, u32[]{:S(2)}) copy-start(bf16[20,80,256]{2,1,0:T(8,128)(2,1)} %copy-done.4) | copy-start | bytes 2457604
  31.8 7.2 %copy-start = (f32[320,32]{1,0:T(8,128)S(1)}, f32[320,32]{1,0:T(8,128)}, u32[]{:S(2)}) copy-start(f32[320,32]{1,0:T(8,128)} %constant.2.clone.matrix) | copy-start | bytes 122884
  31.8 7.3 %copy-start.2 = (s32[4]{0:T(128)S(1)}, s32[4]{0:T(128)}, u32[]{:S(2)}) copy-start(s32[4]{0:T(128)} %contact_sphere.1) | copy-start | bytes 52
  31.8 7.3 %copy-start.3 = (s32[4]{0:T(128)S(1)}, s32[4]{0:T(128)}, u32[]{:S(2)}) copy-start(s32[4]{0:T(128)} %contact_partner.1) | copy-start | bytes 52

commit v6 on v5

--- a/solution.py
+++ b/solution.py
@@ -18,7 +18,7 @@
 TILE_LANES = 128
 CHUNK = 256
 WINDOW = 6
-TOGETHER = 2
+TOGETHER = 4
 GROUP = 6
 RECORD = 24
 X_ROW, Y_ROW, Z_ROW, TARGET, OFFSET, SPHERE, LIVE = 12, 13, 14, 15, 18, 21, 22
@@ -599,7 +599,7 @@
         in_specs=[vmem] * 5,
         out_specs=[vmem] * 5,
         input_output_aliases={4: 0},
-        compiler_params=pltpu.CompilerParams(vmem_limit_bytes=36 * 2**20),
+        compiler_params=pltpu.CompilerParams(vmem_limit_bytes=30 * 2**20),
         cost_estimate=pl.CostEstimate(
             flops=10_000_000_000, bytes_accessed=4_000_000, transcendentals=0
         ),
@@ -623,7 +623,7 @@
         out_specs=[vmem] * 3,
         scratch_shapes=[pltpu.VMEM((groups, 8, CHUNK), f32)],
         input_output_aliases={4: 0},
-        compiler_params=pltpu.CompilerParams(vmem_limit_bytes=36 * 2**20),
+        compiler_params=pltpu.CompilerParams(vmem_limit_bytes=30 * 2**20),
         cost_estimate=pl.CostEstimate(
             flops=20_000_000_000, bytes_accessed=8_000_000, transcendentals=0
         ),

time: 67.7 us -> 66.9 us (0.988)
  local copies, waits for them, and re-layouts: 2.88 us -> 1.72 us
    unnamed x14 -> x10, local copies, waits for them, and re-layouts: 2.88 us -> 1.72 us
    pallas_call x1, Pallas kernels: 26.7 us -> 26 us  [tail(): pl.pallas_call(functools.partial(tail_kernel, columns, rows), out_shape=[...]
  transfers between devices with their start and end apart: 2 -> 2, of which waited for: 0 -> 0; matrix products, arithmetic and copies ran while one was open for 0% -> 0% of each run, Pallas kernels for 11% -> 12%
where the time goes in v6:
time: 66.9 us; the launch traced here: 66.4 us
  Pallas kernels  59.8 us (89%)
  starting transfers between devices  4.22 us (6%)
  local copies, waits for them, and re-layouts  1.72 us (3%)
  between operations  0.72 us (1%)
    pallas_call x1, Pallas kernels, tail(): pl.pallas_call(functools.partial(tail_kernel, columns, rows), out_shape=[...  26 us
    pallas_call x1, Pallas kernels, front(): pl.pallas_call(functools.partial(front_kernel, columns, rows), out_shape=...  19.9 us
    pallas_call x1, Pallas kernels, rest_stage(): pl.pallas_call(functools.partial(rest_kernel, spheres, span_y), out_shape...  7.82 us
    pallas_call x1, Pallas kernels, first_stage(): pl.pallas_call(functools.partial(first_kernel, span_y), out_shape=[pltpu....  6.02 us
    ppermute x2, starting transfers between devices, shift(): lax.ppermute(array, 'gx', [(i, (i + step) % size) for i in range(size)])  4.22 us
    unnamed x10, local copies, waits for them, and re-layouts  1.72 us
  transfers between devices with their start and end apart: 2, of which 0 were waited for; matrix products, arithmetic and copies ran while one was open for 0% of the time, Pallas kernels for 12%

profile of v6, /device:TPU:1, one launch (start us, length us, event | category | flops | bytes accessed | tf_op | source)
XLA Modules:
  0.0 66.4 jit_solution(10698995909041093382)
XLA Ops:
  0.6 19.9 %front.1 = (f32[16,24,256]{2,1,0:T(8,128)S(1)}, f32[8,128]{1,0:T(8,128)S(1)}, bf16[20,48,256]{2,1,0:T(8,128)(2,1)S(1)}, bf16[20,48,256]{2,1,0:T(8,128)(2,1)S(1)}...) custom-call(s32[1,2048]{1,0:T(1,128)} %bitcast.9, ...), custom_call_target="tpu_custom_call" | custom-call | tf_op jit(solution)/shard_map/front/pallas_call | solution.py:379
  20.6 0.0 copy-start.1
  20.6 6.0 %first.1 = (f32[24,40,256]{2,1,0:T(8,128)S(1)}, f32[216,256]{1,0:T(8,128)S(1)}, f32[216,256]{1,0:T(8,128)S(1)}, bf16[16,2,256,256]{3,2,1,0:T(8,128)(2,1)S(1)}, f32[16,8,256]{2,1,0:T(8,128)S(1)}) custom-call(f32[16,24,256]{2,1,0:T(8,128)S(1)} %get-tuple-element.20.placed, f32[8,128]{1,0:T(8,128)S(1)} %get-tuple-element.21.alive, ...), custom_call_target="tpu_custom_call", output_to_operand_aliasing={{0}: (4, {})} | custom-call | flops 10000000000 | bytes 4000000 | tf_op jit(solution)/shard_map/first/pallas_call | solution.py:590
  26.6 1.4 %collective-permute-start = (f32[216,256]{1,0:T(8,128)S(1)}, f32[216,256]{1,0:T(8,128)S(1)}, u32[]{:S(2)}, u32[]{:S(2)}) collective-permute-start(f32[216,256]{1,0:T(8,128)S(1)} %get-tuple-element.32), channel_id=1, source_target_pairs={{0,4},{4,8},{8,12},{12,16},{16,20},{20,24},{24,28},{28,0},{1,5},{5... | collective-permute-start | bytes 663560 | tf_op jit(solution)/shard_map/ppermute | solution.py:636
  28.1 2.8 %collective-permute-start.1 = (f32[216,256]{1,0:T(8,128)S(1)}, f32[216,256]{1,0:T(8,128)S(1)}, u32[]{:S(2)}, u32[]{:S(2)}) collective-permute-start(f32[216,256]{1,0:T(8,128)S(1)} %get-tuple-element.33), channel_id=1, source_target_pairs={{0,28},{4,0},{8,4},{12,8},{16,12},{20,16},{24,20},{28,24},{1,29},{... | collective-permute-start | bytes 663560 | tf_op jit(solution)/shard_map/ppermute | solution.py:636
  30.8 0.0 copy-done.1
  30.8 0.0 copy-start
  30.8 0.0 copy-start.2
  30.8 0.0 copy-start.3
  30.8 7.8 %rest.1 = (f32[24,80,256]{2,1,0:T(8,128)S(1)}, f32[2,2,216,256]{3,2,1,0:T(8,128)S(1)}, f32[1,128]{1,0:T(1,128)S(1)}) custom-call(f32[16,24,256]{2,1,0:T(8,128)S(1)} %get-tuple-element.20.placed, f32[8,128]{1,0:T(8,128)S(1)} %get-tuple-element.21.alive, bf16[20,80,256]{2,1,0:T(8,128)(2,1)S(1)} %get-tuple-element.26.high, ...), custom_call_target="tpu_custom_call", output_to_operand_aliasing={{0}: (4, {})} | custom-call | flops 20000000000 | bytes 8000000 | tf_op jit(solution)/shard_map/rest/pallas_call | solution.py:615
  38.7 0.0 collective-permute-done.got_left
  38.7 0.0 collective-permute-done.1.got_right
  38.7 0.0 copy-done
  38.7 0.0 copy-done.2
  38.7 0.0 copy-done.3
  38.7 26.0 %tail.1 = (f32[3,16,32,256]{3,2,1,0:T(8,128)S(1)}, f32[2,6]{1,0:T(2,128)S(1)}) custom-call(f32[24,40,256]{2,1,0:T(8,128)S(1)} %get-tuple-element.25.frame_0, f32[24,80,256]{2,1,0:T(8,128)S(1)} %get-tuple-element.31.frame_1, f32[216,256]{1,0:T(8,128)S(1)} %collective-permute-done.got_left, f32[216,256]{1,0:T(8,128)S(1)} %collective-permute-done.1.got_right, ...), custom_call_target="tpu_custom_call" | custom-call | tf_op jit(solution)/shard_map/tail/pallas_call | solution.py:924
  64.7 1.1 %copy.19 = f32[3,16,32,256]{3,2,1,0:T(8,128)} copy(f32[3,16,32,256]{3,2,1,0:T(8,128)S(1)} %get-tuple-element.38) | data formatting | bytes 3145728
  65.9 0.6 copy.20
Async XLA Ops:
  20.6 10.3 %copy-start.1 = (f32[6,2]{0,1:T(2,128)S(1)}, f32[6,2]{0,1:T(2,128)}, u32[]{:S(2)}) copy-start(f32[6,2]{0,1:T(2,128)} %param.18) | copy-start | bytes 148
  26.6 12.1 %collective-permute-start = (f32[216,256]{1,0:T(8,128)S(1)}, f32[216,256]{1,0:T(8,128)S(1)}, u32[]{:S(2)}, u32[]{:S(2)}) collective-permute-start(f32[216,256]{1,0:T(8,128)S(1)} %get-tuple-element.32), channel_id=1, source_target_pairs={{0,4},{4,8},{8,12},{12,16},{16,20},{20,24},{24,28},{28,0},{1,5},{5... | collective-permute-start | bytes 663560 | tf_op jit(solution)/shard_map/ppermute | solution.py:636
  28.1 10.6 %collective-permute-start.1 = (f32[216,256]{1,0:T(8,128)S(1)}, f32[216,256]{1,0:T(8,128)S(1)}, u32[]{:S(2)}, u32[]{:S(2)}) collective-permute-start(f32[216,256]{1,0:T(8,128)S(1)} %get-tuple-element.33), channel_id=1, source_target_pairs={{0,28},{4,0},{8,4},{12,8},{16,12},{20,16},{24,20},{28,24},{1,29},{... | collective-permute-start | bytes 663560 | tf_op jit(solution)/shard_map/ppermute | solution.py:636
  30.8 7.9 %copy-start = (f32[320,32]{1,0:T(8,128)S(1)}, f32[320,32]{1,0:T(8,128)}, u32[]{:S(2)}) copy-start(f32[320,32]{1,0:T(8,128)} %constant.2.clone.matrix) | copy-start | bytes 122884
  30.8 7.9 %copy-start.2 = (s32[4]{0:T(128)S(1)}, s32[4]{0:T(128)}, u32[]{:S(2)}) copy-start(s32[4]{0:T(128)} %contact_sphere.1) | copy-start | bytes 52
  30.8 7.9 %copy-start.3 = (s32[4]{0:T(128)S(1)}, s32[4]{0:T(128)}, u32[]{:S(2)}) copy-start(s32[4]{0:T(128)} %contact_partner.1) | copy-start | bytes 52
